TPU v7x, 32 devices: a whole 2x2x4 slice. The times are simulated.
32 devices in a mesh: groups: 2 (over y), gx: 4 (over z), gy: 4 (over x, core).
Axes of the slice: x: 2, y: 2, z: 4, core: 2. Of those that a mesh axis runs over, the one named last changes fastest.
Arguments:
- tokens: bfloat16 [2, 16, 16384], P(None, 'groups', 'gx'), parts along dimension 1, may hold values from -20 to 20, as said below
- lengths: int32 [2, 16], P(None, ('groups', 'gx')), parts along dimension 1, may hold values from 1 to 1024, as said below
- norm_gain: bfloat16 [16384], P('gx'), may hold values from 0.5 to 2
- w_query: bfloat16 [16384, 8192], P('gx', 'gy'), may hold values from -1.171875 to 1.171875
- key_value_weight: bfloat16 [16384, 4, 256], P('gx', 'gy'), may hold values from -0.046875 to 0.046875
- w_out: bfloat16 [8192, 16384], P('gy', 'gx'), may hold values from -0.0625 to 0.0625
- cache: bfloat16 [2, 16, 1024, 4, 2, 128], P(None, ('groups', 'gx'), None, 'gy'), parts along dimension 1, may hold values from -16 to 16
Outputs:
- layer_out: bfloat16 [2, 16, 16384], P(None, 'groups', 'gx'), parts along dimension 1
There are 2 independent parts, one for each index of `groups`. A program takes and returns all parts, laid end to end along the dimension named above; an argument that names none is the same for every part. Nothing has to cross between parts.
Inputs may be any that keep to these rules, and one draw needn't show every extreme that they name: `tokens`: entries vary with the feature and the row. `lengths`: some rollout has exactly 1024 cached positions in every draw.
All inputs are finite; a program needn't handle non-finite values.
Results may differ from a plain program's by a relative error of at most 0.012.
The roundings to bfloat16 on the way count: a program that leaves them out, or rounds other values in their place, can miss the bound.
Values may be sent and summed in bfloat16 or wider, within the bound.
No kernel may reach another device: no remote copies, remote signals or barrier semaphores. Data moves between devices by JAX's collectives and lax.ppermute only.
A program may use at most 128 MiB of HBM per device.

v0:
```python
import jax
import jax.numpy as jnp
from jax import lax
from jax.sharding import PartitionSpec as P

MODEL_WIDTH = 16384
HEAD_SIZE = 128


def rotate(vectors, positions):
    half = vectors.shape[-1] // 2
    freq = 500000.0 ** (-2.0 * jnp.arange(half, dtype=jnp.float32) / vectors.shape[-1])
    angle = positions[..., None] * freq
    cosine = jnp.cos(angle)
    sine = jnp.sin(angle)
    first = vectors[..., :half]
    second = vectors[..., half:]
    return jnp.concatenate(
        [first * cosine - second * sine, second * cosine + first * sine], axis=-1
    )


def attend(query_sum, keyval_sum, local_squares, lengths, cache):
    batches, rows_here = lengths.shape
    score_scale = lax.rsqrt(local_squares / MODEL_WIDTH + 1e-05)
    heads_kv = keyval_sum.shape[2]
    query_group = query_sum.shape[2] // (heads_kv * HEAD_SIZE)
    query = (
        query_sum.reshape(batches, rows_here, heads_kv, query_group, HEAD_SIZE)
        * score_scale[:, :, None, None, None]
    )
    key_value = keyval_sum * score_scale[:, :, None, None]
    positions = lengths.astype(jnp.float32)
    rotated_query = rotate(query, positions[:, :, None, None]).astype(jnp.bfloat16)
    rkey = rotate(key_value[..., :HEAD_SIZE], positions[:, :, None])
    value_new = key_value[..., HEAD_SIZE:]
    inv_root = 1.0 / jnp.sqrt(jnp.float32(HEAD_SIZE))
    keys = cache[:, :, :, :, 0, :]
    values = cache[:, :, :, :, 1, :]
    scores = (
        jnp.einsum("mrkgd,mrskd->mrkgs", rotated_query, keys, preferred_element_type=jnp.float32)
        * inv_root
    )
    valid = jnp.arange(cache.shape[2], dtype=jnp.int32)[None, None, :] < lengths[:, :, None]
    scores = jnp.where(valid[:, :, None, None, :], scores, -1e30)
    new_score = (
        jnp.sum(rotated_query.astype(jnp.float32) * rkey[:, :, :, None, :], axis=-1) * inv_root
    )
    top = jnp.maximum(jnp.max(scores, axis=-1), new_score)
    weights = jnp.exp(scores - top[..., None])
    new_weight = jnp.exp(new_score - top)
    total = jnp.sum(weights, axis=-1) + new_weight
    summed = jnp.einsum(
        "mrkgs,mrskd->mrkgd",
        weights.astype(jnp.bfloat16),
        values,
        preferred_element_type=jnp.float32,
    )
    summed = summed + new_weight[..., None] * value_new[:, :, :, None, :]
    return (
        (summed / total[..., None])
        .astype(jnp.bfloat16)
        .reshape(batches, rows_here, heads_kv * query_group * HEAD_SIZE)
    )


def local(tokens, lengths, norm_gain, w_query, key_value_weight, w_out, cache):
    x_full = tokens.astype(jnp.float32)
    squares = jnp.sum(x_full * x_full, axis=-1)
    normed = (x_full * norm_gain.astype(jnp.float32)).astype(jnp.bfloat16)
    query_part = jnp.einsum("mrd,dc->mrc", normed, w_query, preferred_element_type=jnp.float32)
    keyval_part = jnp.einsum(
        "mrd,dkc->mrkc", normed, key_value_weight, preferred_element_type=jnp.float32
    )
    query_sum, keyval_sum, local_squares = (
        lax.psum_scatter(query_part, "gx", scatter_dimension=1, tiled=True),
        lax.psum_scatter(keyval_part, "gx", scatter_dimension=1, tiled=True),
        lax.psum_scatter(squares, "gx", scatter_dimension=1, tiled=True),
    )
    attended = attend(query_sum, keyval_sum, local_squares, lengths, cache)
    projected = jnp.einsum(
        "mrc,cd->mrd",
        lax.all_gather(attended, "gx", axis=1, tiled=True),
        w_out,
        preferred_element_type=jnp.float32,
    )
    summed_heads = lax.psum(projected, "gy")
    return (x_full + summed_heads).astype(jnp.bfloat16)


def solution(mesh):
    placed = (
        P(None, "groups", "gx"),
        P(None, ("groups", "gx")),
        P("gx"),
        P("gx", "gy"),
        P("gx", "gy", None),
        P("gy", "gx"),
        P(None, ("groups", "gx"), None, "gy", None, None),
    )
    return jax.shard_map(
        local, mesh=mesh, in_specs=placed, out_specs=P(None, "groups", "gx"), check_vma=False
    )
```

profile of v0, /device:TPU:0, one launch (start us, length us, event | category | flops | bytes accessed | tf_op | source)
XLA Modules:
  0.0 122.0 jit_solution(11372717634072038642)
XLA Ops:
  6.5 0.0 copy-start
  6.5 0.0 all-reduce.9.cloned.1.call-start
  6.5 0.8 convert_element_type.46
  7.4 8.8 %fusion.2 = f32[2,8,2048]{2,1,0:T(8,128)} fusion(bf16[4096,2048]{1,0:T(8,128)(2,1)} %param.10, bf16[2,8,4096]{2,1,0:T(8,128)(2,1)} %param.7, f32[4096]{0:T(1024)S(1)} %convert_element_type.46), kind=kOutput, calls=%fused_computation.2 | convolution fusion | flops 268632064 | bytes 17055744 | tf_op jit(solution)/shard_map/mrd,dc->mrc/dot_general | solution.py:71
  16.2 0.0 all-reduce.9.cloned.1.call-update
  16.2 0.0 all-reduce.7.cloned.1.call-start
  16.3 0.0 copy-done.1
  16.3 0.1 fusion.13
  16.4 0.1 iota_compare_fusion
  16.5 0.4 fusion.9
  16.9 0.0 copy-done.3
  16.9 0.7 dynamic-slice
  18.3 0.1 multiply_cosine_fusion.1
  18.4 20.8 %all-reduce.3 = (f32[2,8]{1,0:T(2,128)S(1)}, f32[2,8,1,256]{3,1,0,2:T(8,128)S(1)}) all-reduce(f32[2,8]{1,0:T(2,128)S(1)} %fusion.13, f32[2,8,1,256]{3,1,0,2:T(8,128)S(1)} %fusion.9), channel_id=3, replica_groups=mesh['groups'=2,'gx'=4,'gy'=4] {'gx'}, use_global_device_ids=true, to_apply=%region_2.0.clone | all-reduce | flops 4112 | bytes 32896
  39.2 0.1 fusion.32
  39.3 0.1 dynamic-slice_multiply_fusion
  39.4 0.1 fusion.29
  39.5 6.9 %fusion.35 = (bf16[2,2,1024,1,1,128]{5,4,3,2,1,0:T(2,128)(2,1)}, bf16[2,2,1024,1,1,128]{5,4,3,2,1,0:T(2,128)(2,1)}) fusion(bf16[2,2,1024,1,2,128]{5,4,3,2,1,0:T(2,128)(2,1)} %param.13), kind=kLoop, calls=%fused_computation.55 | loop fusion | bytes 4194304 | tf_op jit(solution)/shard_map/slice | solution.py:38
  46.4 0.1 maximum_bitcast_fusion
  46.5 7.3 %all-reduce.9.cloned.1.call-done = f32[2,8,2048]{2,1,0:T(8,128)} async-done(((f32[2,8,2048]{2,1,0:T(8,128)}), f32[2,8,2048]{2,1,0:T(8,128)}) %all-reduce.9.cloned.1.call-update) | async-done | bytes 131088
  53.9 0.9 constant_dynamic-slice_fusion
  54.8 0.1 broadcast_multiply_fusion
  54.9 0.1 subtract_convert_fusion
  55.0 0.2 multiply_reduce_fusion
  55.1 2.1 %fusion.36 = (f32[2,2,16]{2,1,0:T(2,128)S(1)}, f32[2,2,16,1024]{3,2,1,0:T(8,128)S(1)}) fusion(bf16[2,2,1024,1,1,128]{5,4,3,2,1,0:T(2,128)(2,1)} %get-tuple-element.9, bf16[2,2,16,64]{3,2,1,0:T(8,128)(2,1)S(1)} %bitcast.38, bf16[2,2,16,64]{3,2,1,0:T(8,128)(2,1)S(1)} %bitcast.37, pred[2,2,1024]{2,1,0:T(4,128)(4,1)S(1)} %iota_compare_fusion), kind=kOutput, calls=%fused_computation.56 | convolution fusion | flops 17006528 | bytes 1331456 | tf_op jit(solution)/shard_map/mrkgd,mrskd->mrkgs/dot_general | solution.py:41
  57.3 0.2 fusion.15
  57.5 1.9 %fusion.8 = bf16[2,2,16,128]{3,2,1,0:T(8,128)(2,1)S(1)} fusion(bf16[2,2,1024,1,1,128]{5,4,3,2,1,0:T(2,128)(2,1)} %get-tuple-element.10, f32[2,2,16,1024]{3,2,1,0:T(8,128)S(1)} %get-tuple-element.18, f32[2,2,16]{2,1,0:T(2,128)S(1)} %multiply_maximum_fusion, f32[2,2,16]{2,1,0:T(2,128)S(1)} %get-tuple-element.7, f32[2,2,128]{2,1,0:T(2,128)S(1)} %slice_bitcast_fusion, ...), kind=kOutput, calls=%fused_computation.10 | convolution fusion | flops 16941056 | bytes 1329920 | tf_op jit(solution)/shard_map/mrkgs,mrskd->mrkgd/dot_general | solution.py:53
  59.4 13.1 %all_gather.3 = bf16[2,8,2048]{2,0,1:T(2,128)(2,1)S(1)} all-gather(bf16[2,2,2048]{2,0,1:T(2,128)(2,1)S(1)} %copy.12), channel_id=1, replica_groups=mesh['groups'=2,'gx'=4,'gy'=4] {'gx'}, dimensions={1}, use_global_device_ids=true | all-gather | bytes 81920 | tf_op jit(solution)/shard_map/all_gather | solution.py:83
  72.6 8.8 %fusion = f32[2,8,4096]{2,1,0:T(8,128)} fusion(bf16[2048,4096]{1,0:T(8,128)(2,1)} %param.12, bf16[2,8,2048]{2,0,1:T(2,128)(2,1)S(1)} %all_gather.3), kind=kOutput, calls=%fused_computation | convolution fusion | flops 268435456 | bytes 17104896 | tf_op jit(solution)/shard_map/mrc,cd->mrd/dot_general | solution.py:81
  81.3 0.0 all-reduce.7.cloned.1.call-update
  81.3 32.2 %all-reduce.7.cloned.1.call-done = f32[2,8,4096]{2,1,0:T(8,128)} async-done(((f32[2,8,4096]{2,1,0:T(8,128)}), f32[2,8,4096]{2,1,0:T(8,128)}) %all-reduce.7.cloned.1.call-update) | async-done | bytes 262160 | tf_op jit(solution)/shard_map/psum | solution.py:87
  113.5 1.6 %fusion.14 = bf16[2,8,4096]{2,1,0:T(8,128)(2,1)} fusion(f32[2,8,4096]{2,1,0:T(8,128)} %all-reduce.7.cloned.1.call-done, bf16[2,8,4096]{2,1,0:T(8,128)(2,1)S(1)} %copy-done.1), kind=kLoop, calls=%fused_computation.19 | loop fusion | flops 196608 | bytes 524288 | tf_op jit(solution)/shard_map/convert_element_type | solution.py:88
  (13 shorter events, 0.1 us)
Async XLA Ops:
  6.5 10.0 %copy-start = (bf16[4096,1,256]{2,0,1:T(8,128)(2,1)S(1)}, bf16[4096,1,256]{2,0,1:T(8,128)(2,1)}, u32[]{:S(2)}) copy-start(bf16[4096,1,256]{2,0,1:T(8,128)(2,1)} %param.11) | copy-start | bytes 6291460
  6.5 47.3 %all-reduce.9.cloned.1.call-start = ((), (), s32[]{:S(2)}) async-start(), calls=%async_computation.1 | async-start | bytes 262144
  7.4 8.9 %copy-start.1 = (bf16[2,8,4096]{2,1,0:T(8,128)(2,1)S(1)}, bf16[2,8,4096]{2,1,0:T(8,128)(2,1)}, u32[]{:S(2)}) copy-start(bf16[2,8,4096]{2,1,0:T(8,128)(2,1)} %param.7) | copy-start | bytes 393220
  7.4 9.0 %copy-start.2 = (s32[2,2]{1,0:T(2,128)S(1)}, s32[2,2]{1,0:T(2,128)}, u32[]{:S(2)}) copy-start(s32[2,2]{1,0:T(2,128)} %param.8) | copy-start | bytes 52
  16.2 0.7 copy-start.3
  16.2 97.3 %all-reduce.7.cloned.1.call-start = ((), (), s32[]{:S(2)}) async-start(), calls=%async_computation | async-start | bytes 524288 | tf_op jit(solution)/shard_map/psum | solution.py:87
Sparse Core Ops, SparseCore 0:
  16.4 37.4 all-reduce.8
  81.5 31.9 all-reduce.6
where the time goes:
time: 122 us
  waiting for transfers between devices  39.5 us (32%)
  blocking collectives  33.9 us (28%)
  matrix products  22 us (18%)
  between operations  14.2 us (12%)
  local copies, waits for them, and re-layouts  8.61 us (7%)
  other arithmetic  3.71 us (3%)
    psum x1, waiting for transfers between devices, local(): summed_heads = lax.psum(projected, 'gy')  32.2 us
    unnamed x1, blocking collectives  20.8 us
    all_gather x1, blocking collectives, local(): lax.all_gather(attended, 'gx', axis=1, tiled=True)  13.1 us
    dot_general x1, matrix products, local(): jnp.einsum('mrd,dc->mrc', normed, w_query, preferred_element_type=jnp.flo...  8.81 us
    dot_general x1, matrix products, local(): jnp.einsum('mrc,cd->mrd', lax.all_gather(attended, 'gx', axis=1, tiled=Tr...  8.75 us
    unnamed x3, waiting for transfers between devices  7.38 us
    slice x1, local copies, waits for them, and re-layouts, attend(): keys = cache[:, :, :, :, 0, :]  6.95 us
  transfers between devices with their start and end apart: 2, of which 2 were waited for; matrix products, arithmetic and copies ran while one was open for 7% of the time, Pallas kernels for 0%

commit v1 on v0

v1 whole, which is shorter than its diff:
```python
import functools

import jax
import jax.numpy as jnp
from jax import lax
from jax.experimental import pallas as pl
from jax.experimental.pallas import tpu as pltpu
from jax.sharding import PartitionSpec as P

HEAD_SIZE = 128
LANES = 128
VMEM = pl.BlockSpec(memory_space=pltpu.VMEM)
SMEM = pl.BlockSpec(memory_space=pltpu.SMEM)
ANY = pl.BlockSpec(memory_space=pl.ANY)
HBM = pl.BlockSpec(memory_space=pltpu.HBM)
F32 = jnp.float32
BF16 = jnp.bfloat16


def exchange(value, axis, size, step):
    return lax.ppermute(value, axis, [(i, i ^ step) for i in range(size)])


def in_hbm(value):
    return pltpu.with_memory_space_constraint(value, pltpu.HBM)


def params(mib):
    return pltpu.CompilerParams(vmem_limit_bytes=mib * 2**20)


def project_kernel(chunks, gx, position, tokens, gain, wq_hbm, wkv_hbm, *refs):
    outs = refs[:gx]
    wq, wkv, normed, sums, staged, sems = refs[gx:]
    depth = wq.shape[0] // chunks
    copies = []
    for c in range(chunks):
        part = (pl.ds(c * depth, depth), slice(None))
        copies.append(
            (
                pltpu.make_async_copy(wq_hbm.at[part], wq.at[part], sems.at[0, c]),
                pltpu.make_async_copy(wkv_hbm.at[part], wkv.at[part], sems.at[1, c]),
            )
        )
        for copy in copies[-1]:
            copy.start()
    batches, rows, width = tokens.shape
    total = batches * rows
    queries = wq.shape[1]
    keyvals = wkv.shape[1]
    x_full = tokens[...].astype(F32)
    squares = jnp.sum(x_full * x_full, axis=-1, keepdims=True).reshape(total, 1)
    sums[:, queries + keyvals :] = jnp.broadcast_to(squares, (total, LANES))
    scaled = (x_full * gain[...].astype(F32)).astype(BF16)
    normed[...] = scaled.reshape(total, width)
    for c in range(chunks):
        for copy in copies[c]:
            copy.wait()
        left = normed[:, c * depth : (c + 1) * depth]
        for weights, start, stop in ((wq, 0, queries), (wkv, queries, queries + keyvals)):
            part = jnp.dot(
                left, weights[c * depth : (c + 1) * depth, :], preferred_element_type=F32
            )
            if c == 0:
                sums[:, start:stop] = part
            else:
                sums[:, start:stop] += part
    here = rows // gx
    for place in range(gx):
        for m in range(batches):
            first = m * rows + place * here
            staged[place, m * here : (m + 1) * here, :] = sums[first : first + here, :]
    for k in range(gx):
        outs[k][...] = staged[position[0] ^ k]


def project(position, tokens, gain, wq, wkv, gx):
    batches, rows, width = tokens.shape
    columns = wq.shape[1] + wkv.shape[1] + LANES
    chunks = max(1, width // 256)
    return pl.pallas_call(
        functools.partial(project_kernel, chunks, gx),
        out_shape=[jax.ShapeDtypeStruct((batches * rows // gx, columns), F32)] * gx,
        in_specs=[SMEM, VMEM, VMEM, HBM, HBM],
        out_specs=[VMEM] * gx,
        scratch_shapes=[
            pltpu.VMEM(wq.shape, BF16),
            pltpu.VMEM(wkv.shape, BF16),
            pltpu.VMEM((batches * rows, width), BF16),
            pltpu.VMEM((batches * rows, columns), F32),
            pltpu.VMEM((gx, batches * rows // gx, columns), F32),
            pltpu.SemaphoreType.DMA((2, chunks)),
        ],
        compiler_params=params(24),
        name="project",
    )(position, tokens, gain, wq, wkv)


def stage_kernel(sent, cache_hbm, w_hbm, cache, weights, sems):
    del sent
    copies = [
        pltpu.make_async_copy(cache_hbm, cache, sems.at[0]),
        pltpu.make_async_copy(w_hbm.at[pl.ds(0, weights.shape[0])], weights, sems.at[1]),
    ]
    for copy in copies:
        copy.start()
    for copy in copies:
        copy.wait()


def stage(sent, cache, w_out, rows):
    return pl.pallas_call(
        stage_kernel,
        out_shape=[
            pltpu.VMEM(cache.shape, BF16),
            pltpu.VMEM((rows, w_out.shape[1]), BF16),
        ],
        in_specs=[ANY, HBM, HBM],
        out_specs=[VMEM, VMEM],
        scratch_shapes=[pltpu.SemaphoreType.DMA((2,))],
        compiler_params=params(1),
        name="stage",
    )(sent, cache, w_out)


def attend_kernel(model_width, parts, first, lengths, angles, *refs):
    received = refs[:parts]
    cache, w_hbm, out, weights_out, table, sem = refs[parts:]
    rows = cache.shape[0]
    load = pltpu.make_async_copy(
        w_hbm.at[pl.ds(first, weights_out.shape[0])], weights_out, sem
    )
    load.start()
    half = HEAD_SIZE // 2
    group = out.shape[1] // HEAD_SIZE
    queries = group * HEAD_SIZE
    sums = received[0][...]
    for k in range(1, parts):
        sums = sums + received[k][...]
    scale = lax.rsqrt(sums[:, queries + 2 * HEAD_SIZE :] / model_width + 1e-05)
    cosine = angles[0]
    sine = angles[1]

    def rotate(vectors):
        return vectors * cosine + pltpu.roll(vectors, half, 1) * sine

    def column(start):
        return sums[:, start : start + HEAD_SIZE] * scale

    for h in range(group):
        table[pl.ds(h, rows, stride=group), :] = rotate(column(h * HEAD_SIZE))
    rkey = rotate(column(queries))
    value_new = column(queries + HEAD_SIZE)
    inv_root = 1.0 / jnp.sqrt(jnp.float32(HEAD_SIZE))
    for r in range(rows):
        query = table[r * group : (r + 1) * group, :].astype(BF16)
        pairs = cache[r]
        scores = (
            lax.dot_general(query, pairs, (((1,), (1,)), ((), ())), preferred_element_type=F32)
            * inv_root
        )
        place = lax.broadcasted_iota(jnp.int32, scores.shape, 1)
        valid = jnp.logical_and(place < 2 * lengths[r], (place & 1) == 0)
        scores = jnp.where(valid, scores, -1e30)
        new_score = (
            jnp.sum(query.astype(F32) * rkey[r : r + 1, :], axis=-1, keepdims=True) * inv_root
        )
        top = jnp.maximum(jnp.max(scores, axis=-1, keepdims=True), new_score)
        weights = jnp.exp(scores - top)
        new_weight = jnp.exp(new_score - top)
        total = jnp.sum(weights, axis=-1, keepdims=True) + new_weight
        weights = pltpu.roll(weights, 1, 1).astype(BF16)
        summed = jnp.dot(weights, pairs, preferred_element_type=F32)
        summed = summed + new_weight * value_new[r : r + 1, :]
        table[r * group : (r + 1) * group, :] = summed / total
    for h in range(group):
        out[:, h * HEAD_SIZE : (h + 1) * HEAD_SIZE] = table[
            pl.ds(h, rows, stride=group), :
        ].astype(BF16)
    load.wait()


def attend(model_width, lengths, angles, received, cache, queries, w_out, first, count):
    rows = cache.shape[0]
    return pl.pallas_call(
        functools.partial(attend_kernel, model_width, len(received), first),
        out_shape=[
            jax.ShapeDtypeStruct((rows, queries), BF16),
            pltpu.VMEM((count, w_out.shape[1]), BF16),
        ],
        in_specs=[SMEM, VMEM] + [VMEM] * len(received) + [VMEM, HBM],
        out_specs=[VMEM, VMEM],
        scratch_shapes=[
            pltpu.VMEM((rows * queries // HEAD_SIZE, HEAD_SIZE), F32),
            pltpu.SemaphoreType.DMA,
        ],
        compiler_params=params(4),
        name="attend",
    )(lengths, angles, *received, cache, w_out)


def output_kernel(chunks, gx, batches, position, *refs):
    received = refs[:gx]
    begun, middle, w_hbm, out, weights, blocks, left, sems = refs[gx:]
    first = begun.shape[0] + middle.shape[0]
    depth = weights.shape[0] // chunks
    copies = []
    for c in range(chunks):
        copies.append(
            pltpu.make_async_copy(
                w_hbm.at[pl.ds(first + c * depth, depth)],
                weights.at[pl.ds(c * depth, depth)],
                sems.at[c],
            )
        )
        copies[-1].start()
    here = received[0].shape[0] // batches
    rows = here * gx
    for k in range(gx):
        blocks[position[0] ^ k] = received[k][...].astype(F32)
    for place in range(gx):
        for m in range(batches):
            start = m * rows + place * here
            left[start : start + here, :] = blocks[place, m * here : (m + 1) * here, :]

    def product(start, ref, stop):
        return jnp.dot(
            left[:, start : start + stop].astype(BF16), ref, preferred_element_type=F32
        )

    out[...] = product(0, begun[...], begun.shape[0])
    out[...] += product(begun.shape[0], middle[...], middle.shape[0])
    for c in range(chunks):
        copies[c].wait()
        out[...] += product(
            first + c * depth, weights[c * depth : (c + 1) * depth, :], depth
        )


def output(position, received, begun, middle, w_out, batches):
    gx = len(received)
    rows = received[0].shape[0] * gx
    rest = w_out.shape[0] - begun.shape[0] - middle.shape[0]
    chunks = max(1, rest // 256)
    return pl.pallas_call(
        functools.partial(output_kernel, chunks, gx, batches),
        out_shape=jax.ShapeDtypeStruct((rows, w_out.shape[1]), F32),
        in_specs=[SMEM] + [VMEM] * (gx + 2) + [HBM],
        out_specs=VMEM,
        scratch_shapes=[
            pltpu.VMEM((rest, w_out.shape[1]), BF16),
            pltpu.VMEM((gx, rows // gx, w_out.shape[0]), F32),
            pltpu.VMEM((rows, w_out.shape[0]), F32),
            pltpu.SemaphoreType.DMA((chunks,)),
        ],
        compiler_params=params(8),
        name="output",
    )(position, *received, begun, middle, w_out)


def rotation(lengths):
    half = HEAD_SIZE // 2
    freq = 500000.0 ** (-2.0 * jnp.arange(half, dtype=F32) / HEAD_SIZE)
    angle = lengths.reshape(-1, 1).astype(F32) * freq
    cosine = jnp.cos(angle)
    sine = jnp.sin(angle)
    return jnp.stack(
        [jnp.concatenate([cosine, cosine], axis=-1), jnp.concatenate([-sine, sine], axis=-1)]
    )


def add_heads(value, axis, size):
    step = 1
    while step < size:
        if step > 1:
            value = value.astype(BF16)
        other = exchange(value, axis, size, step)
        value = value.astype(F32) + other.astype(F32)
        step *= 2
    return value


def local(gx, gy, tokens, lengths, norm_gain, w_query, key_value_weight, w_out, cache):
    batches, rows, width = tokens.shape
    queries = w_query.shape[1]
    wkv = in_hbm(key_value_weight.reshape(width, -1))
    w_query = in_hbm(w_query)
    w_out = in_hbm(w_out)
    pairs = in_hbm(cache.reshape(-1, 2 * cache.shape[2], HEAD_SIZE))
    position = lax.axis_index("gx").reshape(1)
    sent = project(position, tokens, norm_gain.reshape(1, -1), w_query, wkv, gx)
    received = [sent[0]] + [exchange(sent[k], "gx", gx, k) for k in reversed(range(1, gx))]
    angles = rotation(lengths)
    depth = w_out.shape[0]
    pairs, begun = stage(sent[0], pairs, w_out, depth // 4)
    attended, middle = attend(
        width * gx, lengths.reshape(-1), angles, received, pairs, queries, w_out, depth // 4, depth // 2
    )
    gathered = {k: exchange(attended, "gx", gx, k) for k in reversed(range(1, gx))}
    gathered[0] = attended
    projected = output(
        position, [gathered[k] for k in range(gx)], begun, middle, w_out, batches
    )
    summed = add_heads(projected, "gy", gy).reshape(tokens.shape)
    return (tokens.astype(F32) + summed).astype(BF16)


def rotate(vectors, positions):
    half = vectors.shape[-1] // 2
    freq = 500000.0 ** (-2.0 * jnp.arange(half, dtype=F32) / vectors.shape[-1])
    angle = positions[..., None] * freq
    cosine = jnp.cos(angle)
    sine = jnp.sin(angle)
    first = vectors[..., :half]
    second = vectors[..., half:]
    return jnp.concatenate(
        [first * cosine - second * sine, second * cosine + first * sine], axis=-1
    )


def attend_wide(model_width, query_sum, keyval_sum, local_squares, lengths, cache):
    batches, rows_here = lengths.shape
    score_scale = lax.rsqrt(local_squares / model_width + 1e-05)
    heads_kv = keyval_sum.shape[2]
    query_group = query_sum.shape[2] // (heads_kv * HEAD_SIZE)
    query = (
        query_sum.reshape(batches, rows_here, heads_kv, query_group, HEAD_SIZE)
        * score_scale[:, :, None, None, None]
    )
    key_value = keyval_sum * score_scale[:, :, None, None]
    positions = lengths.astype(F32)
    rotated_query = rotate(query, positions[:, :, None, None]).astype(BF16)
    rkey = rotate(key_value[..., :HEAD_SIZE], positions[:, :, None])
    value_new = key_value[..., HEAD_SIZE:]
    inv_root = 1.0 / jnp.sqrt(jnp.float32(HEAD_SIZE))
    keys = cache[:, :, :, :, 0, :]
    values = cache[:, :, :, :, 1, :]
    scores = (
        jnp.einsum("mrkgd,mrskd->mrkgs", rotated_query, keys, preferred_element_type=F32)
        * inv_root
    )
    valid = jnp.arange(cache.shape[2], dtype=jnp.int32)[None, None, :] < lengths[:, :, None]
    scores = jnp.where(valid[:, :, None, None, :], scores, -1e30)
    new_score = jnp.sum(rotated_query.astype(F32) * rkey[:, :, :, None, :], axis=-1) * inv_root
    top = jnp.maximum(jnp.max(scores, axis=-1), new_score)
    weights = jnp.exp(scores - top[..., None])
    new_weight = jnp.exp(new_score - top)
    total = jnp.sum(weights, axis=-1) + new_weight
    summed = jnp.einsum(
        "mrkgs,mrskd->mrkgd", weights.astype(BF16), values, preferred_element_type=F32
    )
    summed = summed + new_weight[..., None] * value_new[:, :, :, None, :]
    return (
        (summed / total[..., None])
        .astype(BF16)
        .reshape(batches, rows_here, heads_kv * query_group * HEAD_SIZE)
    )


def local_wide(gx, tokens, lengths, norm_gain, w_query, key_value_weight, w_out, cache):
    x_full = tokens.astype(F32)
    squares = jnp.sum(x_full * x_full, axis=-1)
    normed = (x_full * norm_gain.astype(F32)).astype(BF16)
    query_part = jnp.einsum("mrd,dc->mrc", normed, w_query, preferred_element_type=F32)
    keyval_part = jnp.einsum("mrd,dkc->mrkc", normed, key_value_weight, preferred_element_type=F32)
    query_sum, keyval_sum, local_squares = (
        lax.psum_scatter(query_part, "gx", scatter_dimension=1, tiled=True),
        lax.psum_scatter(keyval_part, "gx", scatter_dimension=1, tiled=True),
        lax.psum_scatter(squares, "gx", scatter_dimension=1, tiled=True),
    )
    attended = attend_wide(
        tokens.shape[-1] * gx, query_sum, keyval_sum, local_squares, lengths, cache
    )
    projected = jnp.einsum(
        "mrc,cd->mrd",
        lax.all_gather(attended, "gx", axis=1, tiled=True),
        w_out,
        preferred_element_type=F32,
    )
    return (x_full + lax.psum(projected, "gy")).astype(BF16)


def solution(mesh):
    gx, gy = mesh.shape["gx"], mesh.shape["gy"]
    placed = (
        P(None, "groups", "gx"),
        P(None, ("groups", "gx")),
        P("gx"),
        P("gx", "gy"),
        P("gx", "gy", None),
        P("gy", "gx"),
        P(None, ("groups", "gx"), None, "gy", None, None),
    )

    def run(*args):
        kv_heads_here = args[4].shape[1]
        direct = gx <= 8 and gx & (gx - 1) == 0 and gy & (gy - 1) == 0 and kv_heads_here == 1
        if direct:
            return local(gx, gy, *args)
        return local_wide(gx, *args)

    return jax.shard_map(
        run, mesh=mesh, in_specs=placed, out_specs=P(None, "groups", "gx"), check_vma=False
    )
```

time: 122 us -> 43.2 us (0.35)
  blocking collectives: 33.9 us -> 0 us
  waiting for transfers between devices: 39.5 us -> 9.59 us
  matrix products: 22 us -> 0 us
  Pallas kernels: 0 us -> 18.8 us
  between operations: 14.2 us -> 0.08 us
  starting transfers between devices: 0.04 us -> 11.9 us
  local copies, waits for them, and re-layouts: 8.61 us -> 1.69 us
  other arithmetic: 3.71 us -> 0.94 us
    psum x1 -> x0, waiting for transfers between devices: 32.2 us -> none  [local(): summed_heads = lax.psum(projected, 'gy')]
    dot_general x5 -> x0, matrix products: 22 us -> none  [the longest x1 8.81 us: local(): jnp.einsum('mrd,dc->mrc', normed, w_query, preferred_element_type=jnp.flo...]
    unnamed x1 -> x0, blocking collectives: 20.8 us -> none
    pallas_call x0 -> x4, Pallas kernels: none -> 18.8 us  [the longest x1 6.96 us: project(): pl.pallas_call(functools.partial(project_kernel, chunks, gx), out_shape=[...]
    all_gather x1 -> x0, blocking collectives: 13.1 us -> none  [local(): lax.all_gather(attended, 'gx', axis=1, tiled=True)]
    ppermute x0 -> x8, starting transfers between devices: none -> 11.9 us  [exchange(): return lax.ppermute(value, axis, [(i, i ^ step) for i in range(size)])]
    ppermute x0 -> x8, waiting for transfers between devices: none -> 9.59 us  [exchange(): return lax.ppermute(value, axis, [(i, i ^ step) for i in range(size)])]
    unnamed x3 -> x0, waiting for transfers between devices: 7.38 us -> none
  transfers between devices with their start and end apart: 2 -> 8, of which waited for: 2 -> 5; matrix products, arithmetic and copies ran while one was open for 7% -> 1% of each run, Pallas kernels for 0% -> 7%
where the time goes in v1:
time: 43.2 us; the launch traced here: 43 us
  Pallas kernels  18.8 us (44%)
  starting transfers between devices  11.9 us (28%)
  waiting for transfers between devices  9.59 us (22%)
  local copies, waits for them, and re-layouts  1.69 us (4%)
  other arithmetic  0.94 us (2%)
    ppermute x8, starting transfers between devices, exchange(): return lax.ppermute(value, axis, [(i, i ^ step) for i in range(size)])  11.9 us
    ppermute x8, waiting for transfers between devices, exchange(): return lax.ppermute(value, axis, [(i, i ^ step) for i in range(size)])  9.59 us
    pallas_call x1, Pallas kernels, project(): pl.pallas_call(functools.partial(project_kernel, chunks, gx), out_shape=[...  6.96 us
    pallas_call x1, Pallas kernels, attend(): pl.pallas_call(functools.partial(attend_kernel, model_width, len(received...  5.87 us
    pallas_call x1, Pallas kernels, output(): pl.pallas_call(functools.partial(output_kernel, chunks, gx, batches), out...  3.16 us
    pallas_call x1, Pallas kernels, stage(): pl.pallas_call(stage_kernel, out_shape=[pltpu.VMEM(cache.shape, BF16), pl...  2.85 us
    unnamed x6, local copies, waits for them, and re-layouts  0.91 us
  transfers between devices with their start and end apart: 8, of which 5 were waited for; matrix products, arithmetic and copies ran while one was open for 1% of the time, Pallas kernels for 7%

profile of v1, /device:TPU:0, one launch (start us, length us, event | category | flops | bytes accessed | tf_op | source)
XLA Modules:
  0.0 43.0 jit_solution(6166377162679792793)
XLA Ops:
  0.0 0.7 %reshape.33.gain = bf16[1,4096]{1,0:T(2,128)(2,1)S(1)} reshape(bf16[4096]{0:T(1024)(128)(2,1)} %param.9) | data formatting | bytes 16384 | tf_op jit(solution)/shard_map/reshape | solution.py:291
  0.7 0.0 copy-start
  0.7 0.9 %copy-done = bf16[2,8,4096]{2,1,0:T(8,128)(2,1)S(1)} copy-done((bf16[2,8,4096]{2,1,0:T(8,128)(2,1)S(1)}, bf16[2,8,4096]{2,1,0:T(8,128)(2,1)}, u32[]{:S(2)}) %copy-start) | copy-done | bytes 131096
  1.6 0.0 copy-start.2
  1.6 7.0 %project.1 = (f32[4,2432]{1,0:T(4,128)S(1)}, f32[4,2432]{1,0:T(4,128)S(1)}, f32[4,2432]{1,0:T(4,128)S(1)}, f32[4,2432]{1,0:T(4,128)S(1)}) custom-call(s32[1]{0:T(128)} %bitcast.position, bf16[2,8,4096]{2,1,0:T(8,128)(2,1)S(1)} %copy-done, bf16[1,4096]{1,0:T(2,128)(2,1)S(1)} %reshape.33.gain, bf16[4096,2048]{1,0:T(8,128)(2,1)} %wq_hbm.1, ...), custom_call_target="tpu_custom_call" | custom-call | tf_op jit(solution)/shard_map/project/pallas_call | solution.py:81
  8.6 5.1 %collective-permute-start = (f32[4,2432]{1,0:T(4,128)S(1)}, f32[4,2432]{1,0:T(4,128)S(1)}, u32[]{:S(2)}, u32[]{:S(2)}) collective-permute-start(f32[4,2432]{1,0:T(4,128)S(1)} %get-tuple-element.14), channel_id=1, source_target_pairs={{0,12},{4,8},{8,4},{12,0},{1,13},{5,9},{9,5},{13,1},{2,14},{6,10},... | collective-permute-start | bytes 116744 | tf_op jit(solution)/shard_map/ppermute | solution.py:21
  13.7 0.0 collective-permute-start.1
  13.7 0.6 %collective-permute-start.2 = (f32[4,2432]{1,0:T(4,128)S(1)}, f32[4,2432]{1,0:T(4,128)S(1)}, u32[]{:S(2)}, u32[]{:S(2)}) collective-permute-start(f32[4,2432]{1,0:T(4,128)S(1)} %get-tuple-element.16), channel_id=1, source_target_pairs={{0,4},{4,0},{8,12},{12,8},{1,5},{5,1},{9,13},{13,9},{2,6},{6,2},{1... | collective-permute-start | bytes 116744 | tf_op jit(solution)/shard_map/ppermute | solution.py:21
  14.4 0.0 copy-done.2
  14.4 0.1 reshape.32.lengths
  14.5 0.1 multiply_cosine_fusion
  14.6 0.1 maximum_bitcast_fusion
  14.7 2.8 %stage.1 = (bf16[4,2048,128]{2,1,0:T(8,128)(2,1)S(1)}, bf16[512,4096]{1,0:T(8,128)(2,1)S(1)}) custom-call(f32[4,2432]{1,0:T(4,128)S(1)} %get-tuple-element.13.sent.refs_0_, bf16[4,2048,128]{2,1,0:T(8,128)(2,1)} %bitcast.12, bf16[2048,4096]{1,0:T(8,128)(2,1)} %refs_6_.1), custom_call_target="tpu_custom_call" | custom-call | tf_op jit(solution)/shard_map/stage/pallas_call | solution.py:112
  17.5 0.0 collective-permute-done.refs_1_
  17.5 1.1 %collective-permute-done.1.refs_2_ = f32[4,2432]{1,0:T(4,128)S(1)} collective-permute-done((f32[4,2432]{1,0:T(4,128)S(1)}, f32[4,2432]{1,0:T(4,128)S(1)}, u32[]{:S(2)}, u32[]{:S(2)}) %collective-permute-start.1) | collective-permute-done | bytes 38944 | tf_op jit(solution)/shard_map/ppermute | solution.py:21
  18.6 0.0 collective-permute-done.2.refs_3_
  18.6 5.9 %attend.1 = (bf16[4,2048]{1,0:T(4,128)(2,1)S(1)}, bf16[1024,4096]{1,0:T(8,128)(2,1)S(1)}) custom-call(s32[4]{0:T(128)S(1)} %reshape.32.lengths, f32[2,4,128]{2,1,0:T(4,128)S(1)} %pad_maximum_fusion.angles, f32[4,2432]{1,0:T(4,128)S(1)} %get-tuple-element.13.sent.refs_0_, f32[4,2432]{1,0:T(4,128)S(1)} %collective-permute-done.refs_1_, ...), custom_call_target="tpu_custom_call" | custom-call | tf_op jit(solution)/shard_map/attend/pallas_call | solution.py:185
  24.5 2.8 %collective-permute-start.5 = (bf16[4,2048]{1,0:T(4,128)(2,1)S(1)}, bf16[4,2048]{1,0:T(4,128)(2,1)S(1)}, u32[]{:S(2)}, u32[]{:S(2)}) collective-permute-start(bf16[4,2048]{1,0:T(4,128)(2,1)S(1)} %get-tuple-element.18.refs_0_), channel_id=1, source_target_pairs={{0,12},{4,8},{8,4},{12,0},{1,13},{5,9},{9,5},{13,1},{2,14},{6,10},... | collective-permute-start | bytes 49160 | tf_op jit(solution)/shard_map/ppermute | solution.py:21
  27.3 0.0 collective-permute-start.4
  27.3 1.7 %collective-permute-start.3 = (bf16[4,2048]{1,0:T(4,128)(2,1)S(1)}, bf16[4,2048]{1,0:T(4,128)(2,1)S(1)}, u32[]{:S(2)}, u32[]{:S(2)}) collective-permute-start(bf16[4,2048]{1,0:T(4,128)(2,1)S(1)} %get-tuple-element.18.refs_0_), channel_id=1, source_target_pairs={{0,4},{4,0},{8,12},{12,8},{1,5},{5,1},{9,13},{13,9},{2,6},{6,2},{1... | collective-permute-start | bytes 49160 | tf_op jit(solution)/shard_map/ppermute | solution.py:21
  29.0 1.1 %collective-permute-done.5.refs_3_ = bf16[4,2048]{1,0:T(4,128)(2,1)S(1)} collective-permute-done((bf16[4,2048]{1,0:T(4,128)(2,1)S(1)}, bf16[4,2048]{1,0:T(4,128)(2,1)S(1)}, u32[]{:S(2)}, u32[]{:S(2)}) %collective-permute-start.5) | collective-permute-done | bytes 16416 | tf_op jit(solution)/shard_map/ppermute | solution.py:21
  30.1 1.8 %collective-permute-done.4.refs_2_ = bf16[4,2048]{1,0:T(4,128)(2,1)S(1)} collective-permute-done((bf16[4,2048]{1,0:T(4,128)(2,1)S(1)}, bf16[4,2048]{1,0:T(4,128)(2,1)S(1)}, u32[]{:S(2)}, u32[]{:S(2)}) %collective-permute-start.4) | collective-permute-done | bytes 16416 | tf_op jit(solution)/shard_map/ppermute | solution.py:21
  31.9 0.0 collective-permute-done.3.refs_1_
  31.9 0.0 copy-start.1
  31.9 3.2 %output.1 = f32[16,4096]{1,0:T(8,128)S(1)} custom-call(s32[1]{0:T(128)} %bitcast.position, bf16[4,2048]{1,0:T(4,128)(2,1)S(1)} %get-tuple-element.18.refs_0_, bf16[4,2048]{1,0:T(4,128)(2,1)S(1)} %collective-permute-done.3.refs_1_, bf16[4,2048]{1,0:T(4,128)(2,1)S(1)} %collective-permute-done.4.refs_2_, bf16[4,2048]{1,0:T(4,128)(2,1)S(1)} %collective-permute-done.5.refs_3_, ...), custom_call_target="tpu_custom_call" | custom-call | tf_op jit(solution)/shard_map/output/pallas_call | solution.py:245
  35.1 0.1 collective-permute-start.6
  35.1 1.5 %collective-permute-done.6 = f32[16,4096]{1,0:T(8,128)S(1)} collective-permute-done((f32[16,4096]{1,0:T(8,128)S(1)}, f32[16,4096]{1,0:T(8,128)S(1)}, u32[]{:S(2)}, u32[]{:S(2)}) %collective-permute-start.6) | collective-permute-done | bytes 262176 | tf_op jit(solution)/shard_map/ppermute | solution.py:21
  36.7 1.6 %collective-permute-start.7 = (bf16[16,4096]{1,0:T(8,128)(2,1)S(1)}, bf16[16,4096]{1,0:T(8,128)(2,1)S(1)}, u32[]{:S(2)}, u32[]{:S(2)}) collective-permute-start(bf16[16,4096]{1,0:T(8,128)(2,1)S(1)} %add_convert_fusion), channel_id=1, source_target_pairs={{0,2},{1,3},{2,0},{3,1},{4,6},{5,7},{6,4},{7,5},{8,10},{9,11},{10,... | collective-permute-start | bytes 393224 | tf_op jit(solution)/shard_map/ppermute | solution.py:21
  38.3 4.0 %collective-permute-done.7 = bf16[16,4096]{1,0:T(8,128)(2,1)S(1)} collective-permute-done((bf16[16,4096]{1,0:T(8,128)(2,1)S(1)}, bf16[16,4096]{1,0:T(8,128)(2,1)S(1)}, u32[]{:S(2)}, u32[]{:S(2)}) %collective-permute-start.7) | collective-permute-done | bytes 131104 | tf_op jit(solution)/shard_map/ppermute | solution.py:21
  42.3 0.0 copy-done.1
  42.3 0.7 %fusion = bf16[2,8,4096]{2,1,0:T(8,128)(2,1)} fusion(bf16[16,4096]{1,0:T(8,128)(2,1)S(1)} %collective-permute-done.7, bf16[16,4096]{1,0:T(8,128)(2,1)S(1)} %add_convert_fusion, bf16[2,8,4096]{2,1,0:T(8,128)(2,1)S(1)} %copy-done.1), kind=kLoop, calls=%fused_computation.1 | loop fusion | flops 393216 | bytes 524288 | tf_op jit(solution)/shard_map/convert_element_type | solution.py:305
  (4 shorter events, 0.0 us)
Async XLA Ops:
  0.7 0.9 %copy-start = (bf16[2,8,4096]{2,1,0:T(8,128)(2,1)S(1)}, bf16[2,8,4096]{2,1,0:T(8,128)(2,1)}, u32[]{:S(2)}) copy-start(bf16[2,8,4096]{2,1,0:T(8,128)(2,1)} %tokens.1) | copy-start | bytes 393220
  1.6 12.8 %copy-start.2 = (s32[2,2]{1,0:T(2,128)S(1)}, s32[2,2]{1,0:T(2,128)}, u32[]{:S(2)}) copy-start(s32[2,2]{1,0:T(2,128)} %param.8) | copy-start | bytes 52
  8.6 8.9 %collective-permute-start = (f32[4,2432]{1,0:T(4,128)S(1)}, f32[4,2432]{1,0:T(4,128)S(1)}, u32[]{:S(2)}, u32[]{:S(2)}) collective-permute-start(f32[4,2432]{1,0:T(4,128)S(1)} %get-tuple-element.14), channel_id=1, source_target_pairs={{0,12},{4,8},{8,4},{12,0},{1,13},{5,9},{9,5},{13,1},{2,14},{6,10},... | collective-permute-start | bytes 116744 | tf_op jit(solution)/shard_map/ppermute | solution.py:21
  13.7 4.9 %collective-permute-start.1 = (f32[4,2432]{1,0:T(4,128)S(1)}, f32[4,2432]{1,0:T(4,128)S(1)}, u32[]{:S(2)}, u32[]{:S(2)}) collective-permute-start(f32[4,2432]{1,0:T(4,128)S(1)} %get-tuple-element.15), channel_id=1, source_target_pairs={{0,8},{4,12},{8,0},{12,4},{1,9},{5,13},{9,1},{13,5},{2,10},{6,14},... | collective-permute-start | bytes 116744 | tf_op jit(solution)/shard_map/ppermute | solution.py:21
  13.7 4.9 %collective-permute-start.2 = (f32[4,2432]{1,0:T(4,128)S(1)}, f32[4,2432]{1,0:T(4,128)S(1)}, u32[]{:S(2)}, u32[]{:S(2)}) collective-permute-start(f32[4,2432]{1,0:T(4,128)S(1)} %get-tuple-element.16), channel_id=1, source_target_pairs={{0,4},{4,0},{8,12},{12,8},{1,5},{5,1},{9,13},{13,9},{2,6},{6,2},{1... | collective-permute-start | bytes 116744 | tf_op jit(solution)/shard_map/ppermute | solution.py:21
  24.5 5.6 %collective-permute-start.5 = (bf16[4,2048]{1,0:T(4,128)(2,1)S(1)}, bf16[4,2048]{1,0:T(4,128)(2,1)S(1)}, u32[]{:S(2)}, u32[]{:S(2)}) collective-permute-start(bf16[4,2048]{1,0:T(4,128)(2,1)S(1)} %get-tuple-element.18.refs_0_), channel_id=1, source_target_pairs={{0,12},{4,8},{8,4},{12,0},{1,13},{5,9},{9,5},{13,1},{2,14},{6,10},... | collective-permute-start | bytes 49160 | tf_op jit(solution)/shard_map/ppermute | solution.py:21
  27.3 4.6 %collective-permute-start.4 = (bf16[4,2048]{1,0:T(4,128)(2,1)S(1)}, bf16[4,2048]{1,0:T(4,128)(2,1)S(1)}, u32[]{:S(2)}, u32[]{:S(2)}) collective-permute-start(bf16[4,2048]{1,0:T(4,128)(2,1)S(1)} %get-tuple-element.18.refs_0_), channel_id=1, source_target_pairs={{0,8},{4,12},{8,0},{12,4},{1,9},{5,13},{9,1},{13,5},{2,10},{6,14},... | collective-permute-start | bytes 49160 | tf_op jit(solution)/shard_map/ppermute | solution.py:21
  27.3 4.6 %collective-permute-start.3 = (bf16[4,2048]{1,0:T(4,128)(2,1)S(1)}, bf16[4,2048]{1,0:T(4,128)(2,1)S(1)}, u32[]{:S(2)}, u32[]{:S(2)}) collective-permute-start(bf16[4,2048]{1,0:T(4,128)(2,1)S(1)} %get-tuple-element.18.refs_0_), channel_id=1, source_target_pairs={{0,4},{4,0},{8,12},{12,8},{1,5},{5,1},{9,13},{13,9},{2,6},{6,2},{1... | collective-permute-start | bytes 49160 | tf_op jit(solution)/shard_map/ppermute | solution.py:21
  31.9 10.4 %copy-start.1 = (bf16[2,8,4096]{2,1,0:T(8,128)(2,1)S(1)}, bf16[2,8,4096]{2,1,0:T(8,128)(2,1)}, u32[]{:S(2)}) copy-start(bf16[2,8,4096]{2,1,0:T(8,128)(2,1)} %tokens.1) | copy-start | bytes 393220
  35.1 1.6 %collective-permute-start.6 = (f32[16,4096]{1,0:T(8,128)S(1)}, f32[16,4096]{1,0:T(8,128)S(1)}, u32[]{:S(2)}, u32[]{:S(2)}) collective-permute-start(f32[16,4096]{1,0:T(8,128)S(1)} %output.1), channel_id=1, source_target_pairs={{0,1},{1,0},{2,3},{3,2},{4,5},{5,4},{6,7},{7,6},{8,9},{9,8},{10,11... | collective-permute-start | bytes 786440 | tf_op jit(solution)/shard_map/ppermute | solution.py:21
  36.7 5.6 %collective-permute-start.7 = (bf16[16,4096]{1,0:T(8,128)(2,1)S(1)}, bf16[16,4096]{1,0:T(8,128)(2,1)S(1)}, u32[]{:S(2)}, u32[]{:S(2)}) collective-permute-start(bf16[16,4096]{1,0:T(8,128)(2,1)S(1)} %add_convert_fusion), channel_id=1, source_target_pairs={{0,2},{1,3},{2,0},{3,1},{4,6},{5,7},{6,4},{7,5},{8,10},{9,11},{10,... | collective-permute-start | bytes 393224 | tf_op jit(solution)/shard_map/ppermute | solution.py:21

commit v2 on v1

--- a/solution.py
+++ b/solution.py
@@ -29,21 +29,32 @@
     return pltpu.CompilerParams(vmem_limit_bytes=mib * 2**20)
 
 
-def project_kernel(chunks, gx, position, tokens, gain, wq_hbm, wkv_hbm, *refs):
+def project_kernel(chunks, gx, position, tokens_hbm, gain_hbm, wq_hbm, wkv_hbm, cache_hbm, *refs):
     outs = refs[:gx]
-    wq, wkv, normed, sums, staged, sems = refs[gx:]
+    cache, tokens, gain, wq, wkv, normed, sums, staged, small_sems, sems = refs[gx:]
     depth = wq.shape[0] // chunks
-    copies = []
-    for c in range(chunks):
+    small = [
+        pltpu.make_async_copy(tokens_hbm, tokens, small_sems.at[0]),
+        pltpu.make_async_copy(gain_hbm, gain, small_sems.at[1]),
+        pltpu.make_async_copy(cache_hbm, cache, small_sems.at[2]),
+    ]
+    small[0].start()
+    small[1].start()
+
+    def chunk(c):
         part = (pl.ds(c * depth, depth), slice(None))
-        copies.append(
-            (
-                pltpu.make_async_copy(wq_hbm.at[part], wq.at[part], sems.at[0, c]),
-                pltpu.make_async_copy(wkv_hbm.at[part], wkv.at[part], sems.at[1, c]),
-            )
-        )
-        for copy in copies[-1]:
+        return (
+            pltpu.make_async_copy(wq_hbm.at[part], wq.at[part], sems.at[0, c]),
+            pltpu.make_async_copy(wkv_hbm.at[part], wkv.at[part], sems.at[1, c]),
+        )
+
+    @pl.loop(0, chunks)
+    def _(c):
+        for copy in chunk(c):
             copy.start()
+
+    small[0].wait()
+    small[1].wait()
     batches, rows, width = tokens.shape
     total = batches * rows
     queries = wq.shape[1]
@@ -54,7 +65,9 @@
     scaled = (x_full * gain[...].astype(F32)).astype(BF16)
     normed[...] = scaled.reshape(total, width)
     for c in range(chunks):
-        for copy in copies[c]:
+        if c == max(0, chunks - 3):
+            small[2].start()
+        for copy in chunk(c):
             copy.wait()
         left = normed[:, c * depth : (c + 1) * depth]
         for weights, start, stop in ((wq, 0, queries), (wkv, queries, queries + keyvals)):
@@ -72,65 +85,84 @@
             staged[place, m * here : (m + 1) * here, :] = sums[first : first + here, :]
     for k in range(gx):
         outs[k][...] = staged[position[0] ^ k]
-
-
-def project(position, tokens, gain, wq, wkv, gx):
+    small[2].wait()
+
+
+def project(position, tokens, gain, wq, wkv, cache, gx):
     batches, rows, width = tokens.shape
     columns = wq.shape[1] + wkv.shape[1] + LANES
     chunks = max(1, width // 256)
     return pl.pallas_call(
         functools.partial(project_kernel, chunks, gx),
-        out_shape=[jax.ShapeDtypeStruct((batches * rows // gx, columns), F32)] * gx,
-        in_specs=[SMEM, VMEM, VMEM, HBM, HBM],
-        out_specs=[VMEM] * gx,
+        out_shape=[jax.ShapeDtypeStruct((batches * rows // gx, columns), F32)] * gx
+        + [pltpu.VMEM(cache.shape, BF16)],
+        in_specs=[SMEM] + [HBM] * 5,
+        out_specs=[VMEM] * (gx + 1),
         scratch_shapes=[
+            pltpu.VMEM(tokens.shape, BF16),
+            pltpu.VMEM(gain.shape, BF16),
             pltpu.VMEM(wq.shape, BF16),
             pltpu.VMEM(wkv.shape, BF16),
             pltpu.VMEM((batches * rows, width), BF16),
             pltpu.VMEM((batches * rows, columns), F32),
             pltpu.VMEM((gx, batches * rows // gx, columns), F32),
+            pltpu.SemaphoreType.DMA((3,)),
             pltpu.SemaphoreType.DMA((2, chunks)),
         ],
-        compiler_params=params(24),
+        compiler_params=params(32),
         name="project",
-    )(position, tokens, gain, wq, wkv)
-
-
-def stage_kernel(sent, cache_hbm, w_hbm, cache, weights, sems):
-    del sent
-    copies = [
-        pltpu.make_async_copy(cache_hbm, cache, sems.at[0]),
-        pltpu.make_async_copy(w_hbm.at[pl.ds(0, weights.shape[0])], weights, sems.at[1]),
-    ]
-    for copy in copies:
-        copy.start()
-    for copy in copies:
-        copy.wait()
-
-
-def stage(sent, cache, w_out, rows):
+    )(position, tokens, gain, wq, wkv, cache)
+
+
+def stage_kernel(first, after, w_hbm, weights, sems):
+    del after
+    pieces = sems.shape[0]
+    depth = weights.shape[0] // pieces
+
+    def piece(c):
+        return pltpu.make_async_copy(
+            w_hbm.at[pl.ds(first + c * depth, depth)],
+            weights.at[pl.ds(c * depth, depth)],
+            sems.at[c],
+        )
+
+    for c in range(pieces):
+        piece(c).start()
+    for c in range(pieces):
+        piece(c).wait()
+
+
+def stage(after, w_out, first, rows):
     return pl.pallas_call(
-        stage_kernel,
-        out_shape=[
-            pltpu.VMEM(cache.shape, BF16),
-            pltpu.VMEM((rows, w_out.shape[1]), BF16),
-        ],
-        in_specs=[ANY, HBM, HBM],
-        out_specs=[VMEM, VMEM],
+        functools.partial(stage_kernel, first),
+        out_shape=pltpu.VMEM((rows, w_out.shape[1]), BF16),
+        in_specs=[ANY, HBM],
+        out_specs=VMEM,
         scratch_shapes=[pltpu.SemaphoreType.DMA((2,))],
         compiler_params=params(1),
         name="stage",
-    )(sent, cache, w_out)
+    )(after, w_out)
 
 
 def attend_kernel(model_width, parts, first, lengths, angles, *refs):
     received = refs[:parts]
-    cache, w_hbm, out, weights_out, table, sem = refs[parts:]
+    cache, staged, w_hbm, out, weights_out, table, sem = refs[parts:]
+    del staged
     rows = cache.shape[0]
-    load = pltpu.make_async_copy(
-        w_hbm.at[pl.ds(first, weights_out.shape[0])], weights_out, sem
-    )
-    load.start()
+    pieces = sem.shape[0]
+    depth = weights_out.shape[0] // pieces
+
+    def load(c):
+        return pltpu.make_async_copy(
+            w_hbm.at[pl.ds(first + c * depth, depth)],
+            weights_out.at[pl.ds(c * depth, depth)],
+            sem.at[c],
+        )
+
+    @pl.loop(0, pieces)
+    def _(c):
+        load(c).start()
+
     half = HEAD_SIZE // 2
     group = out.shape[1] // HEAD_SIZE
     queries = group * HEAD_SIZE
@@ -152,35 +184,54 @@
     rkey = rotate(column(queries))
     value_new = column(queries + HEAD_SIZE)
     inv_root = 1.0 / jnp.sqrt(jnp.float32(HEAD_SIZE))
-    for r in range(rows):
-        query = table[r * group : (r + 1) * group, :].astype(BF16)
-        pairs = cache[r]
+    pair = 2 if rows % 2 == 0 else 1
+    for r in range(0, rows, pair):
+        members = range(r, r + pair)
+        query = table[r * group : (r + pair) * group, :]
+        block = lax.broadcasted_iota(jnp.int32, (pair * group, 1), 0) // group
+        left = jnp.concatenate([jnp.where(block == j, query, 0.0) for j in range(pair)], axis=1)
+        right = jnp.concatenate([cache[n] for n in members], axis=1)
         scores = (
-            lax.dot_general(query, pairs, (((1,), (1,)), ((), ())), preferred_element_type=F32)
+            lax.dot_general(
+                left.astype(BF16), right, (((1,), (1,)), ((), ())), preferred_element_type=F32
+            )
             * inv_root
         )
+        limit = jnp.where(block == 0, lengths[r], lengths[r + pair - 1])
         place = lax.broadcasted_iota(jnp.int32, scores.shape, 1)
-        valid = jnp.logical_and(place < 2 * lengths[r], (place & 1) == 0)
+        valid = jnp.logical_and(place < 2 * limit, (place & 1) == 0)
         scores = jnp.where(valid, scores, -1e30)
+
+        def spread(vectors):
+            return jnp.where(
+                block == 0, vectors[r : r + 1, :], vectors[r + pair - 1 : r + pair, :]
+            )
+
         new_score = (
-            jnp.sum(query.astype(F32) * rkey[r : r + 1, :], axis=-1, keepdims=True) * inv_root
+            jnp.sum(query.astype(BF16).astype(F32) * spread(rkey), axis=-1, keepdims=True)
+            * inv_root
         )
         top = jnp.maximum(jnp.max(scores, axis=-1, keepdims=True), new_score)
         weights = jnp.exp(scores - top)
         new_weight = jnp.exp(new_score - top)
         total = jnp.sum(weights, axis=-1, keepdims=True) + new_weight
         weights = pltpu.roll(weights, 1, 1).astype(BF16)
-        summed = jnp.dot(weights, pairs, preferred_element_type=F32)
-        summed = summed + new_weight * value_new[r : r + 1, :]
-        table[r * group : (r + 1) * group, :] = summed / total
+        both = jnp.dot(weights, right, preferred_element_type=F32)
+        summed = both[:, :HEAD_SIZE]
+        for j in range(1, pair):
+            summed = jnp.where(block == j, both[:, j * HEAD_SIZE : (j + 1) * HEAD_SIZE], summed)
+        summed = summed + new_weight * spread(value_new)
+        table[r * group : (r + pair) * group, :] = summed / total
     for h in range(group):
         out[:, h * HEAD_SIZE : (h + 1) * HEAD_SIZE] = table[
             pl.ds(h, rows, stride=group), :
         ].astype(BF16)
-    load.wait()
-
-
-def attend(model_width, lengths, angles, received, cache, queries, w_out, first, count):
+    for c in range(pieces):
+        load(c).wait()
+
+
+def attend(model_width, lengths, angles, received, cache, queries, staged, w_out, count):
+    first = staged.shape[0]
     rows = cache.shape[0]
     return pl.pallas_call(
         functools.partial(attend_kernel, model_width, len(received), first),
@@ -188,32 +239,35 @@
             jax.ShapeDtypeStruct((rows, queries), BF16),
             pltpu.VMEM((count, w_out.shape[1]), BF16),
         ],
-        in_specs=[SMEM, VMEM] + [VMEM] * len(received) + [VMEM, HBM],
+        in_specs=[SMEM, VMEM] + [VMEM] * len(received) + [VMEM, ANY, HBM],
         out_specs=[VMEM, VMEM],
         scratch_shapes=[
             pltpu.VMEM((rows * queries // HEAD_SIZE, HEAD_SIZE), F32),
-            pltpu.SemaphoreType.DMA,
+            pltpu.SemaphoreType.DMA((4,)),
         ],
         compiler_params=params(4),
         name="attend",
-    )(lengths, angles, *received, cache, w_out)
+    )(lengths, angles, *received, cache, staged, w_out)
 
 
 def output_kernel(chunks, gx, batches, position, *refs):
     received = refs[:gx]
-    begun, middle, w_hbm, out, weights, blocks, left, sems = refs[gx:]
-    first = begun.shape[0] + middle.shape[0]
+    staged = refs[gx:-6]
+    w_hbm, out, weights, blocks, left, sems = refs[-6:]
+    first = sum(ref.shape[0] for ref in staged)
     depth = weights.shape[0] // chunks
-    copies = []
-    for c in range(chunks):
-        copies.append(
-            pltpu.make_async_copy(
-                w_hbm.at[pl.ds(first + c * depth, depth)],
-                weights.at[pl.ds(c * depth, depth)],
-                sems.at[c],
-            )
-        )
-        copies[-1].start()
+
+    def load(c):
+        return pltpu.make_async_copy(
+            w_hbm.at[pl.ds(first + c * depth, depth)],
+            weights.at[pl.ds(c * depth, depth)],
+            sems.at[c],
+        )
+
+    @pl.loop(0, chunks)
+    def _(c):
+        load(c).start()
+
     here = received[0].shape[0] // batches
     rows = here * gx
     for k in range(gx):
@@ -228,24 +282,30 @@
             left[:, start : start + stop].astype(BF16), ref, preferred_element_type=F32
         )
 
-    out[...] = product(0, begun[...], begun.shape[0])
-    out[...] += product(begun.shape[0], middle[...], middle.shape[0])
+    start = 0
+    for ref in staged:
+        part = product(start, ref[...], ref.shape[0])
+        if start == 0:
+            out[...] = part
+        else:
+            out[...] += part
+        start += ref.shape[0]
     for c in range(chunks):
-        copies[c].wait()
+        load(c).wait()
         out[...] += product(
             first + c * depth, weights[c * depth : (c + 1) * depth, :], depth
         )
 
 
-def output(position, received, begun, middle, w_out, batches):
+def output(position, received, staged, w_out, batches):
     gx = len(received)
     rows = received[0].shape[0] * gx
-    rest = w_out.shape[0] - begun.shape[0] - middle.shape[0]
+    rest = w_out.shape[0] - sum(ref.shape[0] for ref in staged)
     chunks = max(1, rest // 256)
     return pl.pallas_call(
         functools.partial(output_kernel, chunks, gx, batches),
         out_shape=jax.ShapeDtypeStruct((rows, w_out.shape[1]), F32),
-        in_specs=[SMEM] + [VMEM] * (gx + 2) + [HBM],
+        in_specs=[SMEM] + [VMEM] * (gx + len(staged)) + [HBM],
         out_specs=VMEM,
         scratch_shapes=[
             pltpu.VMEM((rest, w_out.shape[1]), BF16),
@@ -253,9 +313,9 @@
             pltpu.VMEM((rows, w_out.shape[0]), F32),
             pltpu.SemaphoreType.DMA((chunks,)),
         ],
-        compiler_params=params(8),
+        compiler_params=params(24),
         name="output",
-    )(position, *received, begun, middle, w_out)
+    )(position, *received, *staged, w_out)
 
 
 def rotation(lengths):
@@ -288,18 +348,19 @@
     w_out = in_hbm(w_out)
     pairs = in_hbm(cache.reshape(-1, 2 * cache.shape[2], HEAD_SIZE))
     position = lax.axis_index("gx").reshape(1)
-    sent = project(position, tokens, norm_gain.reshape(1, -1), w_query, wkv, gx)
+    *sent, pairs = project(position, in_hbm(tokens), in_hbm(norm_gain), w_query, wkv, pairs, gx)
     received = [sent[0]] + [exchange(sent[k], "gx", gx, k) for k in reversed(range(1, gx))]
     angles = rotation(lengths)
-    depth = w_out.shape[0]
-    pairs, begun = stage(sent[0], pairs, w_out, depth // 4)
+    depth = w_out.shape[0] // 16
+    begun = stage(sent[0], w_out, 0, 4 * depth)
     attended, middle = attend(
-        width * gx, lengths.reshape(-1), angles, received, pairs, queries, w_out, depth // 4, depth // 2
-    )
+        width * gx, lengths.reshape(-1), angles, received, pairs, queries, begun, w_out, 4 * depth
+    )
+    last = stage(attended, w_out, 8 * depth, 6 * depth)
     gathered = {k: exchange(attended, "gx", gx, k) for k in reversed(range(1, gx))}
     gathered[0] = attended
     projected = output(
-        position, [gathered[k] for k in range(gx)], begun, middle, w_out, batches
+        position, [gathered[k] for k in range(gx)], [begun, middle, last], w_out, batches
     )
     summed = add_heads(projected, "gy", gy).reshape(tokens.shape)
     return (tokens.astype(F32) + summed).astype(BF16)

time: 43.2 us -> 38.2 us (0.88)
  waiting for transfers between devices: 9.59 us -> 7.25 us
  local copies, waits for them, and re-layouts: 1.69 us -> 0.09 us
  Pallas kernels: 18.8 us -> 17.8 us
    pallas_call x1, Pallas kernels: 5.87 us -> 2.76 us  [attend(): pl.pallas_call(functools.partial(attend_kernel, model_width, len(received...]
    ppermute x8, waiting for transfers between devices: 9.59 us -> 7.25 us  [exchange(): return lax.ppermute(value, axis, [(i, i ^ step) for i in range(size)])]
    pallas_call x1 -> x2, Pallas kernels: 2.85 us -> 5.11 us  [stage(): pl.pallas_call(functools.partial(stage_kernel, first), out_shape=pltpu.VM...]
    unnamed x6 -> x4, local copies, waits for them, and re-layouts: 0.91 us -> 0.01 us
    pallas_call x1, Pallas kernels: 3.16 us -> 2.31 us  [output(): pl.pallas_call(functools.partial(output_kernel, chunks, gx, batches), out...]
    pallas_call x1, Pallas kernels: 6.96 us -> 7.68 us  [project(): pl.pallas_call(functools.partial(project_kernel, chunks, gx), out_shape=[...]
    reshape x1 -> x0, local copies, waits for them, and re-layouts: 0.71 us -> none  [local(): sent = project(position, tokens, norm_gain.reshape(1, -1), w_query, wkv, gx)]
  transfers between devices with their start and end apart: 8 -> 8, of which waited for: 5 -> 3; matrix products, arithmetic and copies ran while one was open for 1% -> 1% of each run, Pallas kernels for 7% -> 13%
where the time goes in v2:
time: 38.2 us; the launch traced here: 38.1 us
  Pallas kernels  17.8 us (47%)
  starting transfers between devices  11.9 us (31%)
  waiting for transfers between devices  7.25 us (19%)
  other arithmetic  0.94 us (2%)
    ppermute x8, starting transfers between devices, exchange(): return lax.ppermute(value, axis, [(i, i ^ step) for i in range(size)])  11.9 us
    pallas_call x1, Pallas kernels, project(): pl.pallas_call(functools.partial(project_kernel, chunks, gx), out_shape=[...  7.68 us
    ppermute x8, waiting for transfers between devices, exchange(): return lax.ppermute(value, axis, [(i, i ^ step) for i in range(size)])  7.25 us
    pallas_call x2, Pallas kernels, stage(): pl.pallas_call(functools.partial(stage_kernel, first), out_shape=pltpu.VM...  5.11 us
    pallas_call x1, Pallas kernels, attend(): pl.pallas_call(functools.partial(attend_kernel, model_width, len(received...  2.76 us
    pallas_call x1, Pallas kernels, output(): pl.pallas_call(functools.partial(output_kernel, chunks, gx, batches), out...  2.31 us
  transfers between devices with their start and end apart: 8, of which 3 were waited for; matrix products, arithmetic and copies ran while one was open for 1% of the time, Pallas kernels for 13%

profile of v2, /device:TPU:0, one launch (start us, length us, event | category | flops | bytes accessed | tf_op | source)
XLA Modules:
  0.0 38.1 jit_solution(658492698640017261)
XLA Ops:
  0.0 0.0 copy-start.1
  0.0 7.7 %project.1 = (f32[4,2432]{1,0:T(4,128)S(1)}, f32[4,2432]{1,0:T(4,128)S(1)}, f32[4,2432]{1,0:T(4,128)S(1)}, f32[4,2432]{1,0:T(4,128)S(1)}, bf16[4,2048,128]{2,1,0:T(8,128)(2,1)S(1)}) custom-call(s32[1]{0:T(128)} %bitcast.position, bf16[2,8,4096]{2,1,0:T(8,128)(2,1)} %tokens_hbm.1, bf16[4096]{0:T(1024)(128)(2,1)} %gain_hbm.1, bf16[4096,2048]{1,0:T(8,128)(2,1)} %wq_hbm.1, ...), custom_call_target="tpu_custom_call" | custom-call | tf_op jit(solution)/shard_map/project/pallas_call | solution.py:95
  7.7 5.1 %collective-permute-start = (f32[4,2432]{1,0:T(4,128)S(1)}, f32[4,2432]{1,0:T(4,128)S(1)}, u32[]{:S(2)}, u32[]{:S(2)}) collective-permute-start(f32[4,2432]{1,0:T(4,128)S(1)} %get-tuple-element.13), channel_id=1, source_target_pairs={{0,12},{4,8},{8,4},{12,0},{1,13},{5,9},{9,5},{13,1},{2,14},{6,10},... | collective-permute-start | bytes 116744 | tf_op jit(solution)/shard_map/ppermute | solution.py:21
  12.8 0.0 collective-permute-start.1
  12.8 0.6 %collective-permute-start.2 = (f32[4,2432]{1,0:T(4,128)S(1)}, f32[4,2432]{1,0:T(4,128)S(1)}, u32[]{:S(2)}, u32[]{:S(2)}) collective-permute-start(f32[4,2432]{1,0:T(4,128)S(1)} %get-tuple-element.15), channel_id=1, source_target_pairs={{0,4},{4,0},{8,12},{12,8},{1,5},{5,1},{9,13},{13,9},{2,6},{6,2},{1... | collective-permute-start | bytes 116744 | tf_op jit(solution)/shard_map/ppermute | solution.py:21
  13.5 0.0 copy-done.1
  13.5 0.1 reshape.29.lengths
  13.6 0.1 multiply_cosine_fusion
  13.7 0.1 maximum_bitcast_fusion
  13.8 2.2 %stage.2.refs_5_.refs_4_ = bf16[512,4096]{1,0:T(8,128)(2,1)S(1)} custom-call(f32[4,2432]{1,0:T(4,128)S(1)} %get-tuple-element.12.after.refs_0_, bf16[2048,4096]{1,0:T(8,128)(2,1)} %refs_7_.1), custom_call_target="tpu_custom_call" | custom-call | tf_op jit(solution)/shard_map/stage/pallas_call | solution.py:136
  16.0 0.0 collective-permute-done.refs_1_
  16.0 1.7 %collective-permute-done.1.refs_2_ = f32[4,2432]{1,0:T(4,128)S(1)} collective-permute-done((f32[4,2432]{1,0:T(4,128)S(1)}, f32[4,2432]{1,0:T(4,128)S(1)}, u32[]{:S(2)}, u32[]{:S(2)}) %collective-permute-start.1) | collective-permute-done | bytes 38944 | tf_op jit(solution)/shard_map/ppermute | solution.py:21
  17.7 0.0 collective-permute-done.2.refs_3_
  17.7 2.8 %attend.1 = (bf16[4,2048]{1,0:T(4,128)(2,1)S(1)}, bf16[512,4096]{1,0:T(8,128)(2,1)S(1)}) custom-call(s32[4]{0:T(128)S(1)} %reshape.29.lengths, f32[2,4,128]{2,1,0:T(4,128)S(1)} %pad_maximum_fusion.angles, f32[4,2432]{1,0:T(4,128)S(1)} %get-tuple-element.12.after.refs_0_, f32[4,2432]{1,0:T(4,128)S(1)} %collective-permute-done.refs_1_, ...), custom_call_target="tpu_custom_call" | custom-call | tf_op jit(solution)/shard_map/attend/pallas_call | solution.py:236
  20.5 2.2 %collective-permute-start.5 = (bf16[4,2048]{1,0:T(4,128)(2,1)S(1)}, bf16[4,2048]{1,0:T(4,128)(2,1)S(1)}, u32[]{:S(2)}, u32[]{:S(2)}) collective-permute-start(bf16[4,2048]{1,0:T(4,128)(2,1)S(1)} %get-tuple-element.17.after.refs_0_), channel_id=1, source_target_pairs={{0,12},{4,8},{8,4},{12,0},{1,13},{5,9},{9,5},{13,1},{2,14},{6,10},... | collective-permute-start | bytes 49160 | tf_op jit(solution)/shard_map/ppermute | solution.py:21
  22.6 0.0 collective-permute-start.4
  22.6 2.3 %collective-permute-start.3 = (bf16[4,2048]{1,0:T(4,128)(2,1)S(1)}, bf16[4,2048]{1,0:T(4,128)(2,1)S(1)}, u32[]{:S(2)}, u32[]{:S(2)}) collective-permute-start(bf16[4,2048]{1,0:T(4,128)(2,1)S(1)} %get-tuple-element.17.after.refs_0_), channel_id=1, source_target_pairs={{0,4},{4,0},{8,12},{12,8},{1,5},{5,1},{9,13},{13,9},{2,6},{6,2},{1... | collective-permute-start | bytes 49160 | tf_op jit(solution)/shard_map/ppermute | solution.py:21
  24.9 2.9 %stage.3.refs_6_ = bf16[768,4096]{1,0:T(8,128)(2,1)S(1)} custom-call(bf16[4,2048]{1,0:T(4,128)(2,1)S(1)} %get-tuple-element.17.after.refs_0_, bf16[2048,4096]{1,0:T(8,128)(2,1)} %refs_7_.1), custom_call_target="tpu_custom_call" | custom-call | tf_op jit(solution)/shard_map/stage/pallas_call | solution.py:136
  27.8 0.0 collective-permute-done.5.refs_3_
  27.8 0.0 collective-permute-done.4.refs_2_
  27.8 0.0 collective-permute-done.3.refs_1_
  27.8 0.0 copy-start
  27.8 2.3 %output.1 = f32[16,4096]{1,0:T(8,128)S(1)} custom-call(s32[1]{0:T(128)} %bitcast.position, bf16[4,2048]{1,0:T(4,128)(2,1)S(1)} %get-tuple-element.17.after.refs_0_, bf16[4,2048]{1,0:T(4,128)(2,1)S(1)} %collective-permute-done.3.refs_1_, bf16[4,2048]{1,0:T(4,128)(2,1)S(1)} %collective-permute-done.4.refs_2_, ...), custom_call_target="tpu_custom_call" | custom-call | tf_op jit(solution)/shard_map/output/pallas_call | solution.py:305
  30.2 0.1 collective-permute-start.6
  30.2 1.5 %collective-permute-done.6 = f32[16,4096]{1,0:T(8,128)S(1)} collective-permute-done((f32[16,4096]{1,0:T(8,128)S(1)}, f32[16,4096]{1,0:T(8,128)S(1)}, u32[]{:S(2)}, u32[]{:S(2)}) %collective-permute-start.6) | collective-permute-done | bytes 262176 | tf_op jit(solution)/shard_map/ppermute | solution.py:21
  31.8 1.6 %collective-permute-start.7 = (bf16[16,4096]{1,0:T(8,128)(2,1)S(1)}, bf16[16,4096]{1,0:T(8,128)(2,1)S(1)}, u32[]{:S(2)}, u32[]{:S(2)}) collective-permute-start(bf16[16,4096]{1,0:T(8,128)(2,1)S(1)} %add_convert_fusion), channel_id=1, source_target_pairs={{0,2},{1,3},{2,0},{3,1},{4,6},{5,7},{6,4},{7,5},{8,10},{9,11},{10,... | collective-permute-start | bytes 393224 | tf_op jit(solution)/shard_map/ppermute | solution.py:21
  33.3 4.0 %collective-permute-done.7 = bf16[16,4096]{1,0:T(8,128)(2,1)S(1)} collective-permute-done((bf16[16,4096]{1,0:T(8,128)(2,1)S(1)}, bf16[16,4096]{1,0:T(8,128)(2,1)S(1)}, u32[]{:S(2)}, u32[]{:S(2)}) %collective-permute-start.7) | collective-permute-done | bytes 131104 | tf_op jit(solution)/shard_map/ppermute | solution.py:21
  37.4 0.0 copy-done
  37.4 0.7 %fusion = bf16[2,8,4096]{2,1,0:T(8,128)(2,1)} fusion(bf16[16,4096]{1,0:T(8,128)(2,1)S(1)} %collective-permute-done.7, bf16[16,4096]{1,0:T(8,128)(2,1)S(1)} %add_convert_fusion, bf16[2,8,4096]{2,1,0:T(8,128)(2,1)S(1)} %copy-done), kind=kLoop, calls=%fused_computation.1 | loop fusion | flops 393216 | bytes 524288 | tf_op jit(solution)/shard_map/convert_element_type | solution.py:366
  (4 shorter events, 0.0 us)
Async XLA Ops:
  0.0 13.5 %copy-start.1 = (s32[2,2]{1,0:T(2,128)S(1)}, s32[2,2]{1,0:T(2,128)}, u32[]{:S(2)}) copy-start(s32[2,2]{1,0:T(2,128)} %param.8) | copy-start | bytes 52
  7.7 8.3 %collective-permute-start = (f32[4,2432]{1,0:T(4,128)S(1)}, f32[4,2432]{1,0:T(4,128)S(1)}, u32[]{:S(2)}, u32[]{:S(2)}) collective-permute-start(f32[4,2432]{1,0:T(4,128)S(1)} %get-tuple-element.13), channel_id=1, source_target_pairs={{0,12},{4,8},{8,4},{12,0},{1,13},{5,9},{9,5},{13,1},{2,14},{6,10},... | collective-permute-start | bytes 116744 | tf_op jit(solution)/shard_map/ppermute | solution.py:21
  12.8 4.9 %collective-permute-start.1 = (f32[4,2432]{1,0:T(4,128)S(1)}, f32[4,2432]{1,0:T(4,128)S(1)}, u32[]{:S(2)}, u32[]{:S(2)}) collective-permute-start(f32[4,2432]{1,0:T(4,128)S(1)} %get-tuple-element.14), channel_id=1, source_target_pairs={{0,8},{4,12},{8,0},{12,4},{1,9},{5,13},{9,1},{13,5},{2,10},{6,14},... | collective-permute-start | bytes 116744 | tf_op jit(solution)/shard_map/ppermute | solution.py:21
  12.8 4.9 %collective-permute-start.2 = (f32[4,2432]{1,0:T(4,128)S(1)}, f32[4,2432]{1,0:T(4,128)S(1)}, u32[]{:S(2)}, u32[]{:S(2)}) collective-permute-start(f32[4,2432]{1,0:T(4,128)S(1)} %get-tuple-element.15), channel_id=1, source_target_pairs={{0,4},{4,0},{8,12},{12,8},{1,5},{5,1},{9,13},{13,9},{2,6},{6,2},{1... | collective-permute-start | bytes 116744 | tf_op jit(solution)/shard_map/ppermute | solution.py:21
  20.5 7.3 %collective-permute-start.5 = (bf16[4,2048]{1,0:T(4,128)(2,1)S(1)}, bf16[4,2048]{1,0:T(4,128)(2,1)S(1)}, u32[]{:S(2)}, u32[]{:S(2)}) collective-permute-start(bf16[4,2048]{1,0:T(4,128)(2,1)S(1)} %get-tuple-element.17.after.refs_0_), channel_id=1, source_target_pairs={{0,12},{4,8},{8,4},{12,0},{1,13},{5,9},{9,5},{13,1},{2,14},{6,10},... | collective-permute-start | bytes 49160 | tf_op jit(solution)/shard_map/ppermute | solution.py:21
  22.6 5.2 %collective-permute-start.4 = (bf16[4,2048]{1,0:T(4,128)(2,1)S(1)}, bf16[4,2048]{1,0:T(4,128)(2,1)S(1)}, u32[]{:S(2)}, u32[]{:S(2)}) collective-permute-start(bf16[4,2048]{1,0:T(4,128)(2,1)S(1)} %get-tuple-element.17.after.refs_0_), channel_id=1, source_target_pairs={{0,8},{4,12},{8,0},{12,4},{1,9},{5,13},{9,1},{13,5},{2,10},{6,14},... | collective-permute-start | bytes 49160 | tf_op jit(solution)/shard_map/ppermute | solution.py:21
  22.6 5.2 %collective-permute-start.3 = (bf16[4,2048]{1,0:T(4,128)(2,1)S(1)}, bf16[4,2048]{1,0:T(4,128)(2,1)S(1)}, u32[]{:S(2)}, u32[]{:S(2)}) collective-permute-start(bf16[4,2048]{1,0:T(4,128)(2,1)S(1)} %get-tuple-element.17.after.refs_0_), channel_id=1, source_target_pairs={{0,4},{4,0},{8,12},{12,8},{1,5},{5,1},{9,13},{13,9},{2,6},{6,2},{1... | collective-permute-start | bytes 49160 | tf_op jit(solution)/shard_map/ppermute | solution.py:21
  27.8 9.6 %copy-start = (bf16[2,8,4096]{2,1,0:T(8,128)(2,1)S(1)}, bf16[2,8,4096]{2,1,0:T(8,128)(2,1)}, u32[]{:S(2)}) copy-start(bf16[2,8,4096]{2,1,0:T(8,128)(2,1)} %tokens_hbm.1) | copy-start | bytes 393220
  30.2 1.6 %collective-permute-start.6 = (f32[16,4096]{1,0:T(8,128)S(1)}, f32[16,4096]{1,0:T(8,128)S(1)}, u32[]{:S(2)}, u32[]{:S(2)}) collective-permute-start(f32[16,4096]{1,0:T(8,128)S(1)} %output.1), channel_id=1, source_target_pairs={{0,1},{1,0},{2,3},{3,2},{4,5},{5,4},{6,7},{7,6},{8,9},{9,8},{10,11... | collective-permute-start | bytes 786440 | tf_op jit(solution)/shard_map/ppermute | solution.py:21
  31.8 5.6 %collective-permute-start.7 = (bf16[16,4096]{1,0:T(8,128)(2,1)S(1)}, bf16[16,4096]{1,0:T(8,128)(2,1)S(1)}, u32[]{:S(2)}, u32[]{:S(2)}) collective-permute-start(bf16[16,4096]{1,0:T(8,128)(2,1)S(1)} %add_convert_fusion), channel_id=1, source_target_pairs={{0,2},{1,3},{2,0},{3,1},{4,6},{5,7},{6,4},{7,5},{8,10},{9,11},{10,... | collective-permute-start | bytes 393224 | tf_op jit(solution)/shard_map/ppermute | solution.py:21

commit v3 on v2

--- a/solution.py
+++ b/solution.py
@@ -29,14 +29,13 @@
     return pltpu.CompilerParams(vmem_limit_bytes=mib * 2**20)
 
 
-def project_kernel(chunks, gx, position, tokens_hbm, gain_hbm, wq_hbm, wkv_hbm, cache_hbm, *refs):
+def project_kernel(chunks, gx, position, tokens_hbm, gain_hbm, wq_hbm, wkv_hbm, *refs):
     outs = refs[:gx]
-    cache, tokens, gain, wq, wkv, normed, sums, staged, small_sems, sems = refs[gx:]
+    tokens, gain, wq, wkv, normed, sums, staged, small_sems, sems = refs[gx:]
     depth = wq.shape[0] // chunks
     small = [
         pltpu.make_async_copy(tokens_hbm, tokens, small_sems.at[0]),
         pltpu.make_async_copy(gain_hbm, gain, small_sems.at[1]),
-        pltpu.make_async_copy(cache_hbm, cache, small_sems.at[2]),
     ]
     small[0].start()
     small[1].start()
@@ -65,8 +64,6 @@
     scaled = (x_full * gain[...].astype(F32)).astype(BF16)
     normed[...] = scaled.reshape(total, width)
     for c in range(chunks):
-        if c == max(0, chunks - 3):
-            small[2].start()
         for copy in chunk(c):
             copy.wait()
         left = normed[:, c * depth : (c + 1) * depth]
@@ -85,19 +82,17 @@
             staged[place, m * here : (m + 1) * here, :] = sums[first : first + here, :]
     for k in range(gx):
         outs[k][...] = staged[position[0] ^ k]
-    small[2].wait()
-
-
-def project(position, tokens, gain, wq, wkv, cache, gx):
+
+
+def project(position, tokens, gain, wq, wkv, gx):
     batches, rows, width = tokens.shape
     columns = wq.shape[1] + wkv.shape[1] + LANES
     chunks = max(1, width // 256)
     return pl.pallas_call(
         functools.partial(project_kernel, chunks, gx),
-        out_shape=[jax.ShapeDtypeStruct((batches * rows // gx, columns), F32)] * gx
-        + [pltpu.VMEM(cache.shape, BF16)],
-        in_specs=[SMEM] + [HBM] * 5,
-        out_specs=[VMEM] * (gx + 1),
+        out_shape=[jax.ShapeDtypeStruct((batches * rows // gx, columns), F32)] * gx,
+        in_specs=[SMEM] + [HBM] * 4,
+        out_specs=[VMEM] * gx,
         scratch_shapes=[
             pltpu.VMEM(tokens.shape, BF16),
             pltpu.VMEM(gain.shape, BF16),
@@ -106,63 +101,39 @@
             pltpu.VMEM((batches * rows, width), BF16),
             pltpu.VMEM((batches * rows, columns), F32),
             pltpu.VMEM((gx, batches * rows // gx, columns), F32),
-            pltpu.SemaphoreType.DMA((3,)),
+            pltpu.SemaphoreType.DMA((2,)),
             pltpu.SemaphoreType.DMA((2, chunks)),
         ],
         compiler_params=params(32),
         name="project",
-    )(position, tokens, gain, wq, wkv, cache)
-
-
-def stage_kernel(first, after, w_hbm, weights, sems):
+    )(position, tokens, gain, wq, wkv)
+
+
+def stage_kernel(after, cache_hbm, cache, sems):
     del after
-    pieces = sems.shape[0]
-    depth = weights.shape[0] // pieces
-
-    def piece(c):
-        return pltpu.make_async_copy(
-            w_hbm.at[pl.ds(first + c * depth, depth)],
-            weights.at[pl.ds(c * depth, depth)],
-            sems.at[c],
-        )
-
-    for c in range(pieces):
-        piece(c).start()
-    for c in range(pieces):
-        piece(c).wait()
-
-
-def stage(after, w_out, first, rows):
+    rows = cache.shape[0]
+    for r in range(rows):
+        pltpu.make_async_copy(cache_hbm.at[r], cache.at[r], sems.at[r]).start()
+    for r in range(rows):
+        pltpu.make_async_copy(cache_hbm.at[r], cache.at[r], sems.at[r]).wait()
+
+
+def stage(after, cache):
     return pl.pallas_call(
-        functools.partial(stage_kernel, first),
-        out_shape=pltpu.VMEM((rows, w_out.shape[1]), BF16),
+        stage_kernel,
+        out_shape=pltpu.VMEM(cache.shape, BF16),
         in_specs=[ANY, HBM],
         out_specs=VMEM,
-        scratch_shapes=[pltpu.SemaphoreType.DMA((2,))],
+        scratch_shapes=[pltpu.SemaphoreType.DMA((cache.shape[0],))],
         compiler_params=params(1),
         name="stage",
-    )(after, w_out)
-
-
-def attend_kernel(model_width, parts, first, lengths, angles, *refs):
+    )(after, cache)
+
+
+def attend_kernel(model_width, parts, lengths, angles, *refs):
     received = refs[:parts]
-    cache, staged, w_hbm, out, weights_out, table, sem = refs[parts:]
-    del staged
+    cache, out, table = refs[parts:]
     rows = cache.shape[0]
-    pieces = sem.shape[0]
-    depth = weights_out.shape[0] // pieces
-
-    def load(c):
-        return pltpu.make_async_copy(
-            w_hbm.at[pl.ds(first + c * depth, depth)],
-            weights_out.at[pl.ds(c * depth, depth)],
-            sem.at[c],
-        )
-
-    @pl.loop(0, pieces)
-    def _(c):
-        load(c).start()
-
     half = HEAD_SIZE // 2
     group = out.shape[1] // HEAD_SIZE
     queries = group * HEAD_SIZE
@@ -226,48 +197,27 @@
         out[:, h * HEAD_SIZE : (h + 1) * HEAD_SIZE] = table[
             pl.ds(h, rows, stride=group), :
         ].astype(BF16)
-    for c in range(pieces):
-        load(c).wait()
-
-
-def attend(model_width, lengths, angles, received, cache, queries, staged, w_out, count):
-    first = staged.shape[0]
+
+
+def attend(model_width, lengths, angles, received, cache, queries):
     rows = cache.shape[0]
     return pl.pallas_call(
-        functools.partial(attend_kernel, model_width, len(received), first),
-        out_shape=[
-            jax.ShapeDtypeStruct((rows, queries), BF16),
-            pltpu.VMEM((count, w_out.shape[1]), BF16),
-        ],
-        in_specs=[SMEM, VMEM] + [VMEM] * len(received) + [VMEM, ANY, HBM],
-        out_specs=[VMEM, VMEM],
+        functools.partial(attend_kernel, model_width, len(received)),
+        out_shape=jax.ShapeDtypeStruct((rows, queries), BF16),
+        in_specs=[SMEM, VMEM] + [VMEM] * len(received) + [VMEM],
+        out_specs=VMEM,
         scratch_shapes=[
             pltpu.VMEM((rows * queries // HEAD_SIZE, HEAD_SIZE), F32),
-            pltpu.SemaphoreType.DMA((4,)),
         ],
         compiler_params=params(4),
+        cost_estimate=pl.CostEstimate(flops=10000000000, bytes_accessed=0, transcendentals=0),
         name="attend",
-    )(lengths, angles, *received, cache, staged, w_out)
-
-
-def output_kernel(chunks, gx, batches, position, *refs):
+    )(lengths, angles, *received, cache)
+
+
+def output_kernel(gx, batches, position, *refs):
     received = refs[:gx]
-    staged = refs[gx:-6]
-    w_hbm, out, weights, blocks, left, sems = refs[-6:]
-    first = sum(ref.shape[0] for ref in staged)
-    depth = weights.shape[0] // chunks
-
-    def load(c):
-        return pltpu.make_async_copy(
-            w_hbm.at[pl.ds(first + c * depth, depth)],
-            weights.at[pl.ds(c * depth, depth)],
-            sems.at[c],
-        )
-
-    @pl.loop(0, chunks)
-    def _(c):
-        load(c).start()
-
+    weights, out, blocks, left = refs[gx:]
     here = received[0].shape[0] // batches
     rows = here * gx
     for k in range(gx):
@@ -276,46 +226,24 @@
         for m in range(batches):
             start = m * rows + place * here
             left[start : start + here, :] = blocks[place, m * here : (m + 1) * here, :]
-
-    def product(start, ref, stop):
-        return jnp.dot(
-            left[:, start : start + stop].astype(BF16), ref, preferred_element_type=F32
-        )
-
-    start = 0
-    for ref in staged:
-        part = product(start, ref[...], ref.shape[0])
-        if start == 0:
-            out[...] = part
-        else:
-            out[...] += part
-        start += ref.shape[0]
-    for c in range(chunks):
-        load(c).wait()
-        out[...] += product(
-            first + c * depth, weights[c * depth : (c + 1) * depth, :], depth
-        )
-
-
-def output(position, received, staged, w_out, batches):
+    out[...] = jnp.dot(left[...].astype(BF16), weights[...], preferred_element_type=F32)
+
+
+def output(position, received, w_out, batches):
     gx = len(received)
     rows = received[0].shape[0] * gx
-    rest = w_out.shape[0] - sum(ref.shape[0] for ref in staged)
-    chunks = max(1, rest // 256)
     return pl.pallas_call(
-        functools.partial(output_kernel, chunks, gx, batches),
+        functools.partial(output_kernel, gx, batches),
         out_shape=jax.ShapeDtypeStruct((rows, w_out.shape[1]), F32),
-        in_specs=[SMEM] + [VMEM] * (gx + len(staged)) + [HBM],
+        in_specs=[SMEM] + [VMEM] * (gx + 1),
         out_specs=VMEM,
         scratch_shapes=[
-            pltpu.VMEM((rest, w_out.shape[1]), BF16),
             pltpu.VMEM((gx, rows // gx, w_out.shape[0]), F32),
             pltpu.VMEM((rows, w_out.shape[0]), F32),
-            pltpu.SemaphoreType.DMA((chunks,)),
         ],
-        compiler_params=params(24),
+        compiler_params=params(4),
         name="output",
-    )(position, *received, *staged, w_out)
+    )(position, *received, w_out)
 
 
 def rotation(lengths):
@@ -345,23 +273,18 @@
     queries = w_query.shape[1]
     wkv = in_hbm(key_value_weight.reshape(width, -1))
     w_query = in_hbm(w_query)
-    w_out = in_hbm(w_out)
     pairs = in_hbm(cache.reshape(-1, 2 * cache.shape[2], HEAD_SIZE))
     position = lax.axis_index("gx").reshape(1)
-    *sent, pairs = project(position, in_hbm(tokens), in_hbm(norm_gain), w_query, wkv, pairs, gx)
+    sent = project(position, in_hbm(tokens), in_hbm(norm_gain), w_query, wkv, gx)
+    pairs = stage(sent[0], pairs)
     received = [sent[0]] + [exchange(sent[k], "gx", gx, k) for k in reversed(range(1, gx))]
     angles = rotation(lengths)
-    depth = w_out.shape[0] // 16
-    begun = stage(sent[0], w_out, 0, 4 * depth)
-    attended, middle = attend(
-        width * gx, lengths.reshape(-1), angles, received, pairs, queries, begun, w_out, 4 * depth
-    )
-    last = stage(attended, w_out, 8 * depth, 6 * depth)
+    attended = attend(
+        width * gx, lengths.reshape(-1), angles, received, pairs, queries
+    )
     gathered = {k: exchange(attended, "gx", gx, k) for k in reversed(range(1, gx))}
     gathered[0] = attended
-    projected = output(
-        position, [gathered[k] for k in range(gx)], [begun, middle, last], w_out, batches
-    )
+    projected = output(position, [gathered[k] for k in range(gx)], w_out, batches)
     summed = add_heads(projected, "gy", gy).reshape(tokens.shape)
     return (tokens.astype(F32) + summed).astype(BF16)
 

time: 38.2 us -> 36 us (0.942)
  Pallas kernels: 17.8 us -> 13.2 us
  waiting for transfers between devices: 7.25 us -> 9.65 us
    pallas_call x3 -> x2, Pallas kernels: 7.41 us -> 4 us  [the longest x1 2.29 us: output(): pl.pallas_call(functools.partial(output_kernel, gx, batches), out_shape=j...]
    ppermute x8, waiting for transfers between devices: 7.25 us -> 9.65 us  [exchange(): return lax.ppermute(value, axis, [(i, i ^ step) for i in range(size)])]
    pallas_call x1, Pallas kernels: 2.76 us -> 2.13 us  [attend(): pl.pallas_call(functools.partial(attend_kernel, model_width, len(received...]
    pallas_call x1, Pallas kernels: 7.68 us -> 7.06 us  [project(): pl.pallas_call(functools.partial(project_kernel, chunks, gx), out_shape=[...]
  transfers between devices with their start and end apart: 8 -> 8, of which waited for: 3 -> 5; matrix products, arithmetic and copies ran while one was open for 1% -> 1% of each run, Pallas kernels for 13% -> 5%
where the time goes in v3:
time: 36 us; the launch traced here: 35.8 us
  Pallas kernels  13.2 us (37%)
  starting transfers between devices  11.8 us (33%)
  waiting for transfers between devices  9.65 us (27%)
  other arithmetic  0.94 us (3%)
    ppermute x8, starting transfers between devices, exchange(): return lax.ppermute(value, axis, [(i, i ^ step) for i in range(size)])  11.8 us
    ppermute x8, waiting for transfers between devices, exchange(): return lax.ppermute(value, axis, [(i, i ^ step) for i in range(size)])  9.65 us
    pallas_call x1, Pallas kernels, project(): pl.pallas_call(functools.partial(project_kernel, chunks, gx), out_shape=[...  7.06 us
    pallas_call x1, Pallas kernels, output(): pl.pallas_call(functools.partial(output_kernel, gx, batches), out_shape=j...  2.29 us
    pallas_call x1, Pallas kernels, attend(): pl.pallas_call(functools.partial(attend_kernel, model_width, len(received...  2.13 us
    pallas_call x1, Pallas kernels, stage(): pl.pallas_call(stage_kernel, out_shape=pltpu.VMEM(cache.shape, BF16), in_...  1.71 us
  transfers between devices with their start and end apart: 8, of which 5 were waited for; matrix products, arithmetic and copies ran while one was open for 1% of the time, Pallas kernels for 5%

profile of v3, /device:TPU:0, one launch (start us, length us, event | category | flops | bytes accessed | tf_op | source)
XLA Modules:
  0.0 35.8 jit_solution(13412400665465167320)
XLA Ops:
  0.0 7.1 %project.1 = (f32[4,2432]{1,0:T(4,128)S(1)}, f32[4,2432]{1,0:T(4,128)S(1)}, f32[4,2432]{1,0:T(4,128)S(1)}, f32[4,2432]{1,0:T(4,128)S(1)}) custom-call(s32[1]{0:T(128)} %bitcast.position, bf16[2,8,4096]{2,1,0:T(8,128)(2,1)} %tokens_hbm.1, bf16[4096]{0:T(1024)(128)(2,1)} %gain_hbm.1, bf16[4096,2048]{1,0:T(8,128)(2,1)} %wq_hbm.1, bf16[4096,256]{1,0:T(8,128)(2,1)} %bitcast.13), custom_call_target="tpu_custom_call" | custom-call | tf_op jit(solution)/shard_map/project/pallas_call | solution.py:91
  7.1 5.1 %collective-permute-start = (f32[4,2432]{1,0:T(4,128)S(1)}, f32[4,2432]{1,0:T(4,128)S(1)}, u32[]{:S(2)}, u32[]{:S(2)}) collective-permute-start(f32[4,2432]{1,0:T(4,128)S(1)} %get-tuple-element.10), channel_id=1, source_target_pairs={{0,12},{4,8},{8,4},{12,0},{1,13},{5,9},{9,5},{13,1},{2,14},{6,10},... | collective-permute-start | bytes 116744 | tf_op jit(solution)/shard_map/ppermute | solution.py:21
  12.2 0.0 collective-permute-start.1
  12.2 0.6 %collective-permute-start.2 = (f32[4,2432]{1,0:T(4,128)S(1)}, f32[4,2432]{1,0:T(4,128)S(1)}, u32[]{:S(2)}, u32[]{:S(2)}) collective-permute-start(f32[4,2432]{1,0:T(4,128)S(1)} %get-tuple-element.12), channel_id=1, source_target_pairs={{0,4},{4,0},{8,12},{12,8},{1,5},{5,1},{9,13},{13,9},{2,6},{6,2},{1... | collective-permute-start | bytes 116744 | tf_op jit(solution)/shard_map/ppermute | solution.py:21
  12.9 0.0 copy-done.1
  12.9 0.1 reshape.29.lengths
  13.0 0.1 multiply_cosine_fusion
  13.1 0.1 maximum_bitcast_fusion
  13.2 1.7 %stage.1.refs_4_ = bf16[4,2048,128]{2,1,0:T(8,128)(2,1)S(1)} custom-call(f32[4,2432]{1,0:T(4,128)S(1)} %get-tuple-element.9.after.refs_0_, bf16[4,2048,128]{2,1,0:T(8,128)(2,1)} %bitcast.14), custom_call_target="tpu_custom_call" | custom-call | tf_op jit(solution)/shard_map/stage/pallas_call | solution.py:122
  14.9 0.0 slice-start.1
  14.9 0.0 slice-start.2
  14.9 0.0 slice-start.3
  14.9 0.0 collective-permute-done.refs_1_
  14.9 2.2 %collective-permute-done.1.refs_2_ = f32[4,2432]{1,0:T(4,128)S(1)} collective-permute-done((f32[4,2432]{1,0:T(4,128)S(1)}, f32[4,2432]{1,0:T(4,128)S(1)}, u32[]{:S(2)}, u32[]{:S(2)}) %collective-permute-start.1) | collective-permute-done | bytes 38944 | tf_op jit(solution)/shard_map/ppermute | solution.py:21
  17.1 0.0 collective-permute-done.2.refs_3_
  17.1 2.1 %attend.1.refs_0_ = bf16[4,2048]{1,0:T(4,128)(2,1)S(1)} custom-call(s32[4]{0:T(128)S(1)} %reshape.29.lengths, f32[2,4,128]{2,1,0:T(4,128)S(1)} %pad_maximum_fusion.angles, f32[4,2432]{1,0:T(4,128)S(1)} %get-tuple-element.9.after.refs_0_, f32[4,2432]{1,0:T(4,128)S(1)} %collective-permute-done.refs_1_, f32[4,2432]{1,0:T(4,128)S(1)} %collective-permute-done.1.refs_2_, ...), custom_call_target="tpu_custom_call" | custom-call | flops 10000000000 | tf_op jit(solution)/shard_map/attend/pallas_call | solution.py:204
  19.2 0.0 copy-start
  19.3 1.7 %collective-permute-start.5 = (bf16[4,2048]{1,0:T(4,128)(2,1)S(1)}, bf16[4,2048]{1,0:T(4,128)(2,1)S(1)}, u32[]{:S(2)}, u32[]{:S(2)}) collective-permute-start(bf16[4,2048]{1,0:T(4,128)(2,1)S(1)} %attend.1.refs_0_), channel_id=1, source_target_pairs={{0,12},{4,8},{8,4},{12,0},{1,13},{5,9},{9,5},{13,1},{2,14},{6,10},... | collective-permute-start | bytes 49160 | tf_op jit(solution)/shard_map/ppermute | solution.py:21
  20.9 0.5 %collective-permute-start.4 = (bf16[4,2048]{1,0:T(4,128)(2,1)S(1)}, bf16[4,2048]{1,0:T(4,128)(2,1)S(1)}, u32[]{:S(2)}, u32[]{:S(2)}) collective-permute-start(bf16[4,2048]{1,0:T(4,128)(2,1)S(1)} %attend.1.refs_0_), channel_id=1, source_target_pairs={{0,8},{4,12},{8,0},{12,4},{1,9},{5,13},{9,1},{13,5},{2,10},{6,14},... | collective-permute-start | bytes 49160 | tf_op jit(solution)/shard_map/ppermute | solution.py:21
  21.4 2.3 %collective-permute-start.3 = (bf16[4,2048]{1,0:T(4,128)(2,1)S(1)}, bf16[4,2048]{1,0:T(4,128)(2,1)S(1)}, u32[]{:S(2)}, u32[]{:S(2)}) collective-permute-start(bf16[4,2048]{1,0:T(4,128)(2,1)S(1)} %attend.1.refs_0_), channel_id=1, source_target_pairs={{0,4},{4,0},{8,12},{12,8},{1,5},{5,1},{9,13},{13,9},{2,6},{6,2},{1... | collective-permute-start | bytes 49160 | tf_op jit(solution)/shard_map/ppermute | solution.py:21
  23.7 1.1 %collective-permute-done.5.refs_3_ = bf16[4,2048]{1,0:T(4,128)(2,1)S(1)} collective-permute-done((bf16[4,2048]{1,0:T(4,128)(2,1)S(1)}, bf16[4,2048]{1,0:T(4,128)(2,1)S(1)}, u32[]{:S(2)}, u32[]{:S(2)}) %collective-permute-start.5) | collective-permute-done | bytes 16416 | tf_op jit(solution)/shard_map/ppermute | solution.py:21
  24.9 0.7 %collective-permute-done.4.refs_2_ = bf16[4,2048]{1,0:T(4,128)(2,1)S(1)} collective-permute-done((bf16[4,2048]{1,0:T(4,128)(2,1)S(1)}, bf16[4,2048]{1,0:T(4,128)(2,1)S(1)}, u32[]{:S(2)}, u32[]{:S(2)}) %collective-permute-start.4) | collective-permute-done | bytes 16416 | tf_op jit(solution)/shard_map/ppermute | solution.py:21
  25.6 0.0 collective-permute-done.3.refs_1_
  25.6 0.0 slice-done
  25.6 0.0 slice-done.1
  25.6 0.0 slice-done.2
  25.6 2.3 %output.1 = f32[16,4096]{1,0:T(8,128)S(1)} custom-call(s32[1]{0:T(128)} %bitcast.position, bf16[4,2048]{1,0:T(4,128)(2,1)S(1)} %attend.1.refs_0_, bf16[4,2048]{1,0:T(4,128)(2,1)S(1)} %collective-permute-done.3.refs_1_, bf16[4,2048]{1,0:T(4,128)(2,1)S(1)} %collective-permute-done.4.refs_2_, bf16[4,2048]{1,0:T(4,128)(2,1)S(1)} %collective-permute-done.5.refs_3_, ...), custom_call_target="tpu_custom_call" | custom-call | tf_op jit(solution)/shard_map/output/pallas_call | solution.py:235
  27.9 0.0 collective-permute-start.6
  27.9 1.5 %collective-permute-done.6 = f32[16,4096]{1,0:T(8,128)S(1)} collective-permute-done((f32[16,4096]{1,0:T(8,128)S(1)}, f32[16,4096]{1,0:T(8,128)S(1)}, u32[]{:S(2)}, u32[]{:S(2)}) %collective-permute-start.6) | collective-permute-done | bytes 262176 | tf_op jit(solution)/shard_map/ppermute | solution.py:21
  29.5 1.6 %collective-permute-start.7 = (bf16[16,4096]{1,0:T(8,128)(2,1)S(1)}, bf16[16,4096]{1,0:T(8,128)(2,1)S(1)}, u32[]{:S(2)}, u32[]{:S(2)}) collective-permute-start(bf16[16,4096]{1,0:T(8,128)(2,1)S(1)} %add_convert_fusion), channel_id=1, source_target_pairs={{0,2},{1,3},{2,0},{3,1},{4,6},{5,7},{6,4},{7,5},{8,10},{9,11},{10,... | collective-permute-start | bytes 393224 | tf_op jit(solution)/shard_map/ppermute | solution.py:21
  31.1 4.0 %collective-permute-done.7 = bf16[16,4096]{1,0:T(8,128)(2,1)S(1)} collective-permute-done((bf16[16,4096]{1,0:T(8,128)(2,1)S(1)}, bf16[16,4096]{1,0:T(8,128)(2,1)S(1)}, u32[]{:S(2)}, u32[]{:S(2)}) %collective-permute-start.7) | collective-permute-done | bytes 131104 | tf_op jit(solution)/shard_map/ppermute | solution.py:21
  35.1 0.7 %fusion = bf16[2,8,4096]{2,1,0:T(8,128)(2,1)} fusion(bf16[16,4096]{1,0:T(8,128)(2,1)S(1)} %collective-permute-done.7, bf16[16,4096]{1,0:T(8,128)(2,1)S(1)} %add_convert_fusion, bf16[2,8,4096]{2,1,0:T(8,128)(2,1)S(1)} %copy-done), kind=kLoop, calls=%fused_computation.1 | loop fusion | flops 393216 | bytes 524288 | tf_op jit(solution)/shard_map/convert_element_type | solution.py:289
  (9 shorter events, 0.1 us)
Async XLA Ops:
  0.0 12.9 %copy-start.1 = (s32[2,2]{1,0:T(2,128)S(1)}, s32[2,2]{1,0:T(2,128)}, u32[]{:S(2)}) copy-start(s32[2,2]{1,0:T(2,128)} %param.8) | copy-start | bytes 52
  7.1 7.8 %collective-permute-start = (f32[4,2432]{1,0:T(4,128)S(1)}, f32[4,2432]{1,0:T(4,128)S(1)}, u32[]{:S(2)}, u32[]{:S(2)}) collective-permute-start(f32[4,2432]{1,0:T(4,128)S(1)} %get-tuple-element.10), channel_id=1, source_target_pairs={{0,12},{4,8},{8,4},{12,0},{1,13},{5,9},{9,5},{13,1},{2,14},{6,10},... | collective-permute-start | bytes 116744 | tf_op jit(solution)/shard_map/ppermute | solution.py:21
  12.2 4.9 %collective-permute-start.1 = (f32[4,2432]{1,0:T(4,128)S(1)}, f32[4,2432]{1,0:T(4,128)S(1)}, u32[]{:S(2)}, u32[]{:S(2)}) collective-permute-start(f32[4,2432]{1,0:T(4,128)S(1)} %get-tuple-element.11), channel_id=1, source_target_pairs={{0,8},{4,12},{8,0},{12,4},{1,9},{5,13},{9,1},{13,5},{2,10},{6,14},... | collective-permute-start | bytes 116744 | tf_op jit(solution)/shard_map/ppermute | solution.py:21
  12.2 4.9 %collective-permute-start.2 = (f32[4,2432]{1,0:T(4,128)S(1)}, f32[4,2432]{1,0:T(4,128)S(1)}, u32[]{:S(2)}, u32[]{:S(2)}) collective-permute-start(f32[4,2432]{1,0:T(4,128)S(1)} %get-tuple-element.12), channel_id=1, source_target_pairs={{0,4},{4,0},{8,12},{12,8},{1,5},{5,1},{9,13},{13,9},{2,6},{6,2},{1... | collective-permute-start | bytes 116744 | tf_op jit(solution)/shard_map/ppermute | solution.py:21
  13.2 12.4 %slice-start = ((s8[16777216]{0:T(1024)(128)(4,1)}), s8[4194304]{0:T(1024)(128)(4,1)S(1)}, s32[]{:S(2)}) async-start(s8[16777216]{0:T(1024)(128)(4,1)} %bitcast.11), calls=%async_computation | async-start | bytes 8388608
  14.9 10.7 %slice-start.1 = ((s8[16777216]{0:T(1024)(128)(4,1)}), s8[4194304]{0:T(1024)(128)(4,1)S(1)}, s32[]{:S(2)}) async-start(s8[16777216]{0:T(1024)(128)(4,1)} %bitcast.11), calls=%async_computation.1 | async-start | bytes 8388608
  14.9 10.7 %slice-start.2 = ((s8[16777216]{0:T(1024)(128)(4,1)}), s8[4194304]{0:T(1024)(128)(4,1)S(1)}, s32[]{:S(2)}) async-start(s8[16777216]{0:T(1024)(128)(4,1)} %bitcast.11), calls=%async_computation.2 | async-start | bytes 8388608
  14.9 10.7 %slice-start.3 = ((s8[16777216]{0:T(1024)(128)(4,1)}), s8[4194304]{0:T(1024)(128)(4,1)S(1)}, s32[]{:S(2)}) async-start(s8[16777216]{0:T(1024)(128)(4,1)} %bitcast.11), calls=%async_computation.3 | async-start | bytes 8388608
  19.2 15.9 %copy-start = (bf16[2,8,4096]{2,1,0:T(8,128)(2,1)S(1)}, bf16[2,8,4096]{2,1,0:T(8,128)(2,1)}, u32[]{:S(2)}) copy-start(bf16[2,8,4096]{2,1,0:T(8,128)(2,1)} %tokens_hbm.1) | copy-start | bytes 393220
  19.3 5.6 %collective-permute-start.5 = (bf16[4,2048]{1,0:T(4,128)(2,1)S(1)}, bf16[4,2048]{1,0:T(4,128)(2,1)S(1)}, u32[]{:S(2)}, u32[]{:S(2)}) collective-permute-start(bf16[4,2048]{1,0:T(4,128)(2,1)S(1)} %attend.1.refs_0_), channel_id=1, source_target_pairs={{0,12},{4,8},{8,4},{12,0},{1,13},{5,9},{9,5},{13,1},{2,14},{6,10},... | collective-permute-start | bytes 49160 | tf_op jit(solution)/shard_map/ppermute | solution.py:21
  20.9 4.7 %collective-permute-start.4 = (bf16[4,2048]{1,0:T(4,128)(2,1)S(1)}, bf16[4,2048]{1,0:T(4,128)(2,1)S(1)}, u32[]{:S(2)}, u32[]{:S(2)}) collective-permute-start(bf16[4,2048]{1,0:T(4,128)(2,1)S(1)} %attend.1.refs_0_), channel_id=1, source_target_pairs={{0,8},{4,12},{8,0},{12,4},{1,9},{5,13},{9,1},{13,5},{2,10},{6,14},... | collective-permute-start | bytes 49160 | tf_op jit(solution)/shard_map/ppermute | solution.py:21
  21.4 4.2 %collective-permute-start.3 = (bf16[4,2048]{1,0:T(4,128)(2,1)S(1)}, bf16[4,2048]{1,0:T(4,128)(2,1)S(1)}, u32[]{:S(2)}, u32[]{:S(2)}) collective-permute-start(bf16[4,2048]{1,0:T(4,128)(2,1)S(1)} %attend.1.refs_0_), channel_id=1, source_target_pairs={{0,4},{4,0},{8,12},{12,8},{1,5},{5,1},{9,13},{13,9},{2,6},{6,2},{1... | collective-permute-start | bytes 49160 | tf_op jit(solution)/shard_map/ppermute | solution.py:21
  27.9 1.5 %collective-permute-start.6 = (f32[16,4096]{1,0:T(8,128)S(1)}, f32[16,4096]{1,0:T(8,128)S(1)}, u32[]{:S(2)}, u32[]{:S(2)}) collective-permute-start(f32[16,4096]{1,0:T(8,128)S(1)} %output.1), channel_id=1, source_target_pairs={{0,1},{1,0},{2,3},{3,2},{4,5},{5,4},{6,7},{7,6},{8,9},{9,8},{10,11... | collective-permute-start | bytes 786440 | tf_op jit(solution)/shard_map/ppermute | solution.py:21
  29.5 5.6 %collective-permute-start.7 = (bf16[16,4096]{1,0:T(8,128)(2,1)S(1)}, bf16[16,4096]{1,0:T(8,128)(2,1)S(1)}, u32[]{:S(2)}, u32[]{:S(2)}) collective-permute-start(bf16[16,4096]{1,0:T(8,128)(2,1)S(1)} %add_convert_fusion), channel_id=1, source_target_pairs={{0,2},{1,3},{2,0},{3,1},{4,6},{5,7},{6,4},{7,5},{8,10},{9,11},{10,... | collective-permute-start | bytes 393224 | tf_op jit(solution)/shard_map/ppermute | solution.py:21

commit v4 on v3

--- a/solution.py
+++ b/solution.py
@@ -10,7 +10,6 @@
 HEAD_SIZE = 128
 LANES = 128
 VMEM = pl.BlockSpec(memory_space=pltpu.VMEM)
-SMEM = pl.BlockSpec(memory_space=pltpu.SMEM)
 ANY = pl.BlockSpec(memory_space=pl.ANY)
 HBM = pl.BlockSpec(memory_space=pltpu.HBM)
 F32 = jnp.float32
@@ -29,7 +28,7 @@
     return pltpu.CompilerParams(vmem_limit_bytes=mib * 2**20)
 
 
-def project_kernel(chunks, gx, position, tokens_hbm, gain_hbm, wq_hbm, wkv_hbm, *refs):
+def project_kernel(chunks, gx, tokens_hbm, gain_hbm, wq_hbm, wkv_hbm, *refs):
     outs = refs[:gx]
     tokens, gain, wq, wkv, normed, sums, staged, small_sems, sems = refs[gx:]
     depth = wq.shape[0] // chunks
@@ -81,17 +80,17 @@
             first = m * rows + place * here
             staged[place, m * here : (m + 1) * here, :] = sums[first : first + here, :]
     for k in range(gx):
-        outs[k][...] = staged[position[0] ^ k]
-
-
-def project(position, tokens, gain, wq, wkv, gx):
+        outs[k][...] = staged[lax.axis_index("gx") ^ k]
+
+
+def project(tokens, gain, wq, wkv, gx):
     batches, rows, width = tokens.shape
     columns = wq.shape[1] + wkv.shape[1] + LANES
     chunks = max(1, width // 256)
     return pl.pallas_call(
         functools.partial(project_kernel, chunks, gx),
         out_shape=[jax.ShapeDtypeStruct((batches * rows // gx, columns), F32)] * gx,
-        in_specs=[SMEM] + [HBM] * 4,
+        in_specs=[HBM] * 4,
         out_specs=[VMEM] * gx,
         scratch_shapes=[
             pltpu.VMEM(tokens.shape, BF16),
@@ -106,7 +105,7 @@
         ],
         compiler_params=params(32),
         name="project",
-    )(position, tokens, gain, wq, wkv)
+    )(tokens, gain, wq, wkv)
 
 
 def stage_kernel(after, cache_hbm, cache, sems):
@@ -130,7 +129,7 @@
     )(after, cache)
 
 
-def attend_kernel(model_width, parts, lengths, angles, *refs):
+def attend_kernel(model_width, parts, angles, *refs):
     received = refs[:parts]
     cache, out, table = refs[parts:]
     rows = cache.shape[0]
@@ -143,6 +142,7 @@
     scale = lax.rsqrt(sums[:, queries + 2 * HEAD_SIZE :] / model_width + 1e-05)
     cosine = angles[0]
     sine = angles[1]
+    limits = angles[2]
 
     def rotate(vectors):
         return vectors * cosine + pltpu.roll(vectors, half, 1) * sine
@@ -168,16 +168,15 @@
             )
             * inv_root
         )
-        limit = jnp.where(block == 0, lengths[r], lengths[r + pair - 1])
-        place = lax.broadcasted_iota(jnp.int32, scores.shape, 1)
-        valid = jnp.logical_and(place < 2 * limit, (place & 1) == 0)
-        scores = jnp.where(valid, scores, -1e30)
 
         def spread(vectors):
             return jnp.where(
                 block == 0, vectors[r : r + 1, :], vectors[r + pair - 1 : r + pair, :]
             )
 
+        place = lax.broadcasted_iota(jnp.int32, scores.shape, 1)
+        place = jnp.where((place & 1) == 0, place, 2 * scores.shape[1]).astype(F32)
+        scores = jnp.where(place < spread(limits)[:, :1], scores, -1e30)
         new_score = (
             jnp.sum(query.astype(BF16).astype(F32) * spread(rkey), axis=-1, keepdims=True)
             * inv_root
@@ -199,12 +198,12 @@
         ].astype(BF16)
 
 
-def attend(model_width, lengths, angles, received, cache, queries):
+def attend(model_width, angles, received, cache, queries):
     rows = cache.shape[0]
     return pl.pallas_call(
         functools.partial(attend_kernel, model_width, len(received)),
         out_shape=jax.ShapeDtypeStruct((rows, queries), BF16),
-        in_specs=[SMEM, VMEM] + [VMEM] * len(received) + [VMEM],
+        in_specs=[VMEM] * (len(received) + 2),
         out_specs=VMEM,
         scratch_shapes=[
             pltpu.VMEM((rows * queries // HEAD_SIZE, HEAD_SIZE), F32),
@@ -212,16 +211,16 @@
         compiler_params=params(4),
         cost_estimate=pl.CostEstimate(flops=10000000000, bytes_accessed=0, transcendentals=0),
         name="attend",
-    )(lengths, angles, *received, cache)
-
-
-def output_kernel(gx, batches, position, *refs):
+    )(angles, *received, cache)
+
+
+def output_kernel(gx, batches, *refs):
     received = refs[:gx]
     weights, out, blocks, left = refs[gx:]
     here = received[0].shape[0] // batches
     rows = here * gx
     for k in range(gx):
-        blocks[position[0] ^ k] = received[k][...].astype(F32)
+        blocks[lax.axis_index("gx") ^ k] = received[k][...].astype(F32)
     for place in range(gx):
         for m in range(batches):
             start = m * rows + place * here
@@ -229,13 +228,13 @@
     out[...] = jnp.dot(left[...].astype(BF16), weights[...], preferred_element_type=F32)
 
 
-def output(position, received, w_out, batches):
+def output(received, w_out, batches):
     gx = len(received)
     rows = received[0].shape[0] * gx
     return pl.pallas_call(
         functools.partial(output_kernel, gx, batches),
         out_shape=jax.ShapeDtypeStruct((rows, w_out.shape[1]), F32),
-        in_specs=[SMEM] + [VMEM] * (gx + 1),
+        in_specs=[VMEM] * (gx + 1),
         out_specs=VMEM,
         scratch_shapes=[
             pltpu.VMEM((gx, rows // gx, w_out.shape[0]), F32),
@@ -243,28 +242,33 @@
         ],
         compiler_params=params(4),
         name="output",
-    )(position, *received, w_out)
+    )(*received, w_out)
 
 
 def rotation(lengths):
     half = HEAD_SIZE // 2
     freq = 500000.0 ** (-2.0 * jnp.arange(half, dtype=F32) / HEAD_SIZE)
-    angle = lengths.reshape(-1, 1).astype(F32) * freq
+    positions = lengths.reshape(-1, 1).astype(F32)
+    angle = positions * freq
     cosine = jnp.cos(angle)
     sine = jnp.sin(angle)
     return jnp.stack(
-        [jnp.concatenate([cosine, cosine], axis=-1), jnp.concatenate([-sine, sine], axis=-1)]
+        [
+            jnp.concatenate([cosine, cosine], axis=-1),
+            jnp.concatenate([-sine, sine], axis=-1),
+            jnp.broadcast_to(2.0 * positions, (positions.shape[0], HEAD_SIZE)),
+        ]
     )
 
 
 def add_heads(value, axis, size):
-    step = 1
-    while step < size:
+    step = size // 2
+    while step > 0:
         if step > 1:
             value = value.astype(BF16)
         other = exchange(value, axis, size, step)
         value = value.astype(F32) + other.astype(F32)
-        step *= 2
+        step //= 2
     return value
 
 
@@ -274,17 +278,16 @@
     wkv = in_hbm(key_value_weight.reshape(width, -1))
     w_query = in_hbm(w_query)
     pairs = in_hbm(cache.reshape(-1, 2 * cache.shape[2], HEAD_SIZE))
-    position = lax.axis_index("gx").reshape(1)
-    sent = project(position, in_hbm(tokens), in_hbm(norm_gain), w_query, wkv, gx)
+    sent = project(in_hbm(tokens), in_hbm(norm_gain), w_query, wkv, gx)
     pairs = stage(sent[0], pairs)
     received = [sent[0]] + [exchange(sent[k], "gx", gx, k) for k in reversed(range(1, gx))]
     angles = rotation(lengths)
     attended = attend(
-        width * gx, lengths.reshape(-1), angles, received, pairs, queries
+        width * gx, angles, received, pairs, queries
     )
     gathered = {k: exchange(attended, "gx", gx, k) for k in reversed(range(1, gx))}
     gathered[0] = attended
-    projected = output(position, [gathered[k] for k in range(gx)], w_out, batches)
+    projected = output([gathered[k] for k in range(gx)], w_out, batches)
     summed = add_heads(projected, "gy", gy).reshape(tokens.shape)
     return (tokens.astype(F32) + summed).astype(BF16)
 

time: 36 us -> 34.9 us (0.969)
  waiting for transfers between devices: 9.65 us -> 9.02 us
  Pallas kernels: 13.2 us -> 12.6 us
    ppermute x8, waiting for transfers between devices: 9.65 us -> 9.02 us  [exchange(): return lax.ppermute(value, axis, [(i, i ^ step) for i in range(size)])]
    pallas_call x1, Pallas kernels: 2.13 us -> 1.59 us  [attend(): pl.pallas_call(functools.partial(attend_kernel, model_width, len(received...]
where the time goes in v4:
time: 34.9 us; the launch traced here: 34.8 us
  Pallas kernels  12.6 us (36%)
  starting transfers between devices  11.9 us (34%)
  waiting for transfers between devices  9.02 us (26%)
  other arithmetic  0.97 us (3%)
    ppermute x8, starting transfers between devices, exchange(): return lax.ppermute(value, axis, [(i, i ^ step) for i in range(size)])  11.9 us
    ppermute x8, waiting for transfers between devices, exchange(): return lax.ppermute(value, axis, [(i, i ^ step) for i in range(size)])  9.02 us
    pallas_call x1, Pallas kernels, project(): pl.pallas_call(functools.partial(project_kernel, chunks, gx), out_shape=[...  7.06 us
    pallas_call x1, Pallas kernels, output(): pl.pallas_call(functools.partial(output_kernel, gx, batches), out_shape=j...  2.28 us
    pallas_call x1, Pallas kernels, stage(): pl.pallas_call(stage_kernel, out_shape=pltpu.VMEM(cache.shape, BF16), in_...  1.7 us
    pallas_call x1, Pallas kernels, attend(): pl.pallas_call(functools.partial(attend_kernel, model_width, len(received...  1.59 us
    convert_element_type x1, other arithmetic, local(): return (tokens.astype(F32) + summed).astype(BF16)  0.71 us
  transfers between devices with their start and end apart: 8, of which 5 were waited for; matrix products, arithmetic and copies ran while one was open for 1% of the time, Pallas kernels for 5%

profile of v4, /device:TPU:0, one launch (start us, length us, event | category | flops | bytes accessed | tf_op | source)
XLA Modules:
  0.0 34.8 jit_solution(1237525214289794249)
XLA Ops:
  0.0 7.1 %project.1 = (f32[4,2432]{1,0:T(4,128)S(1)}, f32[4,2432]{1,0:T(4,128)S(1)}, f32[4,2432]{1,0:T(4,128)S(1)}, f32[4,2432]{1,0:T(4,128)S(1)}) custom-call(bf16[2,8,4096]{2,1,0:T(8,128)(2,1)} %tokens_hbm.1, bf16[4096]{0:T(1024)(128)(2,1)} %gain_hbm.1, bf16[4096,2048]{1,0:T(8,128)(2,1)} %wq_hbm.1, bf16[4096,256]{1,0:T(8,128)(2,1)} %bitcast.12), custom_call_target="tpu_custom_call" | custom-call | tf_op jit(solution)/shard_map/project/pallas_call | solution.py:90
  7.1 5.1 %collective-permute-start = (f32[4,2432]{1,0:T(4,128)S(1)}, f32[4,2432]{1,0:T(4,128)S(1)}, u32[]{:S(2)}, u32[]{:S(2)}) collective-permute-start(f32[4,2432]{1,0:T(4,128)S(1)} %get-tuple-element.10), channel_id=1, source_target_pairs={{0,12},{4,8},{8,4},{12,0},{1,13},{5,9},{9,5},{13,1},{2,14},{6,10},... | collective-permute-start | bytes 116744 | tf_op jit(solution)/shard_map/ppermute | solution.py:20
  12.2 0.0 collective-permute-start.1
  12.2 0.6 %collective-permute-start.2 = (f32[4,2432]{1,0:T(4,128)S(1)}, f32[4,2432]{1,0:T(4,128)S(1)}, u32[]{:S(2)}, u32[]{:S(2)}) collective-permute-start(f32[4,2432]{1,0:T(4,128)S(1)} %get-tuple-element.12), channel_id=1, source_target_pairs={{0,4},{4,0},{8,12},{12,8},{1,5},{5,1},{9,13},{13,9},{2,6},{6,2},{1... | collective-permute-start | bytes 116744 | tf_op jit(solution)/shard_map/ppermute | solution.py:20
  12.9 0.0 copy-done.1
  12.9 0.1 convert_element_type.31
  13.0 0.1 multiply_cosine_fusion
  13.1 0.1 maximum_bitcast_fusion
  13.2 0.1 stack_broadcast_in_dim.2
  13.2 1.7 %stage.1.refs_4_ = bf16[4,2048,128]{2,1,0:T(8,128)(2,1)S(1)} custom-call(f32[4,2432]{1,0:T(4,128)S(1)} %get-tuple-element.9.after.refs_0_, bf16[4,2048,128]{2,1,0:T(8,128)(2,1)} %bitcast.13), custom_call_target="tpu_custom_call" | custom-call | tf_op jit(solution)/shard_map/stage/pallas_call | solution.py:121
  15.0 0.0 slice-start.1
  15.0 0.0 slice-start.2
  15.0 0.0 slice-start.3
  15.0 0.0 collective-permute-done.refs_1_
  15.0 2.1 %collective-permute-done.1.refs_2_ = f32[4,2432]{1,0:T(4,128)S(1)} collective-permute-done((f32[4,2432]{1,0:T(4,128)S(1)}, f32[4,2432]{1,0:T(4,128)S(1)}, u32[]{:S(2)}, u32[]{:S(2)}) %collective-permute-start.1) | collective-permute-done | bytes 38944 | tf_op jit(solution)/shard_map/ppermute | solution.py:20
  17.1 0.0 collective-permute-done.2.refs_3_
  17.1 1.6 %attend.1.refs_0_ = bf16[4,2048]{1,0:T(4,128)(2,1)S(1)} custom-call(f32[3,4,128]{2,1,0:T(4,128)S(1)} %pad_maximum_fusion.angles, f32[4,2432]{1,0:T(4,128)S(1)} %get-tuple-element.9.after.refs_0_, f32[4,2432]{1,0:T(4,128)S(1)} %collective-permute-done.refs_1_, f32[4,2432]{1,0:T(4,128)S(1)} %collective-permute-done.1.refs_2_, ...), custom_call_target="tpu_custom_call" | custom-call | flops 10000000000 | tf_op jit(solution)/shard_map/attend/pallas_call | solution.py:203
  18.7 0.0 copy-start
  18.7 1.7 %collective-permute-start.5 = (bf16[4,2048]{1,0:T(4,128)(2,1)S(1)}, bf16[4,2048]{1,0:T(4,128)(2,1)S(1)}, u32[]{:S(2)}, u32[]{:S(2)}) collective-permute-start(bf16[4,2048]{1,0:T(4,128)(2,1)S(1)} %attend.1.refs_0_), channel_id=1, source_target_pairs={{0,12},{4,8},{8,4},{12,0},{1,13},{5,9},{9,5},{13,1},{2,14},{6,10},... | collective-permute-start | bytes 49160 | tf_op jit(solution)/shard_map/ppermute | solution.py:20
  20.4 0.4 %collective-permute-start.4 = (bf16[4,2048]{1,0:T(4,128)(2,1)S(1)}, bf16[4,2048]{1,0:T(4,128)(2,1)S(1)}, u32[]{:S(2)}, u32[]{:S(2)}) collective-permute-start(bf16[4,2048]{1,0:T(4,128)(2,1)S(1)} %attend.1.refs_0_), channel_id=1, source_target_pairs={{0,8},{4,12},{8,0},{12,4},{1,9},{5,13},{9,1},{13,5},{2,10},{6,14},... | collective-permute-start | bytes 49160 | tf_op jit(solution)/shard_map/ppermute | solution.py:20
  20.9 2.3 %collective-permute-start.3 = (bf16[4,2048]{1,0:T(4,128)(2,1)S(1)}, bf16[4,2048]{1,0:T(4,128)(2,1)S(1)}, u32[]{:S(2)}, u32[]{:S(2)}) collective-permute-start(bf16[4,2048]{1,0:T(4,128)(2,1)S(1)} %attend.1.refs_0_), channel_id=1, source_target_pairs={{0,4},{4,0},{8,12},{12,8},{1,5},{5,1},{9,13},{13,9},{2,6},{6,2},{1... | collective-permute-start | bytes 49160 | tf_op jit(solution)/shard_map/ppermute | solution.py:20
  23.2 1.1 %collective-permute-done.5.refs_3_ = bf16[4,2048]{1,0:T(4,128)(2,1)S(1)} collective-permute-done((bf16[4,2048]{1,0:T(4,128)(2,1)S(1)}, bf16[4,2048]{1,0:T(4,128)(2,1)S(1)}, u32[]{:S(2)}, u32[]{:S(2)}) %collective-permute-start.5) | collective-permute-done | bytes 16416 | tf_op jit(solution)/shard_map/ppermute | solution.py:20
  24.3 0.8 %collective-permute-done.4.refs_2_ = bf16[4,2048]{1,0:T(4,128)(2,1)S(1)} collective-permute-done((bf16[4,2048]{1,0:T(4,128)(2,1)S(1)}, bf16[4,2048]{1,0:T(4,128)(2,1)S(1)}, u32[]{:S(2)}, u32[]{:S(2)}) %collective-permute-start.4) | collective-permute-done | bytes 16416 | tf_op jit(solution)/shard_map/ppermute | solution.py:20
  25.1 0.0 collective-permute-done.3.refs_1_
  25.1 0.0 slice-done
  25.1 0.0 slice-done.1
  25.1 2.3 %output.1 = f32[16,4096]{1,0:T(8,128)S(1)} custom-call(bf16[4,2048]{1,0:T(4,128)(2,1)S(1)} %attend.1.refs_0_, bf16[4,2048]{1,0:T(4,128)(2,1)S(1)} %collective-permute-done.3.refs_1_, bf16[4,2048]{1,0:T(4,128)(2,1)S(1)} %collective-permute-done.4.refs_2_, bf16[4,2048]{1,0:T(4,128)(2,1)S(1)} %collective-permute-done.5.refs_3_, bf16[2048,4096]{1,0:T(8,128)(2,1)S(1)} %bitcast.11), custom_call_target="tpu_custom_call" | custom-call | tf_op jit(solution)/shard_map/output/pallas_call | solution.py:234
  27.4 1.6 %collective-permute-start.6 = (bf16[16,4096]{1,0:T(8,128)(2,1)S(1)}, bf16[16,4096]{1,0:T(8,128)(2,1)S(1)}, u32[]{:S(2)}, u32[]{:S(2)}) collective-permute-start(bf16[16,4096]{1,0:T(8,128)(2,1)S(1)} %convert_element_type.32), channel_id=1, source_target_pairs={{0,2},{1,3},{2,0},{3,1},{4,6},{5,7},{6,4},{7,5},{8,10},{9,11},{10,... | collective-permute-start | bytes 393224 | tf_op jit(solution)/shard_map/ppermute | solution.py:20
  29.0 3.5 %collective-permute-done.6 = bf16[16,4096]{1,0:T(8,128)(2,1)S(1)} collective-permute-done((bf16[16,4096]{1,0:T(8,128)(2,1)S(1)}, bf16[16,4096]{1,0:T(8,128)(2,1)S(1)}, u32[]{:S(2)}, u32[]{:S(2)}) %collective-permute-start.6) | collective-permute-done | bytes 131104 | tf_op jit(solution)/shard_map/ppermute | solution.py:20
  32.5 0.1 collective-permute-start.7
  32.6 1.5 %collective-permute-done.7 = f32[16,4096]{1,0:T(8,128)S(1)} collective-permute-done((f32[16,4096]{1,0:T(8,128)S(1)}, f32[16,4096]{1,0:T(8,128)S(1)}, u32[]{:S(2)}, u32[]{:S(2)}) %collective-permute-start.7) | collective-permute-done | bytes 262176 | tf_op jit(solution)/shard_map/ppermute | solution.py:20
  34.1 0.7 %fusion = bf16[2,8,4096]{2,1,0:T(8,128)(2,1)} fusion(f32[16,4096]{1,0:T(8,128)S(1)} %collective-permute-done.7, bf16[2,8,4096]{2,1,0:T(8,128)(2,1)S(1)} %copy-done, bf16[16,4096]{1,0:T(8,128)(2,1)S(1)} %collective-permute-done.6, f32[16,4096]{1,0:T(8,128)S(1)} %output.1), kind=kLoop, calls=%fused_computation.1 | loop fusion | flops 524288 | bytes 917504 | tf_op jit(solution)/shard_map/convert_element_type | solution.py:292
  (12 shorter events, 0.1 us)
Async XLA Ops:
  0.0 12.9 %copy-start.1 = (s32[2,2]{1,0:T(2,128)S(1)}, s32[2,2]{1,0:T(2,128)}, u32[]{:S(2)}) copy-start(s32[2,2]{1,0:T(2,128)} %param.8) | copy-start | bytes 52
  7.1 7.9 %collective-permute-start = (f32[4,2432]{1,0:T(4,128)S(1)}, f32[4,2432]{1,0:T(4,128)S(1)}, u32[]{:S(2)}, u32[]{:S(2)}) collective-permute-start(f32[4,2432]{1,0:T(4,128)S(1)} %get-tuple-element.10), channel_id=1, source_target_pairs={{0,12},{4,8},{8,4},{12,0},{1,13},{5,9},{9,5},{13,1},{2,14},{6,10},... | collective-permute-start | bytes 116744 | tf_op jit(solution)/shard_map/ppermute | solution.py:20
  12.2 4.9 %collective-permute-start.1 = (f32[4,2432]{1,0:T(4,128)S(1)}, f32[4,2432]{1,0:T(4,128)S(1)}, u32[]{:S(2)}, u32[]{:S(2)}) collective-permute-start(f32[4,2432]{1,0:T(4,128)S(1)} %get-tuple-element.11), channel_id=1, source_target_pairs={{0,8},{4,12},{8,0},{12,4},{1,9},{5,13},{9,1},{13,5},{2,10},{6,14},... | collective-permute-start | bytes 116744 | tf_op jit(solution)/shard_map/ppermute | solution.py:20
  12.2 4.9 %collective-permute-start.2 = (f32[4,2432]{1,0:T(4,128)S(1)}, f32[4,2432]{1,0:T(4,128)S(1)}, u32[]{:S(2)}, u32[]{:S(2)}) collective-permute-start(f32[4,2432]{1,0:T(4,128)S(1)} %get-tuple-element.12), channel_id=1, source_target_pairs={{0,4},{4,0},{8,12},{12,8},{1,5},{5,1},{9,13},{13,9},{2,6},{6,2},{1... | collective-permute-start | bytes 116744 | tf_op jit(solution)/shard_map/ppermute | solution.py:20
  13.2 11.8 %slice-start = ((s8[16777216]{0:T(1024)(128)(4,1)}), s8[4194304]{0:T(1024)(128)(4,1)S(1)}, s32[]{:S(2)}) async-start(s8[16777216]{0:T(1024)(128)(4,1)} %bitcast.10), calls=%async_computation | async-start | bytes 8388608
  15.0 10.1 %slice-start.1 = ((s8[16777216]{0:T(1024)(128)(4,1)}), s8[4194304]{0:T(1024)(128)(4,1)S(1)}, s32[]{:S(2)}) async-start(s8[16777216]{0:T(1024)(128)(4,1)} %bitcast.10), calls=%async_computation.1 | async-start | bytes 8388608
  15.0 10.1 %slice-start.2 = ((s8[16777216]{0:T(1024)(128)(4,1)}), s8[4194304]{0:T(1024)(128)(4,1)S(1)}, s32[]{:S(2)}) async-start(s8[16777216]{0:T(1024)(128)(4,1)} %bitcast.10), calls=%async_computation.2 | async-start | bytes 8388608
  15.0 10.1 %slice-start.3 = ((s8[16777216]{0:T(1024)(128)(4,1)}), s8[4194304]{0:T(1024)(128)(4,1)S(1)}, s32[]{:S(2)}) async-start(s8[16777216]{0:T(1024)(128)(4,1)} %bitcast.10), calls=%async_computation.3 | async-start | bytes 8388608
  18.7 15.4 %copy-start = (bf16[2,8,4096]{2,1,0:T(8,128)(2,1)S(1)}, bf16[2,8,4096]{2,1,0:T(8,128)(2,1)}, u32[]{:S(2)}) copy-start(bf16[2,8,4096]{2,1,0:T(8,128)(2,1)} %tokens_hbm.1) | copy-start | bytes 393220
  18.7 5.6 %collective-permute-start.5 = (bf16[4,2048]{1,0:T(4,128)(2,1)S(1)}, bf16[4,2048]{1,0:T(4,128)(2,1)S(1)}, u32[]{:S(2)}, u32[]{:S(2)}) collective-permute-start(bf16[4,2048]{1,0:T(4,128)(2,1)S(1)} %attend.1.refs_0_), channel_id=1, source_target_pairs={{0,12},{4,8},{8,4},{12,0},{1,13},{5,9},{9,5},{13,1},{2,14},{6,10},... | collective-permute-start | bytes 49160 | tf_op jit(solution)/shard_map/ppermute | solution.py:20
  20.4 4.6 %collective-permute-start.4 = (bf16[4,2048]{1,0:T(4,128)(2,1)S(1)}, bf16[4,2048]{1,0:T(4,128)(2,1)S(1)}, u32[]{:S(2)}, u32[]{:S(2)}) collective-permute-start(bf16[4,2048]{1,0:T(4,128)(2,1)S(1)} %attend.1.refs_0_), channel_id=1, source_target_pairs={{0,8},{4,12},{8,0},{12,4},{1,9},{5,13},{9,1},{13,5},{2,10},{6,14},... | collective-permute-start | bytes 49160 | tf_op jit(solution)/shard_map/ppermute | solution.py:20
  20.9 4.2 %collective-permute-start.3 = (bf16[4,2048]{1,0:T(4,128)(2,1)S(1)}, bf16[4,2048]{1,0:T(4,128)(2,1)S(1)}, u32[]{:S(2)}, u32[]{:S(2)}) collective-permute-start(bf16[4,2048]{1,0:T(4,128)(2,1)S(1)} %attend.1.refs_0_), channel_id=1, source_target_pairs={{0,4},{4,0},{8,12},{12,8},{1,5},{5,1},{9,13},{13,9},{2,6},{6,2},{1... | collective-permute-start | bytes 49160 | tf_op jit(solution)/shard_map/ppermute | solution.py:20
  27.4 5.0 %collective-permute-start.6 = (bf16[16,4096]{1,0:T(8,128)(2,1)S(1)}, bf16[16,4096]{1,0:T(8,128)(2,1)S(1)}, u32[]{:S(2)}, u32[]{:S(2)}) collective-permute-start(bf16[16,4096]{1,0:T(8,128)(2,1)S(1)} %convert_element_type.32), channel_id=1, source_target_pairs={{0,2},{1,3},{2,0},{3,1},{4,6},{5,7},{6,4},{7,5},{8,10},{9,11},{10,... | collective-permute-start | bytes 393224 | tf_op jit(solution)/shard_map/ppermute | solution.py:20
  32.5 1.6 %collective-permute-start.7 = (f32[16,4096]{1,0:T(8,128)S(1)}, f32[16,4096]{1,0:T(8,128)S(1)}, u32[]{:S(2)}, u32[]{:S(2)}) collective-permute-start(f32[16,4096]{1,0:T(8,128)S(1)} %convert_add_fusion), channel_id=1, source_target_pairs={{0,1},{1,0},{2,3},{3,2},{4,5},{5,4},{6,7},{7,6},{8,9},{9,8},{10,11... | collective-permute-start | bytes 786440 | tf_op jit(solution)/shard_map/ppermute | solution.py:20

commit v5 on v4

--- a/solution.py
+++ b/solution.py
@@ -108,31 +108,49 @@
     )(tokens, gain, wq, wkv)
 
 
-def stage_kernel(after, cache_hbm, cache, sems):
+def stage_kernel(after, cache_hbm, keys, values, cache, wide, sems):
     del after
-    rows = cache.shape[0]
+    rows, places, _ = cache.shape
+    pair = rows // keys.shape[0]
+    copies = [
+        pltpu.make_async_copy(cache_hbm.at[r], cache.at[r], sems.at[r]) for r in range(rows)
+    ]
+    for copy in copies:
+        copy.start()
     for r in range(rows):
-        pltpu.make_async_copy(cache_hbm.at[r], cache.at[r], sems.at[r]).start()
-    for r in range(rows):
-        pltpu.make_async_copy(cache_hbm.at[r], cache.at[r], sems.at[r]).wait()
+        copies[r].wait()
+        wide[r % 2] = cache[r].astype(F32)
+        lanes = slice((r % pair) * HEAD_SIZE, (r % pair + 1) * HEAD_SIZE)
+        for start, ref in ((0, keys), (1, values)):
+            ref[r // pair, :, lanes] = wide[
+                r % 2, pl.ds(start, places // 2, stride=2), :
+            ].astype(BF16)
 
 
 def stage(after, cache):
+    rows, places, _ = cache.shape
+    pair = 2 if rows % 2 == 0 else 1
+    split = pltpu.VMEM((rows // pair, places // 2, pair * HEAD_SIZE), BF16)
     return pl.pallas_call(
         stage_kernel,
-        out_shape=pltpu.VMEM(cache.shape, BF16),
+        out_shape=[split, split],
         in_specs=[ANY, HBM],
-        out_specs=VMEM,
-        scratch_shapes=[pltpu.SemaphoreType.DMA((cache.shape[0],))],
-        compiler_params=params(1),
+        out_specs=[VMEM, VMEM],
+        scratch_shapes=[
+            pltpu.VMEM(cache.shape, BF16),
+            pltpu.VMEM((2, places, HEAD_SIZE), F32),
+            pltpu.SemaphoreType.DMA((rows,)),
+        ],
+        compiler_params=params(8),
         name="stage",
     )(after, cache)
 
 
 def attend_kernel(model_width, parts, angles, *refs):
     received = refs[:parts]
-    cache, out, table = refs[parts:]
-    rows = cache.shape[0]
+    keys, values, out, table = refs[parts:]
+    rows = out.shape[0]
+    pair = rows // keys.shape[0]
     half = HEAD_SIZE // 2
     group = out.shape[1] // HEAD_SIZE
     queries = group * HEAD_SIZE
@@ -155,16 +173,16 @@
     rkey = rotate(column(queries))
     value_new = column(queries + HEAD_SIZE)
     inv_root = 1.0 / jnp.sqrt(jnp.float32(HEAD_SIZE))
-    pair = 2 if rows % 2 == 0 else 1
     for r in range(0, rows, pair):
-        members = range(r, r + pair)
         query = table[r * group : (r + pair) * group, :]
         block = lax.broadcasted_iota(jnp.int32, (pair * group, 1), 0) // group
         left = jnp.concatenate([jnp.where(block == j, query, 0.0) for j in range(pair)], axis=1)
-        right = jnp.concatenate([cache[n] for n in members], axis=1)
         scores = (
             lax.dot_general(
-                left.astype(BF16), right, (((1,), (1,)), ((), ())), preferred_element_type=F32
+                left.astype(BF16),
+                keys[r // pair],
+                (((1,), (1,)), ((), ())),
+                preferred_element_type=F32,
             )
             * inv_root
         )
@@ -174,8 +192,7 @@
                 block == 0, vectors[r : r + 1, :], vectors[r + pair - 1 : r + pair, :]
             )
 
-        place = lax.broadcasted_iota(jnp.int32, scores.shape, 1)
-        place = jnp.where((place & 1) == 0, place, 2 * scores.shape[1]).astype(F32)
+        place = lax.broadcasted_iota(jnp.int32, scores.shape, 1).astype(F32)
         scores = jnp.where(place < spread(limits)[:, :1], scores, -1e30)
         new_score = (
             jnp.sum(query.astype(BF16).astype(F32) * spread(rkey), axis=-1, keepdims=True)
@@ -185,8 +202,7 @@
         weights = jnp.exp(scores - top)
         new_weight = jnp.exp(new_score - top)
         total = jnp.sum(weights, axis=-1, keepdims=True) + new_weight
-        weights = pltpu.roll(weights, 1, 1).astype(BF16)
-        both = jnp.dot(weights, right, preferred_element_type=F32)
+        both = jnp.dot(weights.astype(BF16), values[r // pair], preferred_element_type=F32)
         summed = both[:, :HEAD_SIZE]
         for j in range(1, pair):
             summed = jnp.where(block == j, both[:, j * HEAD_SIZE : (j + 1) * HEAD_SIZE], summed)
@@ -198,12 +214,12 @@
         ].astype(BF16)
 
 
-def attend(model_width, angles, received, cache, queries):
-    rows = cache.shape[0]
+def attend(model_width, angles, received, keys, values, queries):
+    rows = angles.shape[1]
     return pl.pallas_call(
         functools.partial(attend_kernel, model_width, len(received)),
         out_shape=jax.ShapeDtypeStruct((rows, queries), BF16),
-        in_specs=[VMEM] * (len(received) + 2),
+        in_specs=[VMEM] * (len(received) + 3),
         out_specs=VMEM,
         scratch_shapes=[
             pltpu.VMEM((rows * queries // HEAD_SIZE, HEAD_SIZE), F32),
@@ -211,7 +227,7 @@
         compiler_params=params(4),
         cost_estimate=pl.CostEstimate(flops=10000000000, bytes_accessed=0, transcendentals=0),
         name="attend",
-    )(angles, *received, cache)
+    )(angles, *received, keys, values)
 
 
 def output_kernel(gx, batches, *refs):
@@ -225,7 +241,8 @@
         for m in range(batches):
             start = m * rows + place * here
             left[start : start + here, :] = blocks[place, m * here : (m + 1) * here, :]
-    out[...] = jnp.dot(left[...].astype(BF16), weights[...], preferred_element_type=F32)
+    projected = jnp.dot(left[...].astype(BF16), weights[...], preferred_element_type=F32)
+    out[...] = projected.astype(out.dtype)
 
 
 def output(received, w_out, batches):
@@ -233,7 +250,7 @@
     rows = received[0].shape[0] * gx
     return pl.pallas_call(
         functools.partial(output_kernel, gx, batches),
-        out_shape=jax.ShapeDtypeStruct((rows, w_out.shape[1]), F32),
+        out_shape=jax.ShapeDtypeStruct((rows, w_out.shape[1]), BF16),
         in_specs=[VMEM] * (gx + 1),
         out_specs=VMEM,
         scratch_shapes=[
@@ -256,7 +273,7 @@
         [
             jnp.concatenate([cosine, cosine], axis=-1),
             jnp.concatenate([-sine, sine], axis=-1),
-            jnp.broadcast_to(2.0 * positions, (positions.shape[0], HEAD_SIZE)),
+            jnp.broadcast_to(positions, (positions.shape[0], HEAD_SIZE)),
         ]
     )
 
@@ -279,11 +296,11 @@
     w_query = in_hbm(w_query)
     pairs = in_hbm(cache.reshape(-1, 2 * cache.shape[2], HEAD_SIZE))
     sent = project(in_hbm(tokens), in_hbm(norm_gain), w_query, wkv, gx)
-    pairs = stage(sent[0], pairs)
+    keys, values = stage(sent[0], pairs)
     received = [sent[0]] + [exchange(sent[k], "gx", gx, k) for k in reversed(range(1, gx))]
     angles = rotation(lengths)
     attended = attend(
-        width * gx, angles, received, pairs, queries
+        width * gx, angles, received, keys, values, queries
     )
     gathered = {k: exchange(attended, "gx", gx, k) for k in reversed(range(1, gx))}
     gathered[0] = attended

time: 34.9 us -> 34.4 us (0.986)
  Pallas kernels: 12.6 us -> 12.2 us
    pallas_call x1, Pallas kernels: 1.59 us -> 0.98 us  [attend(): pl.pallas_call(functools.partial(attend_kernel, model_width, len(received...]
where the time goes in v5:
time: 34.4 us; the launch traced here: 34.3 us
  Pallas kernels  12.2 us (35%)
  starting transfers between devices  11.8 us (34%)
  waiting for transfers between devices  9.05 us (26%)
  other arithmetic  0.95 us (3%)
    ppermute x8, starting transfers between devices, exchange(): return lax.ppermute(value, axis, [(i, i ^ step) for i in range(size)])  11.8 us
    ppermute x8, waiting for transfers between devices, exchange(): return lax.ppermute(value, axis, [(i, i ^ step) for i in range(size)])  9.05 us
    pallas_call x1, Pallas kernels, project(): pl.pallas_call(functools.partial(project_kernel, chunks, gx), out_shape=[...  7.06 us
    pallas_call x1, Pallas kernels, output(): pl.pallas_call(functools.partial(output_kernel, gx, batches), out_shape=j...  2.28 us
    pallas_call x1, Pallas kernels, stage(): pl.pallas_call(stage_kernel, out_shape=[split, split], in_specs=[ANY, HBM...  1.86 us
    pallas_call x1, Pallas kernels, attend(): pl.pallas_call(functools.partial(attend_kernel, model_width, len(received...  0.98 us
    convert_element_type x1, other arithmetic, local(): return (tokens.astype(F32) + summed).astype(BF16)  0.71 us
  transfers between devices with their start and end apart: 8, of which 5 were waited for; matrix products, arithmetic and copies ran while one was open for 1% of the time, Pallas kernels for 5%

profile of v5, /device:TPU:0, one launch (start us, length us, event | category | flops | bytes accessed | tf_op | source)
XLA Modules:
  0.0 34.3 jit_solution(4831784884132623771)
XLA Ops:
  0.0 7.1 %project.1 = (f32[4,2432]{1,0:T(4,128)S(1)}, f32[4,2432]{1,0:T(4,128)S(1)}, f32[4,2432]{1,0:T(4,128)S(1)}, f32[4,2432]{1,0:T(4,128)S(1)}) custom-call(bf16[2,8,4096]{2,1,0:T(8,128)(2,1)} %tokens_hbm.1, bf16[4096]{0:T(1024)(128)(2,1)} %gain_hbm.1, bf16[4096,2048]{1,0:T(8,128)(2,1)} %wq_hbm.1, bf16[4096,256]{1,0:T(8,128)(2,1)} %bitcast.12), custom_call_target="tpu_custom_call" | custom-call | tf_op jit(solution)/shard_map/project/pallas_call | solution.py:90
  7.1 5.1 %collective-permute-start = (f32[4,2432]{1,0:T(4,128)S(1)}, f32[4,2432]{1,0:T(4,128)S(1)}, u32[]{:S(2)}, u32[]{:S(2)}) collective-permute-start(f32[4,2432]{1,0:T(4,128)S(1)} %get-tuple-element.12), channel_id=1, source_target_pairs={{0,12},{4,8},{8,4},{12,0},{1,13},{5,9},{9,5},{13,1},{2,14},{6,10},... | collective-permute-start | bytes 116744 | tf_op jit(solution)/shard_map/ppermute | solution.py:20
  12.2 0.0 collective-permute-start.1
  12.2 0.6 %collective-permute-start.2 = (f32[4,2432]{1,0:T(4,128)S(1)}, f32[4,2432]{1,0:T(4,128)S(1)}, u32[]{:S(2)}, u32[]{:S(2)}) collective-permute-start(f32[4,2432]{1,0:T(4,128)S(1)} %get-tuple-element.14), channel_id=1, source_target_pairs={{0,4},{4,0},{8,12},{12,8},{1,5},{5,1},{9,13},{13,9},{2,6},{6,2},{1... | collective-permute-start | bytes 116744 | tf_op jit(solution)/shard_map/ppermute | solution.py:20
  12.9 0.0 copy-done.1
  12.9 0.1 convert_element_type.27
  13.0 0.1 multiply_cosine_fusion
  13.1 0.1 maximum_bitcast_fusion
  13.2 0.1 stack_broadcast_in_dim.2
  13.2 1.9 %stage.1 = (bf16[2,1024,256]{2,1,0:T(8,128)(2,1)S(1)}, bf16[2,1024,256]{2,1,0:T(8,128)(2,1)S(1)}) custom-call(f32[4,2432]{1,0:T(4,128)S(1)} %get-tuple-element.11.after.refs_0_, bf16[4,2048,128]{2,1,0:T(8,128)(2,1)} %bitcast.13), custom_call_target="tpu_custom_call" | custom-call | tf_op jit(solution)/shard_map/stage/pallas_call | solution.py:134
  15.1 0.0 collective-permute-done.refs_1_
  15.1 2.0 %collective-permute-done.1.refs_2_ = f32[4,2432]{1,0:T(4,128)S(1)} collective-permute-done((f32[4,2432]{1,0:T(4,128)S(1)}, f32[4,2432]{1,0:T(4,128)S(1)}, u32[]{:S(2)}, u32[]{:S(2)}) %collective-permute-start.1) | collective-permute-done | bytes 38944 | tf_op jit(solution)/shard_map/ppermute | solution.py:20
  17.1 0.0 collective-permute-done.2.refs_3_
  17.1 1.0 %attend.1.refs_0_ = bf16[4,2048]{1,0:T(4,128)(2,1)S(1)} custom-call(f32[3,4,128]{2,1,0:T(4,128)S(1)} %pad_maximum_fusion.angles, f32[4,2432]{1,0:T(4,128)S(1)} %get-tuple-element.11.after.refs_0_, f32[4,2432]{1,0:T(4,128)S(1)} %collective-permute-done.refs_1_, f32[4,2432]{1,0:T(4,128)S(1)} %collective-permute-done.1.refs_2_, ...), custom_call_target="tpu_custom_call" | custom-call | flops 10000000000 | tf_op jit(solution)/shard_map/attend/pallas_call | solution.py:219
  18.1 0.0 copy-start
  18.1 1.9 %collective-permute-start.5 = (bf16[4,2048]{1,0:T(4,128)(2,1)S(1)}, bf16[4,2048]{1,0:T(4,128)(2,1)S(1)}, u32[]{:S(2)}, u32[]{:S(2)}) collective-permute-start(bf16[4,2048]{1,0:T(4,128)(2,1)S(1)} %attend.1.refs_0_), channel_id=1, source_target_pairs={{0,12},{4,8},{8,4},{12,0},{1,13},{5,9},{9,5},{13,1},{2,14},{6,10},... | collective-permute-start | bytes 49160 | tf_op jit(solution)/shard_map/ppermute | solution.py:20
  20.0 0.3 collective-permute-start.4
  20.3 2.3 %collective-permute-start.3 = (bf16[4,2048]{1,0:T(4,128)(2,1)S(1)}, bf16[4,2048]{1,0:T(4,128)(2,1)S(1)}, u32[]{:S(2)}, u32[]{:S(2)}) collective-permute-start(bf16[4,2048]{1,0:T(4,128)(2,1)S(1)} %attend.1.refs_0_), channel_id=1, source_target_pairs={{0,4},{4,0},{8,12},{12,8},{1,5},{5,1},{9,13},{13,9},{2,6},{6,2},{1... | collective-permute-start | bytes 49160 | tf_op jit(solution)/shard_map/ppermute | solution.py:20
  22.6 1.2 %collective-permute-done.5.refs_3_ = bf16[4,2048]{1,0:T(4,128)(2,1)S(1)} collective-permute-done((bf16[4,2048]{1,0:T(4,128)(2,1)S(1)}, bf16[4,2048]{1,0:T(4,128)(2,1)S(1)}, u32[]{:S(2)}, u32[]{:S(2)}) %collective-permute-start.5) | collective-permute-done | bytes 16416 | tf_op jit(solution)/shard_map/ppermute | solution.py:20
  23.7 0.9 %collective-permute-done.4.refs_2_ = bf16[4,2048]{1,0:T(4,128)(2,1)S(1)} collective-permute-done((bf16[4,2048]{1,0:T(4,128)(2,1)S(1)}, bf16[4,2048]{1,0:T(4,128)(2,1)S(1)}, u32[]{:S(2)}, u32[]{:S(2)}) %collective-permute-start.4) | collective-permute-done | bytes 16416 | tf_op jit(solution)/shard_map/ppermute | solution.py:20
  24.6 0.0 collective-permute-done.3.refs_1_
  24.6 0.0 slice-done
  24.6 0.0 slice-done.1
  24.6 0.0 slice-done.2
  24.6 0.0 slice-done.3
  24.7 2.3 %output.1 = bf16[16,4096]{1,0:T(8,128)(2,1)S(1)} custom-call(bf16[4,2048]{1,0:T(4,128)(2,1)S(1)} %attend.1.refs_0_, bf16[4,2048]{1,0:T(4,128)(2,1)S(1)} %collective-permute-done.3.refs_1_, bf16[4,2048]{1,0:T(4,128)(2,1)S(1)} %collective-permute-done.4.refs_2_, bf16[4,2048]{1,0:T(4,128)(2,1)S(1)} %collective-permute-done.5.refs_3_, ...), custom_call_target="tpu_custom_call" | custom-call | tf_op jit(solution)/shard_map/output/pallas_call | solution.py:251
  26.9 1.5 %collective-permute-start.6 = (bf16[16,4096]{1,0:T(8,128)(2,1)S(1)}, bf16[16,4096]{1,0:T(8,128)(2,1)S(1)}, u32[]{:S(2)}, u32[]{:S(2)}) collective-permute-start(bf16[16,4096]{1,0:T(8,128)(2,1)S(1)} %output.1), channel_id=1, source_target_pairs={{0,2},{1,3},{2,0},{3,1},{4,6},{5,7},{6,4},{7,5},{8,10},{9,11},{10,... | collective-permute-start | bytes 393224 | tf_op jit(solution)/shard_map/ppermute | solution.py:20
  28.4 3.5 %collective-permute-done.6 = bf16[16,4096]{1,0:T(8,128)(2,1)S(1)} collective-permute-done((bf16[16,4096]{1,0:T(8,128)(2,1)S(1)}, bf16[16,4096]{1,0:T(8,128)(2,1)S(1)}, u32[]{:S(2)}, u32[]{:S(2)}) %collective-permute-start.6) | collective-permute-done | bytes 131104 | tf_op jit(solution)/shard_map/ppermute | solution.py:20
  32.0 0.1 collective-permute-start.7
  32.0 1.5 %collective-permute-done.7 = f32[16,4096]{1,0:T(8,128)S(1)} collective-permute-done((f32[16,4096]{1,0:T(8,128)S(1)}, f32[16,4096]{1,0:T(8,128)S(1)}, u32[]{:S(2)}, u32[]{:S(2)}) %collective-permute-start.7) | collective-permute-done | bytes 262176 | tf_op jit(solution)/shard_map/ppermute | solution.py:20
  33.6 0.0 copy-done
  33.6 0.7 %fusion = bf16[2,8,4096]{2,1,0:T(8,128)(2,1)} fusion(f32[16,4096]{1,0:T(8,128)S(1)} %collective-permute-done.7, bf16[2,8,4096]{2,1,0:T(8,128)(2,1)S(1)} %copy-done, bf16[16,4096]{1,0:T(8,128)(2,1)S(1)} %collective-permute-done.6, bf16[16,4096]{1,0:T(8,128)(2,1)S(1)} %output.1), kind=kLoop, calls=%fused_computation.1 | loop fusion | flops 458752 | bytes 786432 | tf_op jit(solution)/shard_map/convert_element_type | solution.py:309
  (10 shorter events, 0.1 us)
Async XLA Ops:
  0.0 12.9 %copy-start.1 = (s32[2,2]{1,0:T(2,128)S(1)}, s32[2,2]{1,0:T(2,128)}, u32[]{:S(2)}) copy-start(s32[2,2]{1,0:T(2,128)} %param.8) | copy-start | bytes 52
  7.1 8.0 %collective-permute-start = (f32[4,2432]{1,0:T(4,128)S(1)}, f32[4,2432]{1,0:T(4,128)S(1)}, u32[]{:S(2)}, u32[]{:S(2)}) collective-permute-start(f32[4,2432]{1,0:T(4,128)S(1)} %get-tuple-element.12), channel_id=1, source_target_pairs={{0,12},{4,8},{8,4},{12,0},{1,13},{5,9},{9,5},{13,1},{2,14},{6,10},... | collective-permute-start | bytes 116744 | tf_op jit(solution)/shard_map/ppermute | solution.py:20
  12.2 4.9 %collective-permute-start.1 = (f32[4,2432]{1,0:T(4,128)S(1)}, f32[4,2432]{1,0:T(4,128)S(1)}, u32[]{:S(2)}, u32[]{:S(2)}) collective-permute-start(f32[4,2432]{1,0:T(4,128)S(1)} %get-tuple-element.13), channel_id=1, source_target_pairs={{0,8},{4,12},{8,0},{12,4},{1,9},{5,13},{9,1},{13,5},{2,10},{6,14},... | collective-permute-start | bytes 116744 | tf_op jit(solution)/shard_map/ppermute | solution.py:20
  12.2 4.9 %collective-permute-start.2 = (f32[4,2432]{1,0:T(4,128)S(1)}, f32[4,2432]{1,0:T(4,128)S(1)}, u32[]{:S(2)}, u32[]{:S(2)}) collective-permute-start(f32[4,2432]{1,0:T(4,128)S(1)} %get-tuple-element.14), channel_id=1, source_target_pairs={{0,4},{4,0},{8,12},{12,8},{1,5},{5,1},{9,13},{13,9},{2,6},{6,2},{1... | collective-permute-start | bytes 116744 | tf_op jit(solution)/shard_map/ppermute | solution.py:20
  13.2 11.4 %slice-start = ((s8[16777216]{0:T(1024)(128)(4,1)}), s8[4194304]{0:T(1024)(128)(4,1)S(1)}, s32[]{:S(2)}) async-start(s8[16777216]{0:T(1024)(128)(4,1)} %bitcast.10), calls=%async_computation | async-start | bytes 8388608
  17.1 7.5 %slice-start.1 = ((s8[16777216]{0:T(1024)(128)(4,1)}), s8[4194304]{0:T(1024)(128)(4,1)S(1)}, s32[]{:S(2)}) async-start(s8[16777216]{0:T(1024)(128)(4,1)} %bitcast.10), calls=%async_computation.1 | async-start | bytes 8388608
  17.1 7.5 %slice-start.2 = ((s8[16777216]{0:T(1024)(128)(4,1)}), s8[4194304]{0:T(1024)(128)(4,1)S(1)}, s32[]{:S(2)}) async-start(s8[16777216]{0:T(1024)(128)(4,1)} %bitcast.10), calls=%async_computation.2 | async-start | bytes 8388608
  17.1 7.5 %slice-start.3 = ((s8[16777216]{0:T(1024)(128)(4,1)}), s8[4194304]{0:T(1024)(128)(4,1)S(1)}, s32[]{:S(2)}) async-start(s8[16777216]{0:T(1024)(128)(4,1)} %bitcast.10), calls=%async_computation.3 | async-start | bytes 8388608
  18.1 15.5 %copy-start = (bf16[2,8,4096]{2,1,0:T(8,128)(2,1)S(1)}, bf16[2,8,4096]{2,1,0:T(8,128)(2,1)}, u32[]{:S(2)}) copy-start(bf16[2,8,4096]{2,1,0:T(8,128)(2,1)} %tokens_hbm.1) | copy-start | bytes 393220
  18.1 5.6 %collective-permute-start.5 = (bf16[4,2048]{1,0:T(4,128)(2,1)S(1)}, bf16[4,2048]{1,0:T(4,128)(2,1)S(1)}, u32[]{:S(2)}, u32[]{:S(2)}) collective-permute-start(bf16[4,2048]{1,0:T(4,128)(2,1)S(1)} %attend.1.refs_0_), channel_id=1, source_target_pairs={{0,12},{4,8},{8,4},{12,0},{1,13},{5,9},{9,5},{13,1},{2,14},{6,10},... | collective-permute-start | bytes 49160 | tf_op jit(solution)/shard_map/ppermute | solution.py:20
  20.0 4.6 %collective-permute-start.4 = (bf16[4,2048]{1,0:T(4,128)(2,1)S(1)}, bf16[4,2048]{1,0:T(4,128)(2,1)S(1)}, u32[]{:S(2)}, u32[]{:S(2)}) collective-permute-start(bf16[4,2048]{1,0:T(4,128)(2,1)S(1)} %attend.1.refs_0_), channel_id=1, source_target_pairs={{0,8},{4,12},{8,0},{12,4},{1,9},{5,13},{9,1},{13,5},{2,10},{6,14},... | collective-permute-start | bytes 49160 | tf_op jit(solution)/shard_map/ppermute | solution.py:20
  20.3 4.3 %collective-permute-start.3 = (bf16[4,2048]{1,0:T(4,128)(2,1)S(1)}, bf16[4,2048]{1,0:T(4,128)(2,1)S(1)}, u32[]{:S(2)}, u32[]{:S(2)}) collective-permute-start(bf16[4,2048]{1,0:T(4,128)(2,1)S(1)} %attend.1.refs_0_), channel_id=1, source_target_pairs={{0,4},{4,0},{8,12},{12,8},{1,5},{5,1},{9,13},{13,9},{2,6},{6,2},{1... | collective-permute-start | bytes 49160 | tf_op jit(solution)/shard_map/ppermute | solution.py:20
  26.9 5.0 %collective-permute-start.6 = (bf16[16,4096]{1,0:T(8,128)(2,1)S(1)}, bf16[16,4096]{1,0:T(8,128)(2,1)S(1)}, u32[]{:S(2)}, u32[]{:S(2)}) collective-permute-start(bf16[16,4096]{1,0:T(8,128)(2,1)S(1)} %output.1), channel_id=1, source_target_pairs={{0,2},{1,3},{2,0},{3,1},{4,6},{5,7},{6,4},{7,5},{8,10},{9,11},{10,... | collective-permute-start | bytes 393224 | tf_op jit(solution)/shard_map/ppermute | solution.py:20
  32.0 1.6 %collective-permute-start.7 = (f32[16,4096]{1,0:T(8,128)S(1)}, f32[16,4096]{1,0:T(8,128)S(1)}, u32[]{:S(2)}, u32[]{:S(2)}) collective-permute-start(f32[16,4096]{1,0:T(8,128)S(1)} %convert_add_fusion), channel_id=1, source_target_pairs={{0,1},{1,0},{2,3},{3,2},{4,5},{5,4},{6,7},{7,6},{8,9},{9,8},{10,11... | collective-permute-start | bytes 786440 | tf_op jit(solution)/shard_map/ppermute | solution.py:20

commit v6 on v5

--- a/solution.py
+++ b/solution.py
@@ -28,10 +28,9 @@
     return pltpu.CompilerParams(vmem_limit_bytes=mib * 2**20)
 
 
-def project_kernel(chunks, gx, tokens_hbm, gain_hbm, wq_hbm, wkv_hbm, *refs):
+def project_kernel(depths, gx, tokens_hbm, gain_hbm, wq_hbm, wkv_hbm, *refs):
     outs = refs[:gx]
-    tokens, gain, wq, wkv, normed, sums, staged, small_sems, sems = refs[gx:]
-    depth = wq.shape[0] // chunks
+    tokens, gain, wq, wkv, blocks, left, normed, sums, small_sems, sems = refs[gx:]
     small = [
         pltpu.make_async_copy(tokens_hbm, tokens, small_sems.at[0]),
         pltpu.make_async_copy(gain_hbm, gain, small_sems.at[1]),
@@ -39,56 +38,75 @@
     small[0].start()
     small[1].start()
 
-    def chunk(c):
-        part = (pl.ds(c * depth, depth), slice(None))
+    def chunk(start, depth, c):
+        part = (pl.ds(start, depth), slice(None))
         return (
             pltpu.make_async_copy(wq_hbm.at[part], wq.at[part], sems.at[0, c]),
             pltpu.make_async_copy(wkv_hbm.at[part], wkv.at[part], sems.at[1, c]),
         )
 
-    @pl.loop(0, chunks)
-    def _(c):
-        for copy in chunk(c):
-            copy.start()
+    chunks = []
+    start = 0
+    for count, depth in depths:
+        index = len(chunks)
+
+        @pl.loop(0, count)
+        def _(c, start=start, depth=depth, index=index):
+            for copy in chunk(start + c * depth, depth, index + c):
+                copy.start()
+
+        chunks += [(start + c * depth, depth, index + c) for c in range(count)]
+        start += count * depth
 
     small[0].wait()
     small[1].wait()
     batches, rows, width = tokens.shape
-    total = batches * rows
     queries = wq.shape[1]
     keyvals = wkv.shape[1]
+    here = rows // gx
+    each = batches * here
     x_full = tokens[...].astype(F32)
-    squares = jnp.sum(x_full * x_full, axis=-1, keepdims=True).reshape(total, 1)
-    sums[:, queries + keyvals :] = jnp.broadcast_to(squares, (total, LANES))
-    scaled = (x_full * gain[...].astype(F32)).astype(BF16)
-    normed[...] = scaled.reshape(total, width)
-    for c in range(chunks):
-        for copy in chunk(c):
-            copy.wait()
-        left = normed[:, c * depth : (c + 1) * depth]
-        for weights, start, stop in ((wq, 0, queries), (wkv, queries, queries + keyvals)):
-            part = jnp.dot(
-                left, weights[c * depth : (c + 1) * depth, :], preferred_element_type=F32
-            )
-            if c == 0:
-                sums[:, start:stop] = part
-            else:
-                sums[:, start:stop] += part
-    here = rows // gx
+    squares = jnp.sum(x_full * x_full, axis=-1, keepdims=True)
+    scaled = x_full * gain[...].astype(F32)
     for place in range(gx):
         for m in range(batches):
-            first = m * rows + place * here
-            staged[place, m * here : (m + 1) * here, :] = sums[first : first + here, :]
+            to = slice(m * here, (m + 1) * here)
+            of = slice(place * here, (place + 1) * here)
+            blocks[place, to, :width] = scaled[m, of, :]
+            blocks[place, to, width:] = jnp.broadcast_to(squares[m, of, :], (here, LANES))
     for k in range(gx):
-        outs[k][...] = staged[lax.axis_index("gx") ^ k]
+        left[k * each : (k + 1) * each, :] = blocks[lax.axis_index("gx") ^ k]
+    normed[...] = left[:, :width].astype(BF16)
+    for k in range(gx):
+        outs[k][:, queries + keyvals :] = left[k * each : (k + 1) * each, width:]
+    for start, depth, index in chunks:
+        for copy in chunk(start, depth, index):
+            copy.wait()
+        rows_in = slice(start, start + depth)
+        for weights, first, last in ((wq, 0, queries), (wkv, queries, queries + keyvals)):
+            part = jnp.dot(normed[:, rows_in], weights[rows_in, :], preferred_element_type=F32)
+            if start > 0:
+                part = part + sums[:, first:last]
+            if start + depth < width:
+                sums[:, first:last] = part
+            else:
+                for k in range(gx):
+                    outs[k][:, first:last] = part[k * each : (k + 1) * each, :]
+
+
+def chunk_depths(width):
+    if width % 1024 or width == 1024:
+        return [(1, width)]
+    return [(width // 1024 - 1, 1024), (1, 512), (1, 256), (2, 128)]
 
 
 def project(tokens, gain, wq, wkv, gx):
     batches, rows, width = tokens.shape
     columns = wq.shape[1] + wkv.shape[1] + LANES
-    chunks = max(1, width // 256)
+    depths = chunk_depths(width)
+    chunks = sum(count for count, _ in depths)
     return pl.pallas_call(
-        functools.partial(project_kernel, chunks, gx),
+        functools.partial(project_kernel, depths, gx),
         out_shape=[jax.ShapeDtypeStruct((batches * rows // gx, columns), F32)] * gx,
         in_specs=[HBM] * 4,
         out_specs=[VMEM] * gx,
@@ -97,9 +115,10 @@
             pltpu.VMEM(gain.shape, BF16),
             pltpu.VMEM(wq.shape, BF16),
             pltpu.VMEM(wkv.shape, BF16),
+            pltpu.VMEM((gx, batches * rows // gx, width + LANES), F32),
+            pltpu.VMEM((batches * rows, width + LANES), F32),
             pltpu.VMEM((batches * rows, width), BF16),
-            pltpu.VMEM((batches * rows, columns), F32),
-            pltpu.VMEM((gx, batches * rows // gx, columns), F32),
+            pltpu.VMEM((batches * rows, columns - LANES), F32),
             pltpu.SemaphoreType.DMA((2,)),
             pltpu.SemaphoreType.DMA((2, chunks)),
         ],
@@ -281,8 +300,7 @@
 def add_heads(value, axis, size):
     step = size // 2
     while step > 0:
-        if step > 1:
-            value = value.astype(BF16)
+        value = value.astype(BF16)
         other = exchange(value, axis, size, step)
         value = value.astype(F32) + other.astype(F32)
         step //= 2

time: 34.4 us -> 33.9 us (0.985)
  no operation moved by 1% of the time
where the time goes in v6:
time: 33.9 us; the launch traced here: 33.8 us
  Pallas kernels  11.9 us (35%)
  starting transfers between devices  11.8 us (35%)
  waiting for transfers between devices  8.85 us (26%)
  other arithmetic  0.95 us (3%)
    ppermute x8, starting transfers between devices, exchange(): return lax.ppermute(value, axis, [(i, i ^ step) for i in range(size)])  11.8 us
    ppermute x8, waiting for transfers between devices, exchange(): return lax.ppermute(value, axis, [(i, i ^ step) for i in range(size)])  8.85 us
    pallas_call x1, Pallas kernels, project(): pl.pallas_call(functools.partial(project_kernel, depths, gx), out_shape=[...  6.77 us
    pallas_call x1, Pallas kernels, output(): pl.pallas_call(functools.partial(output_kernel, gx, batches), out_shape=j...  2.28 us
    pallas_call x1, Pallas kernels, stage(): pl.pallas_call(stage_kernel, out_shape=[split, split], in_specs=[ANY, HBM...  1.86 us
    pallas_call x1, Pallas kernels, attend(): pl.pallas_call(functools.partial(attend_kernel, model_width, len(received...  0.98 us
    convert_element_type x1, other arithmetic, local(): return (tokens.astype(F32) + summed).astype(BF16)  0.71 us
  transfers between devices with their start and end apart: 8, of which 5 were waited for; matrix products, arithmetic and copies ran while one was open for 1% of the time, Pallas kernels for 5%

profile of v6, /device:TPU:0, one launch (start us, length us, event | category | flops | bytes accessed | tf_op | source)
XLA Modules:
  0.0 33.8 jit_solution(12515163414308593449)
XLA Ops:
  0.0 6.8 %project.1 = (f32[4,2432]{1,0:T(4,128)S(1)}, f32[4,2432]{1,0:T(4,128)S(1)}, f32[4,2432]{1,0:T(4,128)S(1)}, f32[4,2432]{1,0:T(4,128)S(1)}) custom-call(bf16[2,8,4096]{2,1,0:T(8,128)(2,1)} %tokens_hbm.1, bf16[4096]{0:T(1024)(128)(2,1)} %gain_hbm.1, bf16[4096,2048]{1,0:T(8,128)(2,1)} %wq_hbm.1, bf16[4096,256]{1,0:T(8,128)(2,1)} %bitcast.12), custom_call_target="tpu_custom_call" | custom-call | tf_op jit(solution)/shard_map/project/pallas_call | solution.py:108
  6.8 5.1 %collective-permute-start = (f32[4,2432]{1,0:T(4,128)S(1)}, f32[4,2432]{1,0:T(4,128)S(1)}, u32[]{:S(2)}, u32[]{:S(2)}) collective-permute-start(f32[4,2432]{1,0:T(4,128)S(1)} %get-tuple-element.12), channel_id=1, source_target_pairs={{0,12},{4,8},{8,4},{12,0},{1,13},{5,9},{9,5},{13,1},{2,14},{6,10},... | collective-permute-start | bytes 116744 | tf_op jit(solution)/shard_map/ppermute | solution.py:20
  11.9 0.0 collective-permute-start.1
  11.9 0.6 %collective-permute-start.2 = (f32[4,2432]{1,0:T(4,128)S(1)}, f32[4,2432]{1,0:T(4,128)S(1)}, u32[]{:S(2)}, u32[]{:S(2)}) collective-permute-start(f32[4,2432]{1,0:T(4,128)S(1)} %get-tuple-element.14), channel_id=1, source_target_pairs={{0,4},{4,0},{8,12},{12,8},{1,5},{5,1},{9,13},{13,9},{2,6},{6,2},{1... | collective-permute-start | bytes 116744 | tf_op jit(solution)/shard_map/ppermute | solution.py:20
  12.6 0.0 copy-done.1
  12.6 0.1 convert_element_type.36
  12.7 0.1 multiply_cosine_fusion
  12.8 0.1 maximum_bitcast_fusion
  12.9 0.1 stack_broadcast_in_dim.2
  12.9 1.9 %stage.1 = (bf16[2,1024,256]{2,1,0:T(8,128)(2,1)S(1)}, bf16[2,1024,256]{2,1,0:T(8,128)(2,1)S(1)}) custom-call(f32[4,2432]{1,0:T(4,128)S(1)} %get-tuple-element.11.after.refs_0_, bf16[4,2048,128]{2,1,0:T(8,128)(2,1)} %bitcast.13), custom_call_target="tpu_custom_call" | custom-call | tf_op jit(solution)/shard_map/stage/pallas_call | solution.py:153
  14.8 0.0 collective-permute-done.refs_1_
  14.8 2.0 %collective-permute-done.1.refs_2_ = f32[4,2432]{1,0:T(4,128)S(1)} collective-permute-done((f32[4,2432]{1,0:T(4,128)S(1)}, f32[4,2432]{1,0:T(4,128)S(1)}, u32[]{:S(2)}, u32[]{:S(2)}) %collective-permute-start.1) | collective-permute-done | bytes 38944 | tf_op jit(solution)/shard_map/ppermute | solution.py:20
  16.8 0.0 collective-permute-done.2.refs_3_
  16.8 1.0 %attend.1.refs_0_ = bf16[4,2048]{1,0:T(4,128)(2,1)S(1)} custom-call(f32[3,4,128]{2,1,0:T(4,128)S(1)} %pad_maximum_fusion.angles, f32[4,2432]{1,0:T(4,128)S(1)} %get-tuple-element.11.after.refs_0_, f32[4,2432]{1,0:T(4,128)S(1)} %collective-permute-done.refs_1_, f32[4,2432]{1,0:T(4,128)S(1)} %collective-permute-done.1.refs_2_, ...), custom_call_target="tpu_custom_call" | custom-call | flops 10000000000 | tf_op jit(solution)/shard_map/attend/pallas_call | solution.py:238
  17.8 0.0 copy-start
  17.8 1.9 %collective-permute-start.5 = (bf16[4,2048]{1,0:T(4,128)(2,1)S(1)}, bf16[4,2048]{1,0:T(4,128)(2,1)S(1)}, u32[]{:S(2)}, u32[]{:S(2)}) collective-permute-start(bf16[4,2048]{1,0:T(4,128)(2,1)S(1)} %attend.1.refs_0_), channel_id=1, source_target_pairs={{0,12},{4,8},{8,4},{12,0},{1,13},{5,9},{9,5},{13,1},{2,14},{6,10},... | collective-permute-start | bytes 49160 | tf_op jit(solution)/shard_map/ppermute | solution.py:20
  19.7 0.3 collective-permute-start.4
  20.0 2.3 %collective-permute-start.3 = (bf16[4,2048]{1,0:T(4,128)(2,1)S(1)}, bf16[4,2048]{1,0:T(4,128)(2,1)S(1)}, u32[]{:S(2)}, u32[]{:S(2)}) collective-permute-start(bf16[4,2048]{1,0:T(4,128)(2,1)S(1)} %attend.1.refs_0_), channel_id=1, source_target_pairs={{0,4},{4,0},{8,12},{12,8},{1,5},{5,1},{9,13},{13,9},{2,6},{6,2},{1... | collective-permute-start | bytes 49160 | tf_op jit(solution)/shard_map/ppermute | solution.py:20
  22.3 1.1 %collective-permute-done.5.refs_3_ = bf16[4,2048]{1,0:T(4,128)(2,1)S(1)} collective-permute-done((bf16[4,2048]{1,0:T(4,128)(2,1)S(1)}, bf16[4,2048]{1,0:T(4,128)(2,1)S(1)}, u32[]{:S(2)}, u32[]{:S(2)}) %collective-permute-start.5) | collective-permute-done | bytes 16416 | tf_op jit(solution)/shard_map/ppermute | solution.py:20
  23.4 0.9 %collective-permute-done.4.refs_2_ = bf16[4,2048]{1,0:T(4,128)(2,1)S(1)} collective-permute-done((bf16[4,2048]{1,0:T(4,128)(2,1)S(1)}, bf16[4,2048]{1,0:T(4,128)(2,1)S(1)}, u32[]{:S(2)}, u32[]{:S(2)}) %collective-permute-start.4) | collective-permute-done | bytes 16416 | tf_op jit(solution)/shard_map/ppermute | solution.py:20
  24.3 0.0 collective-permute-done.3.refs_1_
  24.3 0.0 slice-done
  24.3 0.0 slice-done.1
  24.3 0.0 slice-done.2
  24.3 0.0 slice-done.3
  24.4 2.3 %output.1 = bf16[16,4096]{1,0:T(8,128)(2,1)S(1)} custom-call(bf16[4,2048]{1,0:T(4,128)(2,1)S(1)} %attend.1.refs_0_, bf16[4,2048]{1,0:T(4,128)(2,1)S(1)} %collective-permute-done.3.refs_1_, bf16[4,2048]{1,0:T(4,128)(2,1)S(1)} %collective-permute-done.4.refs_2_, bf16[4,2048]{1,0:T(4,128)(2,1)S(1)} %collective-permute-done.5.refs_3_, ...), custom_call_target="tpu_custom_call" | custom-call | tf_op jit(solution)/shard_map/output/pallas_call | solution.py:270
  26.6 1.5 %collective-permute-start.6 = (bf16[16,4096]{1,0:T(8,128)(2,1)S(1)}, bf16[16,4096]{1,0:T(8,128)(2,1)S(1)}, u32[]{:S(2)}, u32[]{:S(2)}) collective-permute-start(bf16[16,4096]{1,0:T(8,128)(2,1)S(1)} %output.1), channel_id=1, source_target_pairs={{0,2},{1,3},{2,0},{3,1},{4,6},{5,7},{6,4},{7,5},{8,10},{9,11},{10,... | collective-permute-start | bytes 393224 | tf_op jit(solution)/shard_map/ppermute | solution.py:20
  28.1 3.5 %collective-permute-done.6 = bf16[16,4096]{1,0:T(8,128)(2,1)S(1)} collective-permute-done((bf16[16,4096]{1,0:T(8,128)(2,1)S(1)}, bf16[16,4096]{1,0:T(8,128)(2,1)S(1)}, u32[]{:S(2)}, u32[]{:S(2)}) %collective-permute-start.6) | collective-permute-done | bytes 131104 | tf_op jit(solution)/shard_map/ppermute | solution.py:20
  31.7 0.1 collective-permute-start.7
  31.7 1.3 %collective-permute-done.7 = bf16[16,4096]{1,0:T(8,128)(2,1)S(1)} collective-permute-done((bf16[16,4096]{1,0:T(8,128)(2,1)S(1)}, bf16[16,4096]{1,0:T(8,128)(2,1)S(1)}, u32[]{:S(2)}, u32[]{:S(2)}) %collective-permute-start.7) | collective-permute-done | bytes 131104 | tf_op jit(solution)/shard_map/ppermute | solution.py:20
  33.1 0.0 copy-done
  33.1 0.7 %fusion = bf16[2,8,4096]{2,1,0:T(8,128)(2,1)} fusion(bf16[16,4096]{1,0:T(8,128)(2,1)S(1)} %collective-permute-done.7, bf16[16,4096]{1,0:T(8,128)(2,1)S(1)} %add_convert_fusion, bf16[2,8,4096]{2,1,0:T(8,128)(2,1)S(1)} %copy-done), kind=kLoop, calls=%fused_computation.1 | loop fusion | flops 393216 | bytes 524288 | tf_op jit(solution)/shard_map/convert_element_type | solution.py:327
  (10 shorter events, 0.1 us)
Async XLA Ops:
  0.0 12.6 %copy-start.1 = (s32[2,2]{1,0:T(2,128)S(1)}, s32[2,2]{1,0:T(2,128)}, u32[]{:S(2)}) copy-start(s32[2,2]{1,0:T(2,128)} %param.8) | copy-start | bytes 52
  6.8 8.0 %collective-permute-start = (f32[4,2432]{1,0:T(4,128)S(1)}, f32[4,2432]{1,0:T(4,128)S(1)}, u32[]{:S(2)}, u32[]{:S(2)}) collective-permute-start(f32[4,2432]{1,0:T(4,128)S(1)} %get-tuple-element.12), channel_id=1, source_target_pairs={{0,12},{4,8},{8,4},{12,0},{1,13},{5,9},{9,5},{13,1},{2,14},{6,10},... | collective-permute-start | bytes 116744 | tf_op jit(solution)/shard_map/ppermute | solution.py:20
  11.9 4.9 %collective-permute-start.1 = (f32[4,2432]{1,0:T(4,128)S(1)}, f32[4,2432]{1,0:T(4,128)S(1)}, u32[]{:S(2)}, u32[]{:S(2)}) collective-permute-start(f32[4,2432]{1,0:T(4,128)S(1)} %get-tuple-element.13), channel_id=1, source_target_pairs={{0,8},{4,12},{8,0},{12,4},{1,9},{5,13},{9,1},{13,5},{2,10},{6,14},... | collective-permute-start | bytes 116744 | tf_op jit(solution)/shard_map/ppermute | solution.py:20
  11.9 4.9 %collective-permute-start.2 = (f32[4,2432]{1,0:T(4,128)S(1)}, f32[4,2432]{1,0:T(4,128)S(1)}, u32[]{:S(2)}, u32[]{:S(2)}) collective-permute-start(f32[4,2432]{1,0:T(4,128)S(1)} %get-tuple-element.14), channel_id=1, source_target_pairs={{0,4},{4,0},{8,12},{12,8},{1,5},{5,1},{9,13},{13,9},{2,6},{6,2},{1... | collective-permute-start | bytes 116744 | tf_op jit(solution)/shard_map/ppermute | solution.py:20
  12.9 11.4 %slice-start = ((s8[16777216]{0:T(1024)(128)(4,1)}), s8[4194304]{0:T(1024)(128)(4,1)S(1)}, s32[]{:S(2)}) async-start(s8[16777216]{0:T(1024)(128)(4,1)} %bitcast.10), calls=%async_computation | async-start | bytes 8388608
  16.8 7.5 %slice-start.1 = ((s8[16777216]{0:T(1024)(128)(4,1)}), s8[4194304]{0:T(1024)(128)(4,1)S(1)}, s32[]{:S(2)}) async-start(s8[16777216]{0:T(1024)(128)(4,1)} %bitcast.10), calls=%async_computation.1 | async-start | bytes 8388608
  16.8 7.5 %slice-start.2 = ((s8[16777216]{0:T(1024)(128)(4,1)}), s8[4194304]{0:T(1024)(128)(4,1)S(1)}, s32[]{:S(2)}) async-start(s8[16777216]{0:T(1024)(128)(4,1)} %bitcast.10), calls=%async_computation.2 | async-start | bytes 8388608
  16.8 7.5 %slice-start.3 = ((s8[16777216]{0:T(1024)(128)(4,1)}), s8[4194304]{0:T(1024)(128)(4,1)S(1)}, s32[]{:S(2)}) async-start(s8[16777216]{0:T(1024)(128)(4,1)} %bitcast.10), calls=%async_computation.3 | async-start | bytes 8388608
  17.8 15.3 %copy-start = (bf16[2,8,4096]{2,1,0:T(8,128)(2,1)S(1)}, bf16[2,8,4096]{2,1,0:T(8,128)(2,1)}, u32[]{:S(2)}) copy-start(bf16[2,8,4096]{2,1,0:T(8,128)(2,1)} %tokens_hbm.1) | copy-start | bytes 393220
  17.8 5.6 %collective-permute-start.5 = (bf16[4,2048]{1,0:T(4,128)(2,1)S(1)}, bf16[4,2048]{1,0:T(4,128)(2,1)S(1)}, u32[]{:S(2)}, u32[]{:S(2)}) collective-permute-start(bf16[4,2048]{1,0:T(4,128)(2,1)S(1)} %attend.1.refs_0_), channel_id=1, source_target_pairs={{0,12},{4,8},{8,4},{12,0},{1,13},{5,9},{9,5},{13,1},{2,14},{6,10},... | collective-permute-start | bytes 49160 | tf_op jit(solution)/shard_map/ppermute | solution.py:20
  19.7 4.6 %collective-permute-start.4 = (bf16[4,2048]{1,0:T(4,128)(2,1)S(1)}, bf16[4,2048]{1,0:T(4,128)(2,1)S(1)}, u32[]{:S(2)}, u32[]{:S(2)}) collective-permute-start(bf16[4,2048]{1,0:T(4,128)(2,1)S(1)} %attend.1.refs_0_), channel_id=1, source_target_pairs={{0,8},{4,12},{8,0},{12,4},{1,9},{5,13},{9,1},{13,5},{2,10},{6,14},... | collective-permute-start | bytes 49160 | tf_op jit(solution)/shard_map/ppermute | solution.py:20
  20.0 4.3 %collective-permute-start.3 = (bf16[4,2048]{1,0:T(4,128)(2,1)S(1)}, bf16[4,2048]{1,0:T(4,128)(2,1)S(1)}, u32[]{:S(2)}, u32[]{:S(2)}) collective-permute-start(bf16[4,2048]{1,0:T(4,128)(2,1)S(1)} %attend.1.refs_0_), channel_id=1, source_target_pairs={{0,4},{4,0},{8,12},{12,8},{1,5},{5,1},{9,13},{13,9},{2,6},{6,2},{1... | collective-permute-start | bytes 49160 | tf_op jit(solution)/shard_map/ppermute | solution.py:20
  26.6 5.0 %collective-permute-start.6 = (bf16[16,4096]{1,0:T(8,128)(2,1)S(1)}, bf16[16,4096]{1,0:T(8,128)(2,1)S(1)}, u32[]{:S(2)}, u32[]{:S(2)}) collective-permute-start(bf16[16,4096]{1,0:T(8,128)(2,1)S(1)} %output.1), channel_id=1, source_target_pairs={{0,2},{1,3},{2,0},{3,1},{4,6},{5,7},{6,4},{7,5},{8,10},{9,11},{10,... | collective-permute-start | bytes 393224 | tf_op jit(solution)/shard_map/ppermute | solution.py:20
  31.7 1.4 %collective-permute-start.7 = (bf16[16,4096]{1,0:T(8,128)(2,1)S(1)}, bf16[16,4096]{1,0:T(8,128)(2,1)S(1)}, u32[]{:S(2)}, u32[]{:S(2)}) collective-permute-start(bf16[16,4096]{1,0:T(8,128)(2,1)S(1)} %add_convert_fusion), channel_id=1, source_target_pairs={{0,1},{1,0},{2,3},{3,2},{4,5},{5,4},{6,7},{7,6},{8,9},{9,8},{10,11... | collective-permute-start | bytes 393224 | tf_op jit(solution)/shard_map/ppermute | solution.py:20

commit v7 on v6

--- a/solution.py
+++ b/solution.py
@@ -14,6 +14,7 @@
 HBM = pl.BlockSpec(memory_space=pltpu.HBM)
 F32 = jnp.float32
 BF16 = jnp.bfloat16
+COVER = 10**10
 
 
 def exchange(value, axis, size, step):
@@ -140,19 +141,19 @@
         copies[r].wait()
         wide[r % 2] = cache[r].astype(F32)
         lanes = slice((r % pair) * HEAD_SIZE, (r % pair + 1) * HEAD_SIZE)
-        for start, ref in ((0, keys), (1, values)):
-            ref[r // pair, :, lanes] = wide[
-                r % 2, pl.ds(start, places // 2, stride=2), :
-            ].astype(BF16)
+        every = [wide[r % 2, pl.ds(k, places // 2, stride=2), :].astype(BF16) for k in range(2)]
+        keys[r // pair, lanes, :] = every[0].T
+        values[r // pair, :, lanes] = every[1]
 
 
 def stage(after, cache):
     rows, places, _ = cache.shape
     pair = 2 if rows % 2 == 0 else 1
     split = pltpu.VMEM((rows // pair, places // 2, pair * HEAD_SIZE), BF16)
+    turned = pltpu.VMEM((rows // pair, pair * HEAD_SIZE, places // 2), BF16)
     return pl.pallas_call(
         stage_kernel,
-        out_shape=[split, split],
+        out_shape=[turned, split],
         in_specs=[ANY, HBM],
         out_specs=[VMEM, VMEM],
         scratch_shapes=[
@@ -200,7 +201,7 @@
             lax.dot_general(
                 left.astype(BF16),
                 keys[r // pair],
-                (((1,), (1,)), ((), ())),
+                (((1,), (0,)), ((), ())),
                 preferred_element_type=F32,
             )
             * inv_root
@@ -244,23 +245,26 @@
             pltpu.VMEM((rows * queries // HEAD_SIZE, HEAD_SIZE), F32),
         ],
         compiler_params=params(4),
-        cost_estimate=pl.CostEstimate(flops=10000000000, bytes_accessed=0, transcendentals=0),
+        cost_estimate=pl.CostEstimate(flops=COVER, bytes_accessed=0, transcendentals=0),
         name="attend",
     )(angles, *received, keys, values)
 
 
 def output_kernel(gx, batches, *refs):
     received = refs[:gx]
-    weights, out, blocks, left = refs[gx:]
+    weights, out, blocks = refs[gx:]
     here = received[0].shape[0] // batches
-    rows = here * gx
     for k in range(gx):
         blocks[lax.axis_index("gx") ^ k] = received[k][...].astype(F32)
-    for place in range(gx):
-        for m in range(batches):
-            start = m * rows + place * here
-            left[start : start + here, :] = blocks[place, m * here : (m + 1) * here, :]
-    projected = jnp.dot(left[...].astype(BF16), weights[...], preferred_element_type=F32)
+    left = jnp.concatenate(
+        [
+            blocks[place, m * here : (m + 1) * here, :]
+            for m in range(batches)
+            for place in range(gx)
+        ],
+        axis=0,
+    )
+    projected = jnp.dot(left.astype(BF16), weights[...], preferred_element_type=F32)
     out[...] = projected.astype(out.dtype)
 
 
@@ -274,7 +278,6 @@
         out_specs=VMEM,
         scratch_shapes=[
             pltpu.VMEM((gx, rows // gx, w_out.shape[0]), F32),
-            pltpu.VMEM((rows, w_out.shape[0]), F32),
         ],
         compiler_params=params(4),
         name="output",

time: 33.9 us -> 33.9 us (level)
  transfers between devices with their start and end apart: 8 -> 8, of which waited for: 5 -> 5; matrix products, arithmetic and copies ran while one was open for 1% -> 1% of each run, Pallas kernels for 5% -> 6%
where the time goes in v7:
time: 33.9 us; the launch traced here: 33.8 us
  Pallas kernels  11.9 us (35%)
  starting transfers between devices  11.8 us (35%)
  waiting for transfers between devices  8.86 us (26%)
  other arithmetic  0.95 us (3%)
    ppermute x8, starting transfers between devices, exchange(): return lax.ppermute(value, axis, [(i, i ^ step) for i in range(size)])  11.8 us
    ppermute x8, waiting for transfers between devices, exchange(): return lax.ppermute(value, axis, [(i, i ^ step) for i in range(size)])  8.86 us
    pallas_call x1, Pallas kernels, project(): pl.pallas_call(functools.partial(project_kernel, depths, gx), out_shape=[...  6.77 us
    pallas_call x1, Pallas kernels, output(): pl.pallas_call(functools.partial(output_kernel, gx, batches), out_shape=j...  2.27 us
    pallas_call x1, Pallas kernels, stage(): pl.pallas_call(stage_kernel, out_shape=[turned, split], in_specs=[ANY, HB...  1.97 us
    pallas_call x1, Pallas kernels, attend(): pl.pallas_call(functools.partial(attend_kernel, model_width, len(received...  0.88 us
    convert_element_type x1, other arithmetic, local(): return (tokens.astype(F32) + summed).astype(BF16)  0.71 us
  transfers between devices with their start and end apart: 8, of which 5 were waited for; matrix products, arithmetic and copies ran while one was open for 1% of the time, Pallas kernels for 6%

profile of v7, /device:TPU:0, one launch (start us, length us, event | category | flops | bytes accessed | tf_op | source)
XLA Modules:
  0.0 33.8 jit_solution(16703020320392874108)
XLA Ops:
  0.0 6.8 %project.1 = (f32[4,2432]{1,0:T(4,128)S(1)}, f32[4,2432]{1,0:T(4,128)S(1)}, f32[4,2432]{1,0:T(4,128)S(1)}, f32[4,2432]{1,0:T(4,128)S(1)}) custom-call(bf16[2,8,4096]{2,1,0:T(8,128)(2,1)} %tokens_hbm.1, bf16[4096]{0:T(1024)(128)(2,1)} %gain_hbm.1, bf16[4096,2048]{1,0:T(8,128)(2,1)} %wq_hbm.1, bf16[4096,256]{1,0:T(8,128)(2,1)} %bitcast.12), custom_call_target="tpu_custom_call" | custom-call | tf_op jit(solution)/shard_map/project/pallas_call | solution.py:109
  6.8 5.1 %collective-permute-start = (f32[4,2432]{1,0:T(4,128)S(1)}, f32[4,2432]{1,0:T(4,128)S(1)}, u32[]{:S(2)}, u32[]{:S(2)}) collective-permute-start(f32[4,2432]{1,0:T(4,128)S(1)} %get-tuple-element.12), channel_id=1, source_target_pairs={{0,12},{4,8},{8,4},{12,0},{1,13},{5,9},{9,5},{13,1},{2,14},{6,10},... | collective-permute-start | bytes 116744 | tf_op jit(solution)/shard_map/ppermute | solution.py:21
  11.9 0.0 collective-permute-start.1
  11.9 0.6 %collective-permute-start.2 = (f32[4,2432]{1,0:T(4,128)S(1)}, f32[4,2432]{1,0:T(4,128)S(1)}, u32[]{:S(2)}, u32[]{:S(2)}) collective-permute-start(f32[4,2432]{1,0:T(4,128)S(1)} %get-tuple-element.14), channel_id=1, source_target_pairs={{0,4},{4,0},{8,12},{12,8},{1,5},{5,1},{9,13},{13,9},{2,6},{6,2},{1... | collective-permute-start | bytes 116744 | tf_op jit(solution)/shard_map/ppermute | solution.py:21
  12.6 0.0 copy-done.1
  12.6 0.1 convert_element_type.36
  12.7 0.1 multiply_cosine_fusion
  12.8 0.1 maximum_bitcast_fusion
  12.9 0.1 stack_broadcast_in_dim.2
  12.9 2.0 %stage.1 = (bf16[2,256,1024]{2,1,0:T(8,128)(2,1)S(1)}, bf16[2,1024,256]{2,1,0:T(8,128)(2,1)S(1)}) custom-call(f32[4,2432]{1,0:T(4,128)S(1)} %get-tuple-element.11.after.refs_0_, bf16[4,2048,128]{2,1,0:T(8,128)(2,1)} %bitcast.13), custom_call_target="tpu_custom_call" | custom-call | tf_op jit(solution)/shard_map/stage/pallas_call | solution.py:154
  14.9 0.0 collective-permute-done.refs_1_
  14.9 1.9 %collective-permute-done.1.refs_2_ = f32[4,2432]{1,0:T(4,128)S(1)} collective-permute-done((f32[4,2432]{1,0:T(4,128)S(1)}, f32[4,2432]{1,0:T(4,128)S(1)}, u32[]{:S(2)}, u32[]{:S(2)}) %collective-permute-start.1) | collective-permute-done | bytes 38944 | tf_op jit(solution)/shard_map/ppermute | solution.py:21
  16.8 0.0 collective-permute-done.2.refs_3_
  16.8 0.9 %attend.1.refs_0_ = bf16[4,2048]{1,0:T(4,128)(2,1)S(1)} custom-call(f32[3,4,128]{2,1,0:T(4,128)S(1)} %pad_maximum_fusion.angles, f32[4,2432]{1,0:T(4,128)S(1)} %get-tuple-element.11.after.refs_0_, f32[4,2432]{1,0:T(4,128)S(1)} %collective-permute-done.refs_1_, f32[4,2432]{1,0:T(4,128)S(1)} %collective-permute-done.1.refs_2_, ...), custom_call_target="tpu_custom_call" | custom-call | flops 10000000000 | tf_op jit(solution)/shard_map/attend/pallas_call | solution.py:239
  17.7 0.0 copy-start
  17.7 2.0 %collective-permute-start.5 = (bf16[4,2048]{1,0:T(4,128)(2,1)S(1)}, bf16[4,2048]{1,0:T(4,128)(2,1)S(1)}, u32[]{:S(2)}, u32[]{:S(2)}) collective-permute-start(bf16[4,2048]{1,0:T(4,128)(2,1)S(1)} %attend.1.refs_0_), channel_id=1, source_target_pairs={{0,12},{4,8},{8,4},{12,0},{1,13},{5,9},{9,5},{13,1},{2,14},{6,10},... | collective-permute-start | bytes 49160 | tf_op jit(solution)/shard_map/ppermute | solution.py:21
  19.7 0.2 collective-permute-start.4
  19.9 2.3 %collective-permute-start.3 = (bf16[4,2048]{1,0:T(4,128)(2,1)S(1)}, bf16[4,2048]{1,0:T(4,128)(2,1)S(1)}, u32[]{:S(2)}, u32[]{:S(2)}) collective-permute-start(bf16[4,2048]{1,0:T(4,128)(2,1)S(1)} %attend.1.refs_0_), channel_id=1, source_target_pairs={{0,4},{4,0},{8,12},{12,8},{1,5},{5,1},{9,13},{13,9},{2,6},{6,2},{1... | collective-permute-start | bytes 49160 | tf_op jit(solution)/shard_map/ppermute | solution.py:21
  22.2 1.3 %collective-permute-done.5.refs_3_ = bf16[4,2048]{1,0:T(4,128)(2,1)S(1)} collective-permute-done((bf16[4,2048]{1,0:T(4,128)(2,1)S(1)}, bf16[4,2048]{1,0:T(4,128)(2,1)S(1)}, u32[]{:S(2)}, u32[]{:S(2)}) %collective-permute-start.5) | collective-permute-done | bytes 16416 | tf_op jit(solution)/shard_map/ppermute | solution.py:21
  23.4 0.9 %collective-permute-done.4.refs_2_ = bf16[4,2048]{1,0:T(4,128)(2,1)S(1)} collective-permute-done((bf16[4,2048]{1,0:T(4,128)(2,1)S(1)}, bf16[4,2048]{1,0:T(4,128)(2,1)S(1)}, u32[]{:S(2)}, u32[]{:S(2)}) %collective-permute-start.4) | collective-permute-done | bytes 16416 | tf_op jit(solution)/shard_map/ppermute | solution.py:21
  24.3 0.0 collective-permute-done.3.refs_1_
  24.3 0.0 slice-done
  24.3 0.0 slice-done.1
  24.3 0.0 slice-done.2
  24.4 0.0 slice-done.3
  24.4 2.3 %output.1 = bf16[16,4096]{1,0:T(8,128)(2,1)S(1)} custom-call(bf16[4,2048]{1,0:T(4,128)(2,1)S(1)} %attend.1.refs_0_, bf16[4,2048]{1,0:T(4,128)(2,1)S(1)} %collective-permute-done.3.refs_1_, bf16[4,2048]{1,0:T(4,128)(2,1)S(1)} %collective-permute-done.4.refs_2_, bf16[4,2048]{1,0:T(4,128)(2,1)S(1)} %collective-permute-done.5.refs_3_, ...), custom_call_target="tpu_custom_call" | custom-call | tf_op jit(solution)/shard_map/output/pallas_call | solution.py:274
  26.7 1.5 %collective-permute-start.6 = (bf16[16,4096]{1,0:T(8,128)(2,1)S(1)}, bf16[16,4096]{1,0:T(8,128)(2,1)S(1)}, u32[]{:S(2)}, u32[]{:S(2)}) collective-permute-start(bf16[16,4096]{1,0:T(8,128)(2,1)S(1)} %output.1), channel_id=1, source_target_pairs={{0,2},{1,3},{2,0},{3,1},{4,6},{5,7},{6,4},{7,5},{8,10},{9,11},{10,... | collective-permute-start | bytes 393224 | tf_op jit(solution)/shard_map/ppermute | solution.py:21
  28.2 3.5 %collective-permute-done.6 = bf16[16,4096]{1,0:T(8,128)(2,1)S(1)} collective-permute-done((bf16[16,4096]{1,0:T(8,128)(2,1)S(1)}, bf16[16,4096]{1,0:T(8,128)(2,1)S(1)}, u32[]{:S(2)}, u32[]{:S(2)}) %collective-permute-start.6) | collective-permute-done | bytes 131104 | tf_op jit(solution)/shard_map/ppermute | solution.py:21
  31.7 0.1 collective-permute-start.7
  31.8 1.3 %collective-permute-done.7 = bf16[16,4096]{1,0:T(8,128)(2,1)S(1)} collective-permute-done((bf16[16,4096]{1,0:T(8,128)(2,1)S(1)}, bf16[16,4096]{1,0:T(8,128)(2,1)S(1)}, u32[]{:S(2)}, u32[]{:S(2)}) %collective-permute-start.7) | collective-permute-done | bytes 131104 | tf_op jit(solution)/shard_map/ppermute | solution.py:21
  33.1 0.0 copy-done
  33.1 0.7 %fusion = bf16[2,8,4096]{2,1,0:T(8,128)(2,1)} fusion(bf16[16,4096]{1,0:T(8,128)(2,1)S(1)} %collective-permute-done.7, bf16[16,4096]{1,0:T(8,128)(2,1)S(1)} %add_convert_fusion, bf16[2,8,4096]{2,1,0:T(8,128)(2,1)S(1)} %copy-done), kind=kLoop, calls=%fused_computation.1 | loop fusion | flops 393216 | bytes 524288 | tf_op jit(solution)/shard_map/convert_element_type | solution.py:330
  (10 shorter events, 0.1 us)
Async XLA Ops:
  0.0 12.6 %copy-start.1 = (s32[2,2]{1,0:T(2,128)S(1)}, s32[2,2]{1,0:T(2,128)}, u32[]{:S(2)}) copy-start(s32[2,2]{1,0:T(2,128)} %param.8) | copy-start | bytes 52
  6.8 8.1 %collective-permute-start = (f32[4,2432]{1,0:T(4,128)S(1)}, f32[4,2432]{1,0:T(4,128)S(1)}, u32[]{:S(2)}, u32[]{:S(2)}) collective-permute-start(f32[4,2432]{1,0:T(4,128)S(1)} %get-tuple-element.12), channel_id=1, source_target_pairs={{0,12},{4,8},{8,4},{12,0},{1,13},{5,9},{9,5},{13,1},{2,14},{6,10},... | collective-permute-start | bytes 116744 | tf_op jit(solution)/shard_map/ppermute | solution.py:21
  11.9 4.9 %collective-permute-start.1 = (f32[4,2432]{1,0:T(4,128)S(1)}, f32[4,2432]{1,0:T(4,128)S(1)}, u32[]{:S(2)}, u32[]{:S(2)}) collective-permute-start(f32[4,2432]{1,0:T(4,128)S(1)} %get-tuple-element.13), channel_id=1, source_target_pairs={{0,8},{4,12},{8,0},{12,4},{1,9},{5,13},{9,1},{13,5},{2,10},{6,14},... | collective-permute-start | bytes 116744 | tf_op jit(solution)/shard_map/ppermute | solution.py:21
  11.9 4.9 %collective-permute-start.2 = (f32[4,2432]{1,0:T(4,128)S(1)}, f32[4,2432]{1,0:T(4,128)S(1)}, u32[]{:S(2)}, u32[]{:S(2)}) collective-permute-start(f32[4,2432]{1,0:T(4,128)S(1)} %get-tuple-element.14), channel_id=1, source_target_pairs={{0,4},{4,0},{8,12},{12,8},{1,5},{5,1},{9,13},{13,9},{2,6},{6,2},{1... | collective-permute-start | bytes 116744 | tf_op jit(solution)/shard_map/ppermute | solution.py:21
  12.9 11.4 %slice-start = ((s8[16777216]{0:T(1024)(128)(4,1)}), s8[4194304]{0:T(1024)(128)(4,1)S(1)}, s32[]{:S(2)}) async-start(s8[16777216]{0:T(1024)(128)(4,1)} %bitcast.10), calls=%async_computation | async-start | bytes 8388608
  16.8 7.5 %slice-start.1 = ((s8[16777216]{0:T(1024)(128)(4,1)}), s8[4194304]{0:T(1024)(128)(4,1)S(1)}, s32[]{:S(2)}) async-start(s8[16777216]{0:T(1024)(128)(4,1)} %bitcast.10), calls=%async_computation.1 | async-start | bytes 8388608
  16.8 7.5 %slice-start.2 = ((s8[16777216]{0:T(1024)(128)(4,1)}), s8[4194304]{0:T(1024)(128)(4,1)S(1)}, s32[]{:S(2)}) async-start(s8[16777216]{0:T(1024)(128)(4,1)} %bitcast.10), calls=%async_computation.2 | async-start | bytes 8388608
  16.8 7.6 %slice-start.3 = ((s8[16777216]{0:T(1024)(128)(4,1)}), s8[4194304]{0:T(1024)(128)(4,1)S(1)}, s32[]{:S(2)}) async-start(s8[16777216]{0:T(1024)(128)(4,1)} %bitcast.10), calls=%async_computation.3 | async-start | bytes 8388608
  17.7 15.4 %copy-start = (bf16[2,8,4096]{2,1,0:T(8,128)(2,1)S(1)}, bf16[2,8,4096]{2,1,0:T(8,128)(2,1)}, u32[]{:S(2)}) copy-start(bf16[2,8,4096]{2,1,0:T(8,128)(2,1)} %tokens_hbm.1) | copy-start | bytes 393220
  17.7 5.7 %collective-permute-start.5 = (bf16[4,2048]{1,0:T(4,128)(2,1)S(1)}, bf16[4,2048]{1,0:T(4,128)(2,1)S(1)}, u32[]{:S(2)}, u32[]{:S(2)}) collective-permute-start(bf16[4,2048]{1,0:T(4,128)(2,1)S(1)} %attend.1.refs_0_), channel_id=1, source_target_pairs={{0,12},{4,8},{8,4},{12,0},{1,13},{5,9},{9,5},{13,1},{2,14},{6,10},... | collective-permute-start | bytes 49160 | tf_op jit(solution)/shard_map/ppermute | solution.py:21
  19.7 4.6 %collective-permute-start.4 = (bf16[4,2048]{1,0:T(4,128)(2,1)S(1)}, bf16[4,2048]{1,0:T(4,128)(2,1)S(1)}, u32[]{:S(2)}, u32[]{:S(2)}) collective-permute-start(bf16[4,2048]{1,0:T(4,128)(2,1)S(1)} %attend.1.refs_0_), channel_id=1, source_target_pairs={{0,8},{4,12},{8,0},{12,4},{1,9},{5,13},{9,1},{13,5},{2,10},{6,14},... | collective-permute-start | bytes 49160 | tf_op jit(solution)/shard_map/ppermute | solution.py:21
  19.9 4.5 %collective-permute-start.3 = (bf16[4,2048]{1,0:T(4,128)(2,1)S(1)}, bf16[4,2048]{1,0:T(4,128)(2,1)S(1)}, u32[]{:S(2)}, u32[]{:S(2)}) collective-permute-start(bf16[4,2048]{1,0:T(4,128)(2,1)S(1)} %attend.1.refs_0_), channel_id=1, source_target_pairs={{0,4},{4,0},{8,12},{12,8},{1,5},{5,1},{9,13},{13,9},{2,6},{6,2},{1... | collective-permute-start | bytes 49160 | tf_op jit(solution)/shard_map/ppermute | solution.py:21
  26.7 5.0 %collective-permute-start.6 = (bf16[16,4096]{1,0:T(8,128)(2,1)S(1)}, bf16[16,4096]{1,0:T(8,128)(2,1)S(1)}, u32[]{:S(2)}, u32[]{:S(2)}) collective-permute-start(bf16[16,4096]{1,0:T(8,128)(2,1)S(1)} %output.1), channel_id=1, source_target_pairs={{0,2},{1,3},{2,0},{3,1},{4,6},{5,7},{6,4},{7,5},{8,10},{9,11},{10,... | collective-permute-start | bytes 393224 | tf_op jit(solution)/shard_map/ppermute | solution.py:21
  31.7 1.4 %collective-permute-start.7 = (bf16[16,4096]{1,0:T(8,128)(2,1)S(1)}, bf16[16,4096]{1,0:T(8,128)(2,1)S(1)}, u32[]{:S(2)}, u32[]{:S(2)}) collective-permute-start(bf16[16,4096]{1,0:T(8,128)(2,1)S(1)} %add_convert_fusion), channel_id=1, source_target_pairs={{0,1},{1,0},{2,3},{3,2},{4,5},{5,4},{6,7},{7,6},{8,9},{9,8},{10,11... | collective-permute-start | bytes 393224 | tf_op jit(solution)/shard_map/ppermute | solution.py:21

commit v8 on v7

--- a/solution.py
+++ b/solution.py
@@ -98,7 +98,7 @@
 def chunk_depths(width):
     if width % 1024 or width == 1024:
         return [(1, width)]
-    return [(width // 1024 - 1, 1024), (1, 512), (1, 256), (2, 128)]
+    return [(2, 128), (width // 1024 - 1, 1024), (1, 512), (2, 128)]
 
 
 def project(tokens, gain, wq, wkv, gx):

time: 33.9 us -> 34.1 us (level)
  no operation moved by 1% of the time
where the time goes in v8:
time: 34.1 us; the launch traced here: 34 us
  Pallas kernels  12 us (35%)
  starting transfers between devices  11.8 us (35%)
  waiting for transfers between devices  8.86 us (26%)
  other arithmetic  0.95 us (3%)
    ppermute x8, starting transfers between devices, exchange(): return lax.ppermute(value, axis, [(i, i ^ step) for i in range(size)])  11.8 us
    ppermute x8, waiting for transfers between devices, exchange(): return lax.ppermute(value, axis, [(i, i ^ step) for i in range(size)])  8.86 us
    pallas_call x1, Pallas kernels, project(): pl.pallas_call(functools.partial(project_kernel, depths, gx), out_shape=[...  6.92 us
    pallas_call x1, Pallas kernels, output(): pl.pallas_call(functools.partial(output_kernel, gx, batches), out_shape=j...  2.27 us
    pallas_call x1, Pallas kernels, stage(): pl.pallas_call(stage_kernel, out_shape=[turned, split], in_specs=[ANY, HB...  1.97 us
    pallas_call x1, Pallas kernels, attend(): pl.pallas_call(functools.partial(attend_kernel, model_width, len(received...  0.88 us
    convert_element_type x1, other arithmetic, local(): return (tokens.astype(F32) + summed).astype(BF16)  0.71 us
  transfers between devices with their start and end apart: 8, of which 5 were waited for; matrix products, arithmetic and copies ran while one was open for 1% of the time, Pallas kernels for 6%

profile of v8, /device:TPU:0, one launch (start us, length us, event | category | flops | bytes accessed | tf_op | source)
XLA Modules:
  0.0 34.0 jit_solution(5595100961467771400)
XLA Ops:
  0.0 6.9 %project.1 = (f32[4,2432]{1,0:T(4,128)S(1)}, f32[4,2432]{1,0:T(4,128)S(1)}, f32[4,2432]{1,0:T(4,128)S(1)}, f32[4,2432]{1,0:T(4,128)S(1)}) custom-call(bf16[2,8,4096]{2,1,0:T(8,128)(2,1)} %tokens_hbm.1, bf16[4096]{0:T(1024)(128)(2,1)} %gain_hbm.1, bf16[4096,2048]{1,0:T(8,128)(2,1)} %wq_hbm.1, bf16[4096,256]{1,0:T(8,128)(2,1)} %bitcast.12), custom_call_target="tpu_custom_call" | custom-call | tf_op jit(solution)/shard_map/project/pallas_call | solution.py:109
  6.9 5.1 %collective-permute-start = (f32[4,2432]{1,0:T(4,128)S(1)}, f32[4,2432]{1,0:T(4,128)S(1)}, u32[]{:S(2)}, u32[]{:S(2)}) collective-permute-start(f32[4,2432]{1,0:T(4,128)S(1)} %get-tuple-element.12), channel_id=1, source_target_pairs={{0,12},{4,8},{8,4},{12,0},{1,13},{5,9},{9,5},{13,1},{2,14},{6,10},... | collective-permute-start | bytes 116744 | tf_op jit(solution)/shard_map/ppermute | solution.py:21
  12.1 0.0 collective-permute-start.1
  12.1 0.6 %collective-permute-start.2 = (f32[4,2432]{1,0:T(4,128)S(1)}, f32[4,2432]{1,0:T(4,128)S(1)}, u32[]{:S(2)}, u32[]{:S(2)}) collective-permute-start(f32[4,2432]{1,0:T(4,128)S(1)} %get-tuple-element.14), channel_id=1, source_target_pairs={{0,4},{4,0},{8,12},{12,8},{1,5},{5,1},{9,13},{13,9},{2,6},{6,2},{1... | collective-permute-start | bytes 116744 | tf_op jit(solution)/shard_map/ppermute | solution.py:21
  12.7 0.0 copy-done.1
  12.8 0.1 convert_element_type.36
  12.8 0.1 multiply_cosine_fusion
  12.9 0.1 maximum_bitcast_fusion
  13.0 0.1 stack_broadcast_in_dim.2
  13.1 2.0 %stage.1 = (bf16[2,256,1024]{2,1,0:T(8,128)(2,1)S(1)}, bf16[2,1024,256]{2,1,0:T(8,128)(2,1)S(1)}) custom-call(f32[4,2432]{1,0:T(4,128)S(1)} %get-tuple-element.11.after.refs_0_, bf16[4,2048,128]{2,1,0:T(8,128)(2,1)} %bitcast.13), custom_call_target="tpu_custom_call" | custom-call | tf_op jit(solution)/shard_map/stage/pallas_call | solution.py:154
  15.1 0.0 collective-permute-done.refs_1_
  15.1 1.9 %collective-permute-done.1.refs_2_ = f32[4,2432]{1,0:T(4,128)S(1)} collective-permute-done((f32[4,2432]{1,0:T(4,128)S(1)}, f32[4,2432]{1,0:T(4,128)S(1)}, u32[]{:S(2)}, u32[]{:S(2)}) %collective-permute-start.1) | collective-permute-done | bytes 38944 | tf_op jit(solution)/shard_map/ppermute | solution.py:21
  17.0 0.0 collective-permute-done.2.refs_3_
  17.0 0.9 %attend.1.refs_0_ = bf16[4,2048]{1,0:T(4,128)(2,1)S(1)} custom-call(f32[3,4,128]{2,1,0:T(4,128)S(1)} %pad_maximum_fusion.angles, f32[4,2432]{1,0:T(4,128)S(1)} %get-tuple-element.11.after.refs_0_, f32[4,2432]{1,0:T(4,128)S(1)} %collective-permute-done.refs_1_, f32[4,2432]{1,0:T(4,128)S(1)} %collective-permute-done.1.refs_2_, ...), custom_call_target="tpu_custom_call" | custom-call | flops 10000000000 | tf_op jit(solution)/shard_map/attend/pallas_call | solution.py:239
  17.9 0.0 copy-start
  17.9 2.0 %collective-permute-start.5 = (bf16[4,2048]{1,0:T(4,128)(2,1)S(1)}, bf16[4,2048]{1,0:T(4,128)(2,1)S(1)}, u32[]{:S(2)}, u32[]{:S(2)}) collective-permute-start(bf16[4,2048]{1,0:T(4,128)(2,1)S(1)} %attend.1.refs_0_), channel_id=1, source_target_pairs={{0,12},{4,8},{8,4},{12,0},{1,13},{5,9},{9,5},{13,1},{2,14},{6,10},... | collective-permute-start | bytes 49160 | tf_op jit(solution)/shard_map/ppermute | solution.py:21
  19.8 0.2 collective-permute-start.4
  20.0 2.3 %collective-permute-start.3 = (bf16[4,2048]{1,0:T(4,128)(2,1)S(1)}, bf16[4,2048]{1,0:T(4,128)(2,1)S(1)}, u32[]{:S(2)}, u32[]{:S(2)}) collective-permute-start(bf16[4,2048]{1,0:T(4,128)(2,1)S(1)} %attend.1.refs_0_), channel_id=1, source_target_pairs={{0,4},{4,0},{8,12},{12,8},{1,5},{5,1},{9,13},{13,9},{2,6},{6,2},{1... | collective-permute-start | bytes 49160 | tf_op jit(solution)/shard_map/ppermute | solution.py:21
  22.3 1.3 %collective-permute-done.5.refs_3_ = bf16[4,2048]{1,0:T(4,128)(2,1)S(1)} collective-permute-done((bf16[4,2048]{1,0:T(4,128)(2,1)S(1)}, bf16[4,2048]{1,0:T(4,128)(2,1)S(1)}, u32[]{:S(2)}, u32[]{:S(2)}) %collective-permute-start.5) | collective-permute-done | bytes 16416 | tf_op jit(solution)/shard_map/ppermute | solution.py:21
  23.6 0.9 %collective-permute-done.4.refs_2_ = bf16[4,2048]{1,0:T(4,128)(2,1)S(1)} collective-permute-done((bf16[4,2048]{1,0:T(4,128)(2,1)S(1)}, bf16[4,2048]{1,0:T(4,128)(2,1)S(1)}, u32[]{:S(2)}, u32[]{:S(2)}) %collective-permute-start.4) | collective-permute-done | bytes 16416 | tf_op jit(solution)/shard_map/ppermute | solution.py:21
  24.5 0.0 collective-permute-done.3.refs_1_
  24.5 0.0 slice-done
  24.5 0.0 slice-done.1
  24.5 0.0 slice-done.2
  24.5 0.0 slice-done.3
  24.5 2.3 %output.1 = bf16[16,4096]{1,0:T(8,128)(2,1)S(1)} custom-call(bf16[4,2048]{1,0:T(4,128)(2,1)S(1)} %attend.1.refs_0_, bf16[4,2048]{1,0:T(4,128)(2,1)S(1)} %collective-permute-done.3.refs_1_, bf16[4,2048]{1,0:T(4,128)(2,1)S(1)} %collective-permute-done.4.refs_2_, bf16[4,2048]{1,0:T(4,128)(2,1)S(1)} %collective-permute-done.5.refs_3_, ...), custom_call_target="tpu_custom_call" | custom-call | tf_op jit(solution)/shard_map/output/pallas_call | solution.py:274
  26.8 1.5 %collective-permute-start.6 = (bf16[16,4096]{1,0:T(8,128)(2,1)S(1)}, bf16[16,4096]{1,0:T(8,128)(2,1)S(1)}, u32[]{:S(2)}, u32[]{:S(2)}) collective-permute-start(bf16[16,4096]{1,0:T(8,128)(2,1)S(1)} %output.1), channel_id=1, source_target_pairs={{0,2},{1,3},{2,0},{3,1},{4,6},{5,7},{6,4},{7,5},{8,10},{9,11},{10,... | collective-permute-start | bytes 393224 | tf_op jit(solution)/shard_map/ppermute | solution.py:21
  28.3 3.5 %collective-permute-done.6 = bf16[16,4096]{1,0:T(8,128)(2,1)S(1)} collective-permute-done((bf16[16,4096]{1,0:T(8,128)(2,1)S(1)}, bf16[16,4096]{1,0:T(8,128)(2,1)S(1)}, u32[]{:S(2)}, u32[]{:S(2)}) %collective-permute-start.6) | collective-permute-done | bytes 131104 | tf_op jit(solution)/shard_map/ppermute | solution.py:21
  31.8 0.1 collective-permute-start.7
  31.9 1.3 %collective-permute-done.7 = bf16[16,4096]{1,0:T(8,128)(2,1)S(1)} collective-permute-done((bf16[16,4096]{1,0:T(8,128)(2,1)S(1)}, bf16[16,4096]{1,0:T(8,128)(2,1)S(1)}, u32[]{:S(2)}, u32[]{:S(2)}) %collective-permute-start.7) | collective-permute-done | bytes 131104 | tf_op jit(solution)/shard_map/ppermute | solution.py:21
  33.2 0.0 copy-done
  33.3 0.7 %fusion = bf16[2,8,4096]{2,1,0:T(8,128)(2,1)} fusion(bf16[16,4096]{1,0:T(8,128)(2,1)S(1)} %collective-permute-done.7, bf16[16,4096]{1,0:T(8,128)(2,1)S(1)} %add_convert_fusion, bf16[2,8,4096]{2,1,0:T(8,128)(2,1)S(1)} %copy-done), kind=kLoop, calls=%fused_computation.1 | loop fusion | flops 393216 | bytes 524288 | tf_op jit(solution)/shard_map/convert_element_type | solution.py:330
  (10 shorter events, 0.1 us)
Async XLA Ops:
  0.0 12.7 %copy-start.1 = (s32[2,2]{1,0:T(2,128)S(1)}, s32[2,2]{1,0:T(2,128)}, u32[]{:S(2)}) copy-start(s32[2,2]{1,0:T(2,128)} %param.8) | copy-start | bytes 52
  6.9 8.1 %collective-permute-start = (f32[4,2432]{1,0:T(4,128)S(1)}, f32[4,2432]{1,0:T(4,128)S(1)}, u32[]{:S(2)}, u32[]{:S(2)}) collective-permute-start(f32[4,2432]{1,0:T(4,128)S(1)} %get-tuple-element.12), channel_id=1, source_target_pairs={{0,12},{4,8},{8,4},{12,0},{1,13},{5,9},{9,5},{13,1},{2,14},{6,10},... | collective-permute-start | bytes 116744 | tf_op jit(solution)/shard_map/ppermute | solution.py:21
  12.1 4.9 %collective-permute-start.1 = (f32[4,2432]{1,0:T(4,128)S(1)}, f32[4,2432]{1,0:T(4,128)S(1)}, u32[]{:S(2)}, u32[]{:S(2)}) collective-permute-start(f32[4,2432]{1,0:T(4,128)S(1)} %get-tuple-element.13), channel_id=1, source_target_pairs={{0,8},{4,12},{8,0},{12,4},{1,9},{5,13},{9,1},{13,5},{2,10},{6,14},... | collective-permute-start | bytes 116744 | tf_op jit(solution)/shard_map/ppermute | solution.py:21
  12.1 4.9 %collective-permute-start.2 = (f32[4,2432]{1,0:T(4,128)S(1)}, f32[4,2432]{1,0:T(4,128)S(1)}, u32[]{:S(2)}, u32[]{:S(2)}) collective-permute-start(f32[4,2432]{1,0:T(4,128)S(1)} %get-tuple-element.14), channel_id=1, source_target_pairs={{0,4},{4,0},{8,12},{12,8},{1,5},{5,1},{9,13},{13,9},{2,6},{6,2},{1... | collective-permute-start | bytes 116744 | tf_op jit(solution)/shard_map/ppermute | solution.py:21
  13.1 11.4 %slice-start = ((s8[16777216]{0:T(1024)(128)(4,1)}), s8[4194304]{0:T(1024)(128)(4,1)S(1)}, s32[]{:S(2)}) async-start(s8[16777216]{0:T(1024)(128)(4,1)} %bitcast.10), calls=%async_computation | async-start | bytes 8388608
  17.0 7.5 %slice-start.1 = ((s8[16777216]{0:T(1024)(128)(4,1)}), s8[4194304]{0:T(1024)(128)(4,1)S(1)}, s32[]{:S(2)}) async-start(s8[16777216]{0:T(1024)(128)(4,1)} %bitcast.10), calls=%async_computation.1 | async-start | bytes 8388608
  17.0 7.5 %slice-start.2 = ((s8[16777216]{0:T(1024)(128)(4,1)}), s8[4194304]{0:T(1024)(128)(4,1)S(1)}, s32[]{:S(2)}) async-start(s8[16777216]{0:T(1024)(128)(4,1)} %bitcast.10), calls=%async_computation.2 | async-start | bytes 8388608
  17.0 7.6 %slice-start.3 = ((s8[16777216]{0:T(1024)(128)(4,1)}), s8[4194304]{0:T(1024)(128)(4,1)S(1)}, s32[]{:S(2)}) async-start(s8[16777216]{0:T(1024)(128)(4,1)} %bitcast.10), calls=%async_computation.3 | async-start | bytes 8388608
  17.9 15.4 %copy-start = (bf16[2,8,4096]{2,1,0:T(8,128)(2,1)S(1)}, bf16[2,8,4096]{2,1,0:T(8,128)(2,1)}, u32[]{:S(2)}) copy-start(bf16[2,8,4096]{2,1,0:T(8,128)(2,1)} %tokens_hbm.1) | copy-start | bytes 393220
  17.9 5.7 %collective-permute-start.5 = (bf16[4,2048]{1,0:T(4,128)(2,1)S(1)}, bf16[4,2048]{1,0:T(4,128)(2,1)S(1)}, u32[]{:S(2)}, u32[]{:S(2)}) collective-permute-start(bf16[4,2048]{1,0:T(4,128)(2,1)S(1)} %attend.1.refs_0_), channel_id=1, source_target_pairs={{0,12},{4,8},{8,4},{12,0},{1,13},{5,9},{9,5},{13,1},{2,14},{6,10},... | collective-permute-start | bytes 49160 | tf_op jit(solution)/shard_map/ppermute | solution.py:21
  19.8 4.6 %collective-permute-start.4 = (bf16[4,2048]{1,0:T(4,128)(2,1)S(1)}, bf16[4,2048]{1,0:T(4,128)(2,1)S(1)}, u32[]{:S(2)}, u32[]{:S(2)}) collective-permute-start(bf16[4,2048]{1,0:T(4,128)(2,1)S(1)} %attend.1.refs_0_), channel_id=1, source_target_pairs={{0,8},{4,12},{8,0},{12,4},{1,9},{5,13},{9,1},{13,5},{2,10},{6,14},... | collective-permute-start | bytes 49160 | tf_op jit(solution)/shard_map/ppermute | solution.py:21
  20.0 4.5 %collective-permute-start.3 = (bf16[4,2048]{1,0:T(4,128)(2,1)S(1)}, bf16[4,2048]{1,0:T(4,128)(2,1)S(1)}, u32[]{:S(2)}, u32[]{:S(2)}) collective-permute-start(bf16[4,2048]{1,0:T(4,128)(2,1)S(1)} %attend.1.refs_0_), channel_id=1, source_target_pairs={{0,4},{4,0},{8,12},{12,8},{1,5},{5,1},{9,13},{13,9},{2,6},{6,2},{1... | collective-permute-start | bytes 49160 | tf_op jit(solution)/shard_map/ppermute | solution.py:21
  26.8 5.0 %collective-permute-start.6 = (bf16[16,4096]{1,0:T(8,128)(2,1)S(1)}, bf16[16,4096]{1,0:T(8,128)(2,1)S(1)}, u32[]{:S(2)}, u32[]{:S(2)}) collective-permute-start(bf16[16,4096]{1,0:T(8,128)(2,1)S(1)} %output.1), channel_id=1, source_target_pairs={{0,2},{1,3},{2,0},{3,1},{4,6},{5,7},{6,4},{7,5},{8,10},{9,11},{10,... | collective-permute-start | bytes 393224 | tf_op jit(solution)/shard_map/ppermute | solution.py:21
  31.8 1.4 %collective-permute-start.7 = (bf16[16,4096]{1,0:T(8,128)(2,1)S(1)}, bf16[16,4096]{1,0:T(8,128)(2,1)S(1)}, u32[]{:S(2)}, u32[]{:S(2)}) collective-permute-start(bf16[16,4096]{1,0:T(8,128)(2,1)S(1)} %add_convert_fusion), channel_id=1, source_target_pairs={{0,1},{1,0},{2,3},{3,2},{4,5},{5,4},{6,7},{7,6},{8,9},{9,8},{10,11... | collective-permute-start | bytes 393224 | tf_op jit(solution)/shard_map/ppermute | solution.py:21
